TPU v7x, 32 devices: a whole 2x2x4 slice. The times are simulated.
32 devices in a mesh: section: 2 (over core), ctx: 8 (over z, x), dp: 2 (over y).
Axes of the slice: x: 2, y: 2, z: 4, core: 2. Of those that a mesh axis runs over, the one named last changes fastest.
Arguments:
- hidden: bfloat16 [4, 2048, 5376], P(('section', 'dp'), 'ctx'), may hold values from -6 to 6
- frozen_query_rows: bfloat16 [4, 2048, 2048], P(('section', 'dp'), 'ctx'), may hold values from -12 to 12
- frozen_key_rows: bfloat16 [4, 2048, 1024], P(('section', 'dp'), 'ctx'), may hold values from -12 to 12
- frozen_value_rows: bfloat16 [4, 2048, 1024], P(('section', 'dp'), 'ctx'), may hold values from -6 to 6
- next_output_gradient: bfloat16 [4, 2048, 2048], P(('section', 'dp'), 'ctx'), may hold values from -0.011962891 to 0.011962891
- document_lengths: int32 [4, 16], P(('section', 'dp')), may hold values from 1 to 512, 2048 in all within a row
- document_adapter: int32 [4, 16], P(('section', 'dp')), may hold values from 0 to 3
- adapter_down_maps: bfloat16 [5376, 2, 4, 16], replicated, may hold values from -0.078125 to 0.078125
- adapter_up_maps: bfloat16 [2, 4, 16, 1024], replicated, may hold values from -1.5 to 1.5
Outputs:
- handed_on: bfloat16 [4, 2048, 2048], P(('section', 'dp'), 'ctx')
- down_map_gradient: float32 [5376, 2, 4, 16], replicated
- up_map_gradient: float32 [2, 4, 16, 1024], replicated
Inputs may be any that keep to these rules, and one draw needn't show every extreme that they name: `document_lengths`: each sequence's 16 lengths sum to 2048, and the longest is exactly 512.
All inputs are finite; a program needn't handle non-finite values.
Results may differ from a plain program's by a relative error of at most 0.016.
Values may be sent and summed in bfloat16 or wider, within the bound.
No kernel may reach another device: no remote copies, remote signals or barrier semaphores. Data moves between devices by JAX's collectives and lax.ppermute only.
A program may use at most 128 MiB of HBM per device.

v0:
```python
from functools import partial

import jax
import jax.numpy as jnp
from jax import lax
from jax.sharding import PartitionSpec as P

HD = 128
WINDOW = 1024


query_scale = 168.0 ** (-0.5)
adapter_scale = 0.5
rope_base = 10000.0
masked_score = -1e30


def passed_along(value, axis, by):
    length = lax.axis_size(axis)
    return lax.ppermute(value, axis, [(i, (i + by) % length) for i in range(length)])


def passed_along_2(value, axis, steps):
    count = lax.axis_size(axis)
    initial, last = (max(0, -steps), min(count, count - steps))
    return lax.ppermute(value, axis, [(source, source + steps) for source in range(initial, last)])


def rotate(vectors, positions, direction):
    head_dim = vectors.shape[-1]
    half_dim = head_dim // 2
    frequency = rope_base ** (-(jnp.arange(half_dim, dtype=jnp.float32) * 2.0) / head_dim)
    angles = positions[:, None] * frequency[None, :]
    cos_part = jnp.cos(angles)[:, None, :]
    sine_part = direction * jnp.sin(angles)[:, None, :]
    front_half = vectors[..., :half_dim]
    back_half = vectors[..., half_dim:]
    return jnp.concatenate(
        [
            front_half * cos_part - back_half * sine_part,
            back_half * cos_part + front_half * sine_part,
        ],
        axis=-1,
    )


def doc_index(sequence_lengths, positions):
    doc_ends = jnp.cumsum(sequence_lengths)
    return jnp.sum((doc_ends[None, :] <= positions[:, None]).astype(jnp.int32), axis=1)


def tenant_rows(sequence_lengths, adapter_bank, positions):
    doc_ids = doc_index(sequence_lengths, positions)
    picked = (
        doc_ids[:, None] == jnp.arange(sequence_lengths.shape[0], dtype=jnp.int32)[None, :]
    ).astype(jnp.int32)
    return (doc_ids, jnp.sum(picked * adapter_bank[None, :], axis=1))


def adapter_token_rows(
    hidden, frozen_key_rows, frozen_value_rows, adapter_down_maps, adapter_up_maps, adapter_choice
):
    token_row_count = hidden.shape[0]
    adapter_choices = adapter_up_maps.shape[1]
    adapter_rank_size = adapter_up_maps.shape[2]
    key_value_width = adapter_up_maps.shape[3]
    adapter_onehot_mask = (
        adapter_choice[:, None] == jnp.arange(adapter_choices, dtype=jnp.int32)[None, :]
    ).astype(jnp.float32)
    low_rank_rows = jnp.dot(
        hidden,
        adapter_down_maps.reshape(
            adapter_down_maps.shape[0], 2 * adapter_choices * adapter_rank_size
        ),
        preferred_element_type=jnp.float32,
    )
    low_rank_rows = low_rank_rows.reshape(token_row_count, 2, adapter_choices, adapter_rank_size)
    low_rank = jnp.sum(low_rank_rows * adapter_onehot_mask[:, None, :, None], axis=2).astype(
        jnp.bfloat16
    )
    adapter_spread = low_rank[:, :, None, :] * adapter_onehot_mask[:, None, :, None].astype(
        jnp.bfloat16
    )
    key_adapter_shift = jnp.dot(
        adapter_spread[:, 0].reshape(token_row_count, adapter_choices * adapter_rank_size),
        adapter_up_maps[0].reshape(adapter_choices * adapter_rank_size, key_value_width),
        preferred_element_type=jnp.float32,
    )
    value_adapter_shift = jnp.dot(
        adapter_spread[:, 1].reshape(token_row_count, adapter_choices * adapter_rank_size),
        adapter_up_maps[1].reshape(adapter_choices * adapter_rank_size, key_value_width),
        preferred_element_type=jnp.float32,
    )
    key_before_rotary = frozen_key_rows.astype(jnp.float32) + adapter_scale * key_adapter_shift
    value_token_rows = (
        frozen_value_rows.astype(jnp.float32) + adapter_scale * value_adapter_shift
    ).astype(jnp.bfloat16)
    return (adapter_onehot_mask, adapter_spread, key_before_rotary, value_token_rows)


def adapter_gradients(
    hidden, adapter_spread, adapter_onehot_mask, key_gradient, value_gradient, adapter_up_maps
):
    token_row_count = hidden.shape[0]
    adapter_choices = adapter_up_maps.shape[1]
    adapter_rank_size = adapter_up_maps.shape[2]
    key_value_width = adapter_up_maps.shape[3]
    up_gradient_parts = []
    down_parts = []
    for adapter_selector, adapter_field_gradient in ((0, key_gradient), (1, value_gradient)):
        flat_adapter_spread = adapter_spread[:, adapter_selector].reshape(
            token_row_count, adapter_choices * adapter_rank_size
        )
        up_gradient_parts.append(
            adapter_scale
            * jnp.dot(
                flat_adapter_spread.T, adapter_field_gradient, preferred_element_type=jnp.float32
            )
        )
        low_rank_gradient = adapter_scale * jnp.dot(
            adapter_field_gradient,
            adapter_up_maps[adapter_selector]
            .reshape(adapter_choices * adapter_rank_size, key_value_width)
            .T,
            preferred_element_type=jnp.float32,
        )
        down_parts.append(
            (
                low_rank_gradient.reshape(token_row_count, adapter_choices, adapter_rank_size)
                * adapter_onehot_mask[:, :, None]
            ).astype(jnp.bfloat16)
        )
    up_map_gradient = jnp.stack(up_gradient_parts).reshape(
        2, adapter_choices, adapter_rank_size, key_value_width
    )
    low_grads = jnp.stack(down_parts, axis=1).reshape(
        token_row_count, 2 * adapter_choices * adapter_rank_size
    )
    down_map_gradient = jnp.dot(hidden.T, low_grads, preferred_element_type=jnp.float32).reshape(
        hidden.shape[1], 2, adapter_choices, adapter_rank_size
    )
    return (down_map_gradient, up_map_gradient)


def masked_scores(query_part, key_part, allowed):
    scores = (
        jnp.einsum("trd,ld->trl", query_part, key_part, preferred_element_type=jnp.float32)
        * query_scale
    )
    return jnp.where(allowed[:, None, :], scores, masked_score)


def group_forward(operands, allowed):
    query_part, key_part, value_part = operands
    scores = masked_scores(query_part, key_part, allowed)
    row_max = jnp.max(scores, axis=2, keepdims=True)
    shifted = jnp.exp(scores - row_max)
    row_total = jnp.sum(shifted, axis=2, keepdims=True)
    weights = (shifted / row_total).astype(jnp.bfloat16)
    output_rows = jnp.einsum(
        "trl,ld->trd", weights, value_part, preferred_element_type=jnp.float32
    ).astype(jnp.bfloat16)
    return (output_rows, (row_max + jnp.log(row_total))[..., 0])


def group_backward(operands, allowed):
    query_part, key_part, value_part, out_part, grad_part, log_total = operands
    scores = masked_scores(query_part, key_part, allowed)
    weights = jnp.exp(scores - log_total[:, :, None])
    weights_low = weights.astype(jnp.bfloat16)
    drift_rows = jnp.sum(grad_part.astype(jnp.float32) * out_part.astype(jnp.float32), axis=2)
    grad_weights = jnp.einsum(
        "trd,ld->trl", grad_part, value_part, preferred_element_type=jnp.float32
    )
    grad_scores = (weights * (grad_weights - drift_rows[:, :, None])).astype(jnp.bfloat16)
    value_step = jnp.einsum(
        "trl,trd->ld", weights_low, grad_part, preferred_element_type=jnp.float32
    )
    key_step = (
        jnp.einsum("trl,trd->ld", grad_scores, query_part, preferred_element_type=jnp.float32)
        * query_scale
    )
    return (key_step, value_step)


def body(
    hidden,
    frozen_query_rows,
    frozen_key_rows,
    frozen_value_rows,
    next_output_gradient,
    document_lengths,
    document_adapter,
    adapter_down_maps,
    adapter_up_maps,
):
    tok_rows = hidden.shape[1]
    query_width = frozen_query_rows.shape[2]
    key_value_width = frozen_key_rows.shape[2]
    kv_heads = key_value_width // HD
    group_size = query_width // key_value_width
    ctx_index = lax.axis_index("ctx")
    reach_devs = min(WINDOW // tok_rows, lax.axis_size("ctx") - 1)
    returned_values = passed_along(next_output_gradient, "section", -1)
    positions = ctx_index * tok_rows + jnp.arange(tok_rows, dtype=jnp.int32)
    doc_ids, adapter_choice = tenant_rows(document_lengths[0], document_adapter[0], positions)
    adapter_onehot_mask, adapter_spread, key_before_rotary, value_token_rows = adapter_token_rows(
        hidden[0],
        frozen_key_rows[0],
        frozen_value_rows[0],
        adapter_down_maps,
        adapter_up_maps,
        adapter_choice,
    )
    pos_float = positions.astype(jnp.float32)
    key_rows = (
        rotate(key_before_rotary.reshape(tok_rows, kv_heads, HD), pos_float, 1.0)
        .astype(jnp.bfloat16)
        .reshape(tok_rows, key_value_width)
    )
    query_rows = rotate(
        frozen_query_rows[0].astype(jnp.float32).reshape(tok_rows, kv_heads * group_size, HD),
        pos_float,
        1.0,
    ).astype(jnp.bfloat16)
    received = []
    moving = (key_rows, value_token_rows)
    for distance in range(reach_devs):
        moving = passed_along_2((moving[0], moving[1]), "ctx", 1)
        received.append(moving)
    far_first = received[::-1]
    key_all = jnp.concatenate([kv_pair[0] for kv_pair in far_first] + [key_rows], axis=0)
    value_all = jnp.concatenate([kv_pair[1] for kv_pair in far_first] + [value_token_rows], axis=0)
    key_pos = (ctx_index - reach_devs) * tok_rows + jnp.arange(
        (reach_devs + 1) * tok_rows, dtype=jnp.int32
    )
    key_docs = doc_index(document_lengths[0], key_pos)
    key_gap = positions[:, None] - key_pos[None, :]
    allowed = (
        (doc_ids[:, None] == key_docs[None, :])
        & (key_gap >= 0)
        & (key_gap < WINDOW)
        & (key_pos >= 0)[None, :]
    )
    query_groups = jnp.moveaxis(query_rows.reshape(tok_rows, kv_heads, group_size, HD), 1, 0)
    key_groups = jnp.moveaxis(key_all.reshape(-1, kv_heads, HD), 1, 0)
    value_groups = jnp.moveaxis(value_all.reshape(-1, kv_heads, HD), 1, 0)
    out_groups, log_groups = lax.map(
        partial(group_forward, allowed=allowed), (query_groups, key_groups, value_groups)
    )
    attention_output = jnp.moveaxis(out_groups, 0, 1).reshape(1, tok_rows, query_width)
    handed = passed_along(attention_output, "section", 1)
    grad_groups = jnp.moveaxis(returned_values[0].reshape(tok_rows, kv_heads, group_size, HD), 1, 0)
    key_grads, value_grads = lax.map(
        partial(group_backward, allowed=allowed),
        (query_groups, key_groups, value_groups, out_groups, grad_groups, log_groups),
    )
    key_grads = jnp.moveaxis(key_grads, 0, 1).reshape(-1, key_value_width)
    value_grads = jnp.moveaxis(value_grads, 0, 1).reshape(-1, key_value_width)

    def rows_at(field_rows, distance):
        return field_rows[
            (reach_devs - distance) * tok_rows : (reach_devs - distance + 1) * tok_rows
        ]

    carried = (rows_at(key_grads, reach_devs), rows_at(value_grads, reach_devs))
    for distance in range(reach_devs - 1, -1, -1):
        carried = passed_along_2((carried[0], carried[1]), "ctx", -1)
        carried = (
            carried[0] + rows_at(key_grads, distance),
            carried[1] + rows_at(value_grads, distance),
        )
    key_back, value_back = carried
    key_gradient = (
        rotate(key_back.reshape(tok_rows, kv_heads, HD), pos_float, -1.0)
        .astype(jnp.bfloat16)
        .reshape(tok_rows, key_value_width)
    )
    value_gradient = value_back.astype(jnp.bfloat16)
    down_map_gradient, up_map_gradient = adapter_gradients(
        hidden[0],
        adapter_spread,
        adapter_onehot_mask,
        key_gradient,
        value_gradient,
        adapter_up_maps,
    )
    summed = lax.psum((down_map_gradient, up_map_gradient), ("section", "ctx", "dp"))
    return (handed, summed[0], summed[1])


def solution(mesh):
    return jax.shard_map(
        body,
        mesh=mesh,
        in_specs=(
            P(("section", "dp"), "ctx", None),
            P(("section", "dp"), "ctx", None),
            P(("section", "dp"), "ctx", None),
            P(("section", "dp"), "ctx", None),
            P(("section", "dp"), "ctx", None),
            P(("section", "dp"), None),
            P(("section", "dp"), None),
            P(),
            P(),
        ),
        out_specs=(P(("section", "dp"), "ctx", None), P(), P()),
        check_vma=False,
    )
```

profile of v0, /device:TPU:0, one launch (start us, length us, event | category | flops | bytes accessed | tf_op | source)
XLA Modules:
  0.0 638.7 jit_solution(13565225289575519029)
XLA Ops:
  17.9 5.7 collective-permute-start
  28.1 6.9 %collective-permute-done = bf16[256,1024]{0,1:T(8,128)(2,1)} collective-permute-done((bf16[256,1024]{0,1:T(8,128)(2,1)S(1)}, bf16[256,1024]{0,1:T(8,128)(2,1)}, u32[]{:S(2)}, u32[]{:S(2)}) %collective-permute-start) | collective-permute-done | bytes 524320 | tf_op jit(solution)/shard_map/ppermute | solution.py:26
  35.0 5.3 collective-permute-start.1
  46.4 5.2 collective-permute-start.5
  51.5 6.1 collective-permute-done.1
  57.6 5.2 collective-permute-start.2
  68.8 5.2 collective-permute-start.6
  74.0 6.0 collective-permute-done.2
  80.1 4.4 collective-permute-start.3
  91.3 5.2 collective-permute-start.7
  96.5 6.1 collective-permute-done.3
  109.8 4.4 copy.48
  121.6 46.0 %while.26 = (s32[]{:T(128)}, bf16[8,256,2,128]{3,1,2,0:T(8,128)(2,1)}, f32[8,256,2]{1,2,0:T(2,128)}, bf16[8,256,2,128]{3,1,2,0:T(8,128)(2,1)}, bf16[8,1280,128]{...) while((s32[]{:T(128)}, ...), condition=%wide.region_8.9_spmd.clone, body=%wide.region_5.8_spmd.clone.sunk | while | flops 343145984 | bytes 9469813 | solution.py:248
  167.7 127.0 %while.27 = (s32[]{:T(128)}, f32[8,1280,128]{1,2,0:T(8,128)}, f32[8,1280,128]{1,2,0:T(8,128)}, bf16[8,256,2,128]{3,1,2,0:T(8,128)(2,1)}, bf16[8,1280,128]{2,1,0:...) while((s32[]{:T(128)}, f32[8,1280,128]{1,2,0:T(8,128)}, ...), condition=%wide.region_11.12_spmd.clone, body=%wide.region_9.11_spmd.clone.sunk | while | flops 678395392 | bytes 14472769 | solution.py:254
  206.1 3.9 fusion.130
  301.2 24.9 %collective-permute-done.14 = f32[256,1024]{0,1:T(8,128)S(1)} collective-permute-done((f32[256,1024]{0,1:T(8,128)S(1)}, f32[256,1024]{0,1:T(8,128)S(1)}, u32[]{:S(2)}, u32[]{:S(2)}) %collective-permute-start.14) | collective-permute-done | bytes 1048608 | tf_op jit(solution)/shard_map/ppermute | solution.py:26
  327.6 21.0 %collective-permute-done.10 = f32[256,1024]{0,1:T(8,128)S(1)} collective-permute-done((f32[256,1024]{0,1:T(8,128)S(1)}, f32[256,1024]{0,1:T(8,128)S(1)}, u32[]{:S(2)}, u32[]{:S(2)}) %collective-permute-start.10) | collective-permute-done | bytes 1048608 | tf_op jit(solution)/shard_map/ppermute | solution.py:26
  350.1 21.0 %collective-permute-done.15 = f32[256,1024]{0,1:T(8,128)S(1)} collective-permute-done((f32[256,1024]{0,1:T(8,128)S(1)}, f32[256,1024]{0,1:T(8,128)S(1)}, u32[]{:S(2)}, u32[]{:S(2)}) %collective-permute-start.15) | collective-permute-done | bytes 1048608 | tf_op jit(solution)/shard_map/ppermute | solution.py:26
  372.6 21.0 %collective-permute-done.11 = f32[256,1024]{0,1:T(8,128)S(1)} collective-permute-done((f32[256,1024]{0,1:T(8,128)S(1)}, f32[256,1024]{0,1:T(8,128)S(1)}, u32[]{:S(2)}, u32[]{:S(2)}) %collective-permute-start.11) | collective-permute-done | bytes 1048608 | tf_op jit(solution)/shard_map/ppermute | solution.py:26
  395.0 21.0 %collective-permute-done.16 = f32[256,1024]{0,1:T(8,128)S(1)} collective-permute-done((f32[256,1024]{0,1:T(8,128)S(1)}, f32[256,1024]{0,1:T(8,128)S(1)}, u32[]{:S(2)}, u32[]{:S(2)}) %collective-permute-start.16) | collective-permute-done | bytes 1048608 | tf_op jit(solution)/shard_map/ppermute | solution.py:26
  417.5 21.0 %collective-permute-done.12 = f32[256,1024]{0,1:T(8,128)S(1)} collective-permute-done((f32[256,1024]{0,1:T(8,128)S(1)}, f32[256,1024]{0,1:T(8,128)S(1)}, u32[]{:S(2)}, u32[]{:S(2)}) %collective-permute-start.12) | collective-permute-done | bytes 1048608 | tf_op jit(solution)/shard_map/ppermute | solution.py:26
  440.3 20.8 %collective-permute-done.17 = f32[256,1024]{0,1:T(8,128)S(1)} collective-permute-done((f32[256,1024]{0,1:T(8,128)S(1)}, f32[256,1024]{0,1:T(8,128)S(1)}, u32[]{:S(2)}, u32[]{:S(2)}) %collective-permute-start.17) | collective-permute-done | bytes 1048608 | tf_op jit(solution)/shard_map/ppermute | solution.py:26
  461.7 18.9 %collective-permute-done.13 = f32[256,1024]{0,1:T(8,128)S(1)} collective-permute-done((f32[256,1024]{0,1:T(8,128)S(1)}, f32[256,1024]{0,1:T(8,128)S(1)}, u32[]{:S(2)}, u32[]{:S(2)}) %collective-permute-start.13) | collective-permute-done | bytes 1048608 | tf_op jit(solution)/shard_map/ppermute | solution.py:26
  493.7 131.4 %all-reduce.3.cloned.1.call-done = (f32[5376,2,4,16]{0,3,2,1:T(8,128)}, f32[2,4,16,1024]{3,2,1,0:T(8,128)}) async-done(((f32[5376,2,4,16]{0,3,2,1:T(8,128)}, f32[2,4,16,1024]{3,2,1,0:T(8,128)}), (f32[5376,2,4,16]{0,3,2,1:T(8,128)}, f32[2,4,16,1024]{3,2,1,0:T(8,128)})) %all-reduce.3.cloned.1.call-update) | async-done | bytes 3276816 | tf_op jit(solution)/shard_map/psum | solution.py:288
  (343 shorter events, 252.8 us)
Async XLA Ops:
  7.2 618.0 %all-reduce.3.cloned.1.call-start = ((), (), s32[]{:S(2)}) async-start(), calls=%async_computation | async-start | bytes 6553600 | tf_op jit(solution)/shard_map/psum | solution.py:288
  15.5 8.0 %copy-start.22 = (bf16[1,256,1024]{2,1,0:T(8,128)(2,1)S(1)}, bf16[1,256,1024]{2,1,0:T(8,128)(2,1)}, u32[]{:S(2)}) copy-start(bf16[1,256,1024]{2,1,0:T(8,128)(2,1)} %param.16) | copy-start | bytes 1572868
  17.9 17.2 %collective-permute-start = (bf16[256,1024]{0,1:T(8,128)(2,1)S(1)}, bf16[256,1024]{0,1:T(8,128)(2,1)}, u32[]{:S(2)}, u32[]{:S(2)}) collective-permute-start(bf16[256,1024]{0,1:T(8,128)(2,1)S(1)} %bitcast.243), channel_id=1, source_target_pairs={{0,2},{2,4},{4,6},{6,8},{8,10},{10,12},{12,14},{1,3},{3,5},{5,7},{... | collective-permute-start | bytes 1572872 | tf_op jit(solution)/shard_map/ppermute | solution.py:26
  24.7 21.7 %collective-permute-start.4 = (bf16[256,1024]{1,0:T(8,128)(2,1)}, bf16[256,1024]{1,0:T(8,128)(2,1)}, u32[]{:S(2)}, u32[]{:S(2)}) collective-permute-start(bf16[256,1024]{1,0:T(8,128)(2,1)} %fusion.59), channel_id=1, source_target_pairs={{0,2},{2,4},{4,6},{6,8},{8,10},{10,12},{12,14},{1,3},{3,5},{5,7},{... | collective-permute-start | bytes 1572872 | tf_op jit(solution)/shard_map/ppermute | solution.py:26
  35.0 22.6 %collective-permute-start.1 = (bf16[256,1024]{0,1:T(8,128)(2,1)}, bf16[256,1024]{0,1:T(8,128)(2,1)}, u32[]{:S(2)}, u32[]{:S(2)}) collective-permute-start(bf16[256,1024]{0,1:T(8,128)(2,1)} %collective-permute-done), channel_id=1, source_target_pairs={{0,2},{2,4},{4,6},{6,8},{8,10},{10,12},{12,14},{1,3},{3,5},{5,7},{... | collective-permute-start | bytes 1572872 | tf_op jit(solution)/shard_map/ppermute | solution.py:26
  42.6 125.1 %collective-permute-start.9 = (bf16[1,256,2048]{1,2,0:T(8,128)(2,1)}, bf16[1,256,2048]{1,2,0:T(8,128)(2,1)}, u32[]{:S(2)}, u32[]{:S(2)}) collective-permute-start(bf16[1,256,2048]{1,2,0:T(8,128)(2,1)} %copy.50), channel_id=1, source_target_pairs={{0,16},{16,0},{1,17},{17,1},{2,18},{18,2},{3,19},{19,3},{4,20},{20... | collective-permute-start | bytes 3145736 | tf_op jit(solution)/shard_map/ppermute | solution.py:20
  46.4 22.5 %collective-permute-start.5 = (bf16[256,1024]{1,0:T(8,128)(2,1)}, bf16[256,1024]{1,0:T(8,128)(2,1)}, u32[]{:S(2)}, u32[]{:S(2)}) collective-permute-start(bf16[256,1024]{1,0:T(8,128)(2,1)} %collective-permute-done.4), channel_id=1, source_target_pairs={{0,2},{2,4},{4,6},{6,8},{8,10},{10,12},{12,14},{1,3},{3,5},{5,7},{... | collective-permute-start | bytes 1572872 | tf_op jit(solution)/shard_map/ppermute | solution.py:26
  57.6 22.5 %collective-permute-start.2 = (bf16[256,1024]{0,1:T(8,128)(2,1)}, bf16[256,1024]{0,1:T(8,128)(2,1)}, u32[]{:S(2)}, u32[]{:S(2)}) collective-permute-start(bf16[256,1024]{0,1:T(8,128)(2,1)} %collective-permute-done.1), channel_id=1, source_target_pairs={{0,2},{2,4},{4,6},{6,8},{8,10},{10,12},{12,14},{1,3},{3,5},{5,7},{... | collective-permute-start | bytes 1572872 | tf_op jit(solution)/shard_map/ppermute | solution.py:26
  66.9 17.6 %copy-start.1 = (f32[256,64]{1,0:T(8,128)S(1)}, f32[256,64]{1,0:T(8,128)}, u32[]{:S(2)}) copy-start(f32[256,64]{1,0:T(8,128)} %copy.41) | copy-start | bytes 196612
  66.9 17.6 %copy-start.2 = (f32[256,64]{1,0:T(8,128)S(1)}, f32[256,64]{1,0:T(8,128)}, u32[]{:S(2)}) copy-start(f32[256,64]{1,0:T(8,128)} %copy.43) | copy-start | bytes 196612
  68.8 22.5 %collective-permute-start.6 = (bf16[256,1024]{1,0:T(8,128)(2,1)}, bf16[256,1024]{1,0:T(8,128)(2,1)}, u32[]{:S(2)}, u32[]{:S(2)}) collective-permute-start(bf16[256,1024]{1,0:T(8,128)(2,1)} %collective-permute-done.5), channel_id=1, source_target_pairs={{0,2},{2,4},{4,6},{6,8},{8,10},{10,12},{12,14},{1,3},{3,5},{5,7},{... | collective-permute-start | bytes 1572872 | tf_op jit(solution)/shard_map/ppermute | solution.py:26
  80.1 22.5 %collective-permute-start.3 = (bf16[256,1024]{0,1:T(8,128)(2,1)}, bf16[256,1024]{0,1:T(8,128)(2,1)S(1)}, u32[]{:S(2)}, u32[]{:S(2)}) collective-permute-start(bf16[256,1024]{0,1:T(8,128)(2,1)} %collective-permute-done.2), channel_id=1, source_target_pairs={{0,2},{2,4},{4,6},{6,8},{8,10},{10,12},{12,14},{1,3},{3,5},{5,7},{... | collective-permute-start | bytes 1572872 | tf_op jit(solution)/shard_map/ppermute | solution.py:26
  91.3 22.9 %collective-permute-start.7 = (bf16[256,1024]{1,0:T(8,128)(2,1)}, bf16[256,1024]{1,0:T(8,128)(2,1)}, u32[]{:S(2)}, u32[]{:S(2)}) collective-permute-start(bf16[256,1024]{1,0:T(8,128)(2,1)} %collective-permute-done.6), channel_id=1, source_target_pairs={{0,2},{2,4},{4,6},{6,8},{8,10},{10,12},{12,14},{1,3},{3,5},{5,7},{... | collective-permute-start | bytes 1572872 | tf_op jit(solution)/shard_map/ppermute | solution.py:26
  297.8 28.4 %collective-permute-start.14 = (f32[256,1024]{0,1:T(8,128)S(1)}, f32[256,1024]{0,1:T(8,128)S(1)}, u32[]{:S(2)}, u32[]{:S(2)}) collective-permute-start(f32[256,1024]{0,1:T(8,128)S(1)} %bitcast.238), channel_id=1, source_target_pairs={{2,0},{4,2},{6,4},{8,6},{10,8},{12,10},{14,12},{3,1},{5,3},{7,5},{... | collective-permute-start | bytes 3145736 | tf_op jit(solution)/shard_map/ppermute | solution.py:26
  299.9 48.7 %collective-permute-start.10 = (f32[256,1024]{0,1:T(8,128)S(1)}, f32[256,1024]{0,1:T(8,128)S(1)}, u32[]{:S(2)}, u32[]{:S(2)}) collective-permute-start(f32[256,1024]{0,1:T(8,128)S(1)} %bitcast.239), channel_id=1, source_target_pairs={{2,0},{4,2},{6,4},{8,6},{10,8},{12,10},{14,12},{3,1},{5,3},{7,5},{... | collective-permute-start | bytes 3145736 | tf_op jit(solution)/shard_map/ppermute | solution.py:26
  326.3 44.8 %collective-permute-start.15 = (f32[256,1024]{0,1:T(8,128)S(1)}, f32[256,1024]{0,1:T(8,128)S(1)}, u32[]{:S(2)}, u32[]{:S(2)}) collective-permute-start(f32[256,1024]{0,1:T(8,128)S(1)} %bitcast_add_fusion.3), channel_id=1, source_target_pairs={{2,0},{4,2},{6,4},{8,6},{10,8},{12,10},{14,12},{3,1},{5,3},{7,5},{... | collective-permute-start | bytes 3145736 | tf_op jit(solution)/shard_map/ppermute | solution.py:26
  348.8 44.8 %collective-permute-start.11 = (f32[256,1024]{0,1:T(8,128)S(1)}, f32[256,1024]{0,1:T(8,128)S(1)}, u32[]{:S(2)}, u32[]{:S(2)}) collective-permute-start(f32[256,1024]{0,1:T(8,128)S(1)} %bitcast_add_fusion.7), channel_id=1, source_target_pairs={{2,0},{4,2},{6,4},{8,6},{10,8},{12,10},{14,12},{3,1},{5,3},{7,5},{... | collective-permute-start | bytes 3145736 | tf_op jit(solution)/shard_map/ppermute | solution.py:26
  371.3 44.8 %collective-permute-start.16 = (f32[256,1024]{0,1:T(8,128)S(1)}, f32[256,1024]{0,1:T(8,128)S(1)}, u32[]{:S(2)}, u32[]{:S(2)}) collective-permute-start(f32[256,1024]{0,1:T(8,128)S(1)} %bitcast_add_fusion.2), channel_id=1, source_target_pairs={{2,0},{4,2},{6,4},{8,6},{10,8},{12,10},{14,12},{3,1},{5,3},{7,5},{... | collective-permute-start | bytes 3145736 | tf_op jit(solution)/shard_map/ppermute | solution.py:26
  393.7 44.8 %collective-permute-start.12 = (f32[256,1024]{0,1:T(8,128)S(1)}, f32[256,1024]{0,1:T(8,128)S(1)}, u32[]{:S(2)}, u32[]{:S(2)}) collective-permute-start(f32[256,1024]{0,1:T(8,128)S(1)} %bitcast_add_fusion.6), channel_id=1, source_target_pairs={{2,0},{4,2},{6,4},{8,6},{10,8},{12,10},{14,12},{3,1},{5,3},{7,5},{... | collective-permute-start | bytes 3145736 | tf_op jit(solution)/shard_map/ppermute | solution.py:26
  416.1 24.1 %copy-start.6 = (bf16[2,4,16,1024]{3,2,1,0:T(8,128)(2,1)S(1)}, bf16[2,4,16,1024]{3,2,1,0:T(8,128)(2,1)}, u32[]{:S(2)}) copy-start(bf16[2,4,16,1024]{3,2,1,0:T(8,128)(2,1)} %param.21) | copy-start | bytes 786436
  416.2 44.8 %collective-permute-start.17 = (f32[256,1024]{0,1:T(8,128)S(1)}, f32[256,1024]{0,1:T(8,128)S(1)}, u32[]{:S(2)}, u32[]{:S(2)}) collective-permute-start(f32[256,1024]{0,1:T(8,128)S(1)} %bitcast_add_fusion.1), channel_id=1, source_target_pairs={{2,0},{4,2},{6,4},{8,6},{10,8},{12,10},{14,12},{3,1},{5,3},{7,5},{... | collective-permute-start | bytes 3145736 | tf_op jit(solution)/shard_map/ppermute | solution.py:26
  438.7 42.0 %collective-permute-start.13 = (f32[256,1024]{0,1:T(8,128)S(1)}, f32[256,1024]{0,1:T(8,128)S(1)}, u32[]{:S(2)}, u32[]{:S(2)}) collective-permute-start(f32[256,1024]{0,1:T(8,128)S(1)} %bitcast_add_fusion.5), channel_id=1, source_target_pairs={{2,0},{4,2},{6,4},{8,6},{10,8},{12,10},{14,12},{3,1},{5,3},{7,5},{... | collective-permute-start | bytes 3145736 | tf_op jit(solution)/shard_map/ppermute | solution.py:26
  461.2 19.6 %copy-start.7 = (f32[256,64]{0,1:T(8,128)S(1)}, f32[256,64]{0,1:T(8,128)}, u32[]{:S(2)}) copy-start(f32[256,64]{0,1:T(8,128)} %get-tuple-element.290) | copy-start | bytes 196612
  490.4 3.3 collective-permute-start.8
  (62 other events, 225.1 us)
Sparse Core Ops, SparseCore 0:
  484.6 140.5 all-reduce.2
where the time goes:
time: 642 us; the launch traced here: 639 us
  waiting for transfers between devices  336 us (52%)
  matrix products  123 us (19%)
  local copies, waits for them, and re-layouts  75.9 us (12%)
  starting transfers between devices  50.3 us (8%)
  other arithmetic  39.1 us (6%)
  between operations  14.5 us (2%)
    ppermute x16, waiting for transfers between devices, passed_along_2(): lax.ppermute(value, axis, [(source, source + steps) for source in range(i...  201 us
    psum x1, waiting for transfers between devices, body(): lax.psum((down_map_gradient, up_map_gradient), ('section', 'ctx', 'dp'))  131 us
    ppermute x16, starting transfers between devices, passed_along_2(): lax.ppermute(value, axis, [(source, source + steps) for source in range(i...  50.3 us
    dot_general x16, matrix products, masked_scores(): jnp.einsum('trd,ld->trl', query_part, key_part, preferred_element_type=jn...  40.9 us
    dot_general x8, matrix products, group_backward(): jnp.einsum('trl,trd->ld', grad_scores, query_part, preferred_element_type...  31.1 us
    unnamed x52, local copies, waits for them, and re-layouts  26.1 us
    dot_general x8, matrix products, group_backward(): jnp.einsum('trl,trd->ld', weights_low, grad_part, preferred_element_type=...  24.3 us
    dot_general x8, matrix products, group_forward(): jnp.einsum('trl,ld->trd', weights, value_part, preferred_element_type=jnp...  18.2 us
  transfers between devices with their start and end apart: 19, of which 17 were waited for; matrix products, arithmetic and copies ran while one was open for 14% of the time, Pallas kernels for 0%

commit v1 on v0

v1 whole, which is shorter than its diff:
```python
from functools import partial

import jax
import jax.numpy as jnp
from jax import lax
from jax.experimental import pallas as pl
from jax.experimental.pallas import tpu as pltpu
from jax.sharding import PartitionSpec as P

HD = 128
WINDOW = 1024
SUB = 8
SPLITS = 4

query_scale = 168.0 ** (-0.5)
adapter_scale = 0.5
rope_base = 10000.0
masked_score = -1e30
f32 = jnp.float32
bf16 = jnp.bfloat16


def permute_by(value, axis, steps):
    count = lax.axis_size(axis)
    first, last = max(0, -steps), min(count, count - steps)
    return lax.ppermute(value, axis, [(i, i + steps) for i in range(first, last)])


def permute_cyclic(value, axis, by):
    count = lax.axis_size(axis)
    return lax.ppermute(value, axis, [(i, (i + by) % count) for i in range(count)])


def permute_xor(value, axis, bit):
    count = lax.axis_size(axis)
    return lax.ppermute(value, axis, [(i, i ^ bit) for i in range(count)])


def window_blocks(own, steps):
    count = lax.axis_size("ctx")
    even_to_odd = [(i, i + 1) for i in range(0, count - 1, 2)]
    odd_to_even = [(i + 1, i) for i in range(0, count - 1, 2)]
    chain = [own]
    for _ in range(steps):
        chain.append(permute_by(chain[-1], "ctx", 2))
    blocks = []
    for i in range(steps):
        blocks.append(
            [
                lax.ppermute(chain[i], "ctx", even_to_odd),
                lax.ppermute(chain[i + 1], "ctx", odd_to_even),
            ]
        )
        blocks.append([chain[i + 1]])
    return blocks


def doc_index(sequence_lengths, positions):
    doc_ends = jnp.cumsum(sequence_lengths)
    return jnp.sum((doc_ends[None, :] <= positions[:, None]).astype(jnp.int32), axis=1)


def attention_kernel(*refs, counts, tok, group):
    n_in = sum(counts)
    k_refs, v_refs = refs[:n_in], refs[n_in : 2 * n_in]
    q_ref, g_ref, spread_ref, up_ref, bias_ref, cos_ref, sin_ref = refs[2 * n_in : 2 * n_in + 7]
    out_ref, lg_ref, u_ref = refs[2 * n_in + 7 :]
    up = up_ref[0]
    spread = spread_ref[...]
    shift = adapter_scale * jnp.dot(spread, up, preferred_element_type=f32)

    def stacked(block_refs):
        rows, at = [], 0
        for n in counts:
            block = block_refs[at][...].astype(f32)
            for extra in block_refs[at + 1 : at + n]:
                block = block + extra[...].astype(f32)
            rows.append(block)
            at += n
        return jnp.concatenate(rows, axis=0)

    cos, sin = cos_ref[...], sin_ref[...]
    key = stacked(k_refs) + shift[:, :HD]
    key = (key * cos + pltpu.roll(key, HD // 2, 1) * sin).astype(bf16)
    val = (stacked(v_refs) + shift[:, HD:]).astype(bf16)
    cos_q, sin_q = cos[:tok], sin[:tok]
    queries, grads = [], []
    for h in range(group):
        q = q_ref[:, h * HD : (h + 1) * HD].astype(f32)
        queries.append((q * cos_q + pltpu.roll(q, HD // 2, 1) * sin_q).astype(bf16))
        grads.append(g_ref[:, h * HD : (h + 1) * HD])
    q = jnp.concatenate(queries, axis=0)
    g = jnp.concatenate(grads, axis=0)
    dot = partial(lax.dot_general, preferred_element_type=f32)
    last, first = (((1,), (1,)), ((), ())), (((0,), (0,)), ((), ()))
    bias = jnp.concatenate([bias_ref[...]] * group, axis=1)
    scores = dot(key, q, last) * query_scale + bias
    top = jnp.max(scores, axis=0, keepdims=True)
    probs = jnp.exp(scores - top)
    total = jnp.sum(probs, axis=0, keepdims=True)
    probs = probs * (1.0 / total)
    low_probs = probs.astype(bf16)
    out_t = dot(val, low_probs, first)
    out = out_t.T.astype(bf16)
    for h in range(group):
        out_ref[:, h * HD : (h + 1) * HD] = out[h * tok : (h + 1) * tok]
    drift = jnp.sum(out_t.astype(bf16).astype(f32) * g.astype(f32).T, axis=0, keepdims=True)
    dprob = dot(val, g, last)
    dscore = (probs * (dprob - drift)).astype(bf16)
    dkey = query_scale * jnp.dot(dscore, q, preferred_element_type=f32)
    dval = jnp.dot(low_probs, g, preferred_element_type=f32)
    dkey = dkey * cos - pltpu.roll(dkey, HD // 2, 1) * sin
    both = jnp.concatenate([dkey.astype(bf16), dval.astype(bf16)], axis=1)
    lg = dot(both, up, last)

    @pl.when(pl.program_id(0) == 0)
    def _():
        lg_ref[...] = lg

    @pl.when(pl.program_id(0) != 0)
    def _():
        lg_ref[...] += lg

    u = adapter_scale * dot(spread, both, first)
    half = spread.shape[1] // 2
    u_ref[0] = u[:half, :HD].astype(bf16)
    u_ref[1] = u[half:, HD:].astype(bf16)


def attention(blocks, start, q_rows, g_rows, spread, up_cat, bias, cos, sin):
    tok = q_rows.shape[0]
    heads = blocks[0][0].shape[1] // (2 * HD)
    kv_heads, width, _ = up_cat.shape
    group = q_rows.shape[1] // (kv_heads * HD)
    counts = tuple(len(b) for b in blocks)
    flat = [a for b in blocks for a in b]
    span = spread.shape[0]
    half = width // 2
    whole = lambda shape: pl.BlockSpec(shape, lambda h: (0,) * len(shape))
    in_specs = (
        [pl.BlockSpec((tok, HD), lambda h: (0, h))] * len(flat)
        + [pl.BlockSpec((tok, HD), lambda h: (0, h + heads))] * len(flat)
        + [pl.BlockSpec((tok, group * HD), lambda h: (0, h + start))] * 2
        + [
            whole((span, width)),
            pl.BlockSpec((1, width, 2 * HD), lambda h: (h + start, 0, 0)),
            whole((span, tok)),
            whole((span, HD)),
            whole((span, HD)),
        ]
    )
    return pl.pallas_call(
        partial(attention_kernel, counts=counts, tok=tok, group=group),
        grid=(heads,),
        in_specs=in_specs,
        out_specs=[
            pl.BlockSpec((tok, group * HD), lambda h: (0, h)),
            whole((span, width)),
            pl.BlockSpec((2, half, HD), lambda h: (0, 0, h)),
        ],
        out_shape=[
            jax.ShapeDtypeStruct((tok, heads * group * HD), bf16),
            jax.ShapeDtypeStruct((span, width), f32),
            jax.ShapeDtypeStruct((2, half, heads * HD), bf16),
        ],
        compiler_params=pltpu.CompilerParams(dimension_semantics=("arbitrary",)),
        name="attention",
    )(*flat, *flat, q_rows, g_rows, spread, up_cat, bias, cos, sin)


def product_kernel(*refs, n_recv, n_up, cols, up_cols):
    side_ref, lg_ref = refs[:2]
    recv = refs[2 : 2 + n_recv]
    mask_ref, hidden_ref = refs[2 + n_recv : 4 + n_recv]
    ups = refs[4 + n_recv : 4 + n_recv + n_up]
    keep_ref, send_ref = refs[4 + n_recv + n_up :]
    side = side_ref[0]
    total = lg_ref[...]
    for r in recv:
        total = total + r[...].astype(f32)
    total = total * mask_ref[...]
    width = total.shape[1]
    half = width // 2
    total = jnp.where(side == 0, total, pltpu.roll(total, half, 1)).astype(bf16)
    per_row = cols + up_cols
    rows = half // SUB
    step = 2 if cols % 2 == 0 else 1
    for c in range(0, cols, step):
        w = lax.dot_general(
            total,
            hidden_ref[:, c * HD : (c + step) * HD],
            (((0,), (0,)), ((), ())),
            preferred_element_type=f32,
        ).astype(bf16)
        for j in range(step):
            for r in range(rows):
                tile = w[:, j * HD : (j + 1) * HD]
                keep_ref[r * per_row + c + j] = tile[r * SUB : (r + 1) * SUB]
                send_ref[r * per_row + c + j] = tile[half + r * SUB : half + (r + 1) * SUB]
    at = cols
    for up in ups:
        for h in range(up.shape[2] // HD):
            for r in range(rows):
                where = (slice(r * SUB, (r + 1) * SUB), slice(h * HD, (h + 1) * HD))
                keep_ref[r * per_row + at] = up[(side,) + where]
                send_ref[r * per_row + at] = up[(1 - side,) + where]
            at += 1
    used = rows * per_row
    if keep_ref.shape[0] > used:
        rest = keep_ref.shape[0] - used
        keep_ref[pl.ds(used, rest)] = jnp.zeros((rest, SUB, HD), bf16)
        send_ref[pl.ds(used, rest)] = jnp.zeros((rest, SUB, HD), bf16)


def assemble_kernel(scalars_ref, ma_ref, mb_ref, ra_ref, rb_ref, w_ref, u_ref, *, cols, rows):
    side, me_a, me_b = scalars_ref[0], scalars_ref[1], scalars_ref[2]
    n_a, a = ma_ref.shape[:2]
    b = mb_ref.shape[1]
    up_cols = u_ref.shape[1] // HD
    per_row = cols + up_cols
    for r in range(rows):
        for c in range(per_row):
            t = r * per_row + c
            if t < n_a * a:
                mine, theirs, piece, off = ma_ref, ra_ref, (t // a) ^ me_a, t % a
            else:
                t -= n_a * a
                mine, theirs, piece, off = mb_ref, rb_ref, (t // b) ^ me_b, t % b
            for src, m in ((mine, side), (theirs, 1 - side)):
                at = pl.multiple_of((m * rows + r) * SUB, SUB)
                tile = src[piece, off].astype(f32)
                if c < cols:
                    w_ref[pl.ds(at, SUB), c * HD : (c + 1) * HD] = tile
                else:
                    u_ref[pl.ds(at, SUB), (c - cols) * HD : (c - cols + 1) * HD] = tile


def axis_bits(axis):
    bits, bit = [], 1
    while bit < lax.axis_size(axis):
        bits.append((axis, bit))
        bit *= 2
    return bits


def bit_of(stage):
    axis, bit = stage
    return ((lax.axis_index(axis) & bit) != 0).astype(jnp.int32)


def scatter_stage(tiles, stage):
    n = tiles.shape[0] // 2
    bit = bit_of(stage)
    send = lax.dynamic_slice_in_dim(tiles, (1 - bit) * n, n, 0)
    keep = lax.dynamic_slice_in_dim(tiles, bit * n, n, 0)
    recv = permute_xor(send, *stage)
    return (keep.astype(f32) + recv.astype(f32)).astype(bf16)


def gather_stage(tiles, stage):
    return jnp.concatenate([tiles, permute_xor(tiles, *stage)], axis=0)


def body(
    hidden,
    frozen_query_rows,
    frozen_key_rows,
    frozen_value_rows,
    next_output_gradient,
    document_lengths,
    document_adapter,
    adapter_down_maps,
    adapter_up_maps,
):
    tok, model_width = hidden.shape[1:]
    kv_width = frozen_key_rows.shape[2]
    kv_heads = kv_width // HD
    _, adapters, rank, _ = adapter_up_maps.shape
    width = 2 * adapters * rank
    half = width // 2
    ctx_index, ctx_size = lax.axis_index("ctx"), lax.axis_size("ctx")
    longest = tok * ctx_size // 4
    reach = min(-(-(min(WINDOW, longest) - 1) // tok), ctx_size - 1)
    steps = (reach + 1) // 2

    splits = SPLITS if kv_heads % SPLITS == 0 else 1
    per = kv_heads // splits
    keys, vals = frozen_key_rows[0], frozen_value_rows[0]
    parts = []
    for i in range(splits):
        cut = slice(i * per * HD, (i + 1) * per * HD)
        own = jnp.concatenate([keys[:, cut], vals[:, cut]], axis=1)
        parts.append([[own]] + window_blocks(own, steps))
    returned = permute_cyclic(next_output_gradient, "section", -1)

    block_starts = jnp.stack([(ctx_index - d) * tok for d in range(2 * steps + 1)])
    key_pos = (block_starts[:, None] + jnp.arange(tok, dtype=jnp.int32)[None, :]).reshape(-1)
    key_docs = doc_index(document_lengths[0], key_pos)
    positions, docs = key_pos[:tok], key_docs[:tok]
    picked = docs[:, None] == jnp.arange(document_lengths.shape[1], dtype=jnp.int32)[None, :]
    tenant = jnp.sum(picked.astype(jnp.int32) * document_adapter[0][None, :], axis=1)
    lane_adapter = (jnp.arange(width, dtype=jnp.int32) // rank) % adapters
    mask = (tenant[:, None] == lane_adapter[None, :]).astype(f32)
    gap = positions[None, :] - key_pos[:, None]
    allowed = (
        (key_docs[:, None] == docs[None, :])
        & (gap >= 0)
        & (gap < WINDOW)
        & (key_pos >= 0)[:, None]
    )
    bias = jnp.where(allowed, 0.0, masked_score).astype(f32)
    frequency = rope_base ** (-(jnp.arange(HD // 2, dtype=f32) * 2.0) / HD)
    angles = key_pos.astype(f32)[:, None] * frequency[None, :]
    cos_half, sin_half = jnp.cos(angles), jnp.sin(angles)
    cos = jnp.concatenate([cos_half, cos_half], axis=1)
    sin = jnp.concatenate([-sin_half, sin_half], axis=1)

    low = jnp.dot(
        hidden[0], adapter_down_maps.reshape(model_width, width), preferred_element_type=f32
    )
    spread_own = (low * mask).astype(bf16)
    spread = jnp.concatenate(
        [spread_own]
        + [sum(b[1:], b[0]) for b in window_blocks(spread_own, steps)],
        axis=0,
    )
    up_flat = adapter_up_maps.reshape(2, half, kv_heads, HD)
    zero = jnp.zeros((kv_heads, half, HD), bf16)
    up_heads = jnp.moveaxis(up_flat, 2, 1)
    up_cat = jnp.concatenate(
        [
            jnp.concatenate([up_heads[0], zero], axis=2),
            jnp.concatenate([zero, up_heads[1]], axis=2),
        ],
        axis=1,
    )

    outs, lgs, ups = [], [], []
    for i in range(splits):
        out, lg, u = attention(
            parts[i],
            i * per,
            frozen_query_rows[0],
            returned[0],
            spread,
            up_cat,
            bias,
            cos,
            sin,
        )
        outs.append(permute_cyclic(out, "section", 1))
        lgs.append(lg)
        ups.append(u)
    handed = jnp.concatenate(outs, axis=1)[None]

    lg = sum(lgs[1:], lgs[0]).reshape(2 * steps + 1, tok, width)
    received = [permute_by(lg[d].astype(bf16), "ctx", -d) for d in range(1, 2 * steps + 1)]

    other = (
        axis_bits("ctx")[:1] + axis_bits("dp"),
        axis_bits("dp") + axis_bits("ctx")[:1],
    )
    tail = axis_bits("ctx")[1:]
    group = lax.axis_size("ctx") * lax.axis_size("dp")
    cols, up_cols, rows = model_width // HD, kv_heads, half // SUB
    units = -(-(rows * (cols + up_cols)) // group)
    a = (units + 1) // 2
    b = units - a
    side = lax.axis_index("section").astype(jnp.int32)
    smem = pl.BlockSpec(memory_space=pltpu.SMEM)
    vmem = pl.BlockSpec(memory_space=pltpu.VMEM)
    keep, send = pl.pallas_call(
        partial(
            product_kernel, n_recv=len(received), n_up=len(ups), cols=cols, up_cols=up_cols
        ),
        in_specs=[smem] + [vmem] * (3 + len(received) + len(ups)),
        out_specs=[vmem, vmem],
        out_shape=[jax.ShapeDtypeStruct((units * group, SUB, HD), bf16)] * 2,
        name="product",
    )(side[None], lg[0], *received, adapter_scale * mask, hidden[0], *ups)
    recv = permute_cyclic(send, "section", 1)
    tiles = (keep.astype(f32) + recv.astype(f32)).astype(bf16)
    colours = [tiles[: a * group], tiles[a * group :]]
    ids = []
    stages = [list(other[c]) + list(tail) for c in range(2)]
    for k in range(len(stages[0])):
        colours = [scatter_stage(colours[c], stages[c][k]) for c in range(2)]
    for c in range(2):
        me = jnp.int32(0)
        for stage in stages[c]:
            me = me * 2 + bit_of(stage)
        ids.append(me)
    for k in reversed(range(len(stages[0]))):
        colours = [gather_stage(colours[c], stages[c][k]) for c in range(2)]
    theirs = [permute_cyclic(t, "section", 1) for t in colours]
    shapes = [(group, a, SUB, HD), (group, b, SUB, HD)]
    w, u = pl.pallas_call(
        partial(assemble_kernel, cols=cols, rows=rows),
        in_specs=[smem] + [vmem] * 4,
        out_specs=[vmem, vmem],
        out_shape=[
            jax.ShapeDtypeStruct((width, model_width), f32),
            jax.ShapeDtypeStruct((width, kv_width), f32),
        ],
        name="assemble",
    )(
        jnp.stack([side, ids[0], ids[1]]),
        colours[0].reshape(shapes[0]),
        colours[1].reshape(shapes[1]),
        theirs[0].reshape(shapes[0]),
        theirs[1].reshape(shapes[1]),
    )
    down_map_gradient = w.T.reshape(model_width, 2, adapters, rank)
    up_map_gradient = u.reshape(2, adapters, rank, kv_width)
    return (handed, down_map_gradient, up_map_gradient)


def solution(mesh):
    return jax.shard_map(
        body,
        mesh=mesh,
        in_specs=(
            P(("section", "dp"), "ctx", None),
            P(("section", "dp"), "ctx", None),
            P(("section", "dp"), "ctx", None),
            P(("section", "dp"), "ctx", None),
            P(("section", "dp"), "ctx", None),
            P(("section", "dp"), None),
            P(("section", "dp"), None),
            P(),
            P(),
        ),
        out_specs=(P(("section", "dp"), "ctx", None), P(), P()),
        check_vma=False,
    )
```

time: 642 us -> 165 us (0.26)
  waiting for transfers between devices: 336 us -> 48.2 us
  matrix products: 123 us -> 2.75 us
  local copies, waits for them, and re-layouts: 75.9 us -> 5.63 us
  Pallas kernels: 0 us -> 36.2 us
  other arithmetic: 39.1 us -> 12.5 us
  between operations: 14.5 us -> 1.46 us
  starting transfers between devices: 50.3 us -> 57.5 us
    ppermute x18 -> x41, waiting for transfers between devices: 204 us -> 48.2 us  [the longest x16 30.6 us: permute_xor(): return lax.ppermute(value, axis, [(i, i ^ bit) for i in range(count)])]
    psum x1 -> x0, waiting for transfers between devices: 131 us -> none  [body(): lax.psum((down_map_gradient, up_map_gradient), ('section', 'ctx', 'dp'))]
    dot_general x48 -> x1, matrix products: 123 us -> 2.75 us  [body(): jnp.dot(hidden[0], adapter_down_maps.reshape(model_width, width), preferr...]
    pallas_call x0 -> x6, Pallas kernels: none -> 36.2 us  [the longest x4 29 us: attention(): pl.pallas_call(partial(attention_kernel, counts=counts, tok=tok, group=gr...]
    unnamed x52 -> x57, local copies, waits for them, and re-layouts: 26.1 us -> 2.41 us
    dynamic_update_slice x16 -> x0, local copies, waits for them, and re-layouts: 17.7 us -> none  [body(): lax.map(partial(group_backward, allowed=allowed), (query_groups, key_grou...]
    reduce_sum x17 -> x1, other arithmetic: 13.6 us -> 0.09 us  [body(): jnp.sum(picked.astype(jnp.int32) * document_adapter[0][None, :], axis=1)]
    and x16 -> x0, other arithmetic: 8.9 us -> none  [body(): (doc_ids[:, None] == key_docs[None, :]) & (key_gap >= 0)]
  transfers between devices with their start and end apart: 19 -> 41, of which waited for: 17 -> 18; matrix products, arithmetic and copies ran while one was open for 14% -> 8% of each run, Pallas kernels for 0% -> 13%
where the time goes in v1:
time: 165 us; the launch traced here: 164 us
  starting transfers between devices  57.5 us (35%)
  waiting for transfers between devices  48.2 us (29%)
  Pallas kernels  36.2 us (22%)
  other arithmetic  12.5 us (8%)
  local copies, waits for them, and re-layouts  5.63 us (3%)
  matrix products  2.75 us (2%)
    ppermute x16, waiting for transfers between devices, permute_xor(): return lax.ppermute(value, axis, [(i, i ^ bit) for i in range(count)])  30.6 us
    pallas_call x4, Pallas kernels, attention(): pl.pallas_call(partial(attention_kernel, counts=counts, tok=tok, group=gr...  29 us
    ppermute x7, starting transfers between devices, permute_by(): lax.ppermute(value, axis, [(i, i + steps) for i in range(first, last)])  19.2 us
    ppermute x16, starting transfers between devices, permute_xor(): return lax.ppermute(value, axis, [(i, i ^ bit) for i in range(count)])  16.9 us
    ppermute x5, starting transfers between devices, window_blocks(): lax.ppermute(chain[i], 'ctx', even_to_odd)  13.5 us
    ppermute x7, waiting for transfers between devices, permute_by(): lax.ppermute(value, axis, [(i, i + steps) for i in range(first, last)])  7.82 us
    ppermute x5, starting transfers between devices, window_blocks(): lax.ppermute(chain[i + 1], 'ctx', odd_to_even)  6.63 us
    ppermute x5, waiting for transfers between devices, window_blocks(): lax.ppermute(chain[i + 1], 'ctx', odd_to_even)  4.81 us
  transfers between devices with their start and end apart: 41, of which 18 were waited for; matrix products, arithmetic and copies ran while one was open for 8% of the time, Pallas kernels for 13%

profile of v1, /device:TPU:0, one launch (start us, length us, event | category | flops | bytes accessed | tf_op | source)
XLA Modules:
  0.0 164.2 jit_solution(474692834885636943)
XLA Ops:
  2.9 5.7 %collective-permute-start.1 = (bf16[256,512]{1,0:T(8,128)(2,1)S(1)}, bf16[256,512]{1,0:T(8,128)(2,1)}, u32[]{:S(2)}, u32[]{:S(2)}) collective-permute-start(bf16[256,512]{1,0:T(8,128)(2,1)S(1)} %pad_maximum_fusion.2.refs_0_.refs_4_), channel_id=1, source_target_pairs={{0,4},{2,6},{4,8},{6,10},{8,12},{10,14},{1,5},{3,7},{5,9},{7,11},{... | collective-permute-start | bytes 786440 | tf_op jit(solution)/shard_map/ppermute | solution.py:26
  8.5 4.1 %collective-permute-start = (bf16[256,512]{1,0:T(8,128)(2,1)S(1)}, bf16[256,512]{1,0:T(8,128)(2,1)}, u32[]{:S(2)}, u32[]{:S(2)}) collective-permute-start(bf16[256,512]{1,0:T(8,128)(2,1)S(1)} %pad_maximum_fusion.2.refs_0_.refs_4_), channel_id=1, source_target_pairs={{0,2},{4,6},{8,10},{12,14},{1,3},{5,7},{9,11},{13,15},{16,18},{20,... | collective-permute-start | bytes 786440 | tf_op jit(solution)/shard_map/ppermute | solution.py:50
  13.3 2.8 %fusion = bf16[256,128]{1,0:T(8,128)(2,1)S(1)} fusion(bf16[5376,128]{0,1:T(8,128)(2,1)S(1)} %bitcast.40, s32[128]{0:T(128)S(1)} %and_select_fusion, s32[256]{0:T(256)S(1)} %select_reduce_fusion, bf16[1,256,5376]{2,1,0:T(8,128)(2,1)} %param.9), kind=kOutput, calls=%fused_computation.4 | convolution fusion | flops 352419840 | bytes 4195840 | tf_op jit(solution)/shard_map/dot_general | solution.py:318
  16.1 2.9 %collective-permute-start.5 = (bf16[256,128]{1,0:T(8,128)(2,1)S(1)}, bf16[256,128]{1,0:T(8,128)(2,1)S(1)}, u32[]{:S(2)}, u32[]{:S(2)}) collective-permute-start(bf16[256,128]{1,0:T(8,128)(2,1)S(1)} %fusion), channel_id=1, source_target_pairs={{0,4},{2,6},{4,8},{6,10},{8,12},{10,14},{1,5},{3,7},{5,9},{7,11},{... | collective-permute-start | bytes 196616 | tf_op jit(solution)/shard_map/ppermute | solution.py:26
  19.1 4.2 %collective-permute-start.9 = (bf16[256,512]{1,0:T(8,128)(2,1)S(1)}, bf16[256,512]{1,0:T(8,128)(2,1)}, u32[]{:S(2)}, u32[]{:S(2)}) collective-permute-start(bf16[256,512]{1,0:T(8,128)(2,1)S(1)} %pad_maximum_fusion.3.refs_0_.refs_4_), channel_id=1, source_target_pairs={{0,4},{2,6},{4,8},{6,10},{8,12},{10,14},{1,5},{3,7},{5,9},{7,11},{... | collective-permute-start | bytes 786440 | tf_op jit(solution)/shard_map/ppermute | solution.py:26
  29.6 4.8 %collective-permute-done.6 = bf16[256,128]{1,0:T(8,128)(2,1)S(1)} collective-permute-done((bf16[256,128]{1,0:T(8,128)(2,1)S(1)}, bf16[256,128]{1,0:T(8,128)(2,1)S(1)}, u32[]{:S(2)}, u32[]{:S(2)}) %collective-permute-start.6) | collective-permute-done | bytes 65568 | tf_op jit(solution)/shard_map/ppermute | solution.py:51
  36.0 2.2 %collective-permute-start.13 = (bf16[256,512]{1,0:T(8,128)(2,1)S(1)}, bf16[256,512]{1,0:T(8,128)(2,1)}, u32[]{:S(2)}, u32[]{:S(2)}) collective-permute-start(bf16[256,512]{1,0:T(8,128)(2,1)S(1)} %pad_maximum_fusion.4.refs_0_.refs_4_), channel_id=1, source_target_pairs={{0,4},{2,6},{4,8},{6,10},{8,12},{10,14},{1,5},{3,7},{5,9},{7,11},{... | collective-permute-start | bytes 786440 | tf_op jit(solution)/shard_map/ppermute | solution.py:26
  42.4 5.3 %collective-permute-start.12 = (bf16[256,512]{1,0:T(8,128)(2,1)S(1)}, bf16[256,512]{1,0:T(8,128)(2,1)}, u32[]{:S(2)}, u32[]{:S(2)}) collective-permute-start(bf16[256,512]{1,0:T(8,128)(2,1)S(1)} %pad_maximum_fusion.4.refs_0_.refs_4_), channel_id=1, source_target_pairs={{0,2},{4,6},{8,10},{12,14},{1,3},{5,7},{9,11},{13,15},{16,18},{20,... | collective-permute-start | bytes 786440 | tf_op jit(solution)/shard_map/ppermute | solution.py:50
  55.8 7.2 %attention.4 = (bf16[256,512]{1,0:T(8,128)(2,1)}, f32[768,128]{1,0:T(8,128)}, bf16[2,64,256]{2,1,0:T(8,128)(2,1)}) custom-call(bf16[256,512]{1,0:T(8,128)(2,1)} %copy-done.2, bf16[256,512]{1,0:T(8,128)(2,1)} %collective-permute-done.refs_1_.refs_5_, bf16[256,512]{1,0:T(8,128)(2,1)} %copy-done.9, bf16[256,512]{1,0:T(8,128)(2,1)} %collective-permute-done.1.refs_3_.refs_7_, ...), custom_call_target="tpu_custom_call" | custom-call | tf_op jit(solution)/shard_map/attention/pallas_call | solution.py:152
  63.1 7.2 %attention.5 = (bf16[256,512]{1,0:T(8,128)(2,1)}, f32[768,128]{1,0:T(8,128)}, bf16[2,64,256]{2,1,0:T(8,128)(2,1)}) custom-call(bf16[256,512]{1,0:T(8,128)(2,1)} %copy-done.3, bf16[256,512]{1,0:T(8,128)(2,1)} %copy-done.7, bf16[256,512]{1,0:T(8,128)(2,1)} %collective-permute-done.10.refs_2_.refs_6_, bf16[256,512]{1,0:T(8,128)(2,1)} %collective-permute-done.9.refs_3_.refs_7_, ...), custom_call_target="tpu_custom_call" | custom-call | tf_op jit(solution)/shard_map/attention/pallas_call | solution.py:152
  70.3 7.3 %attention.6 = (bf16[256,512]{1,0:T(8,128)(2,1)}, f32[768,128]{1,0:T(8,128)}, bf16[2,64,256]{2,1,0:T(8,128)(2,1)}) custom-call(bf16[256,512]{1,0:T(8,128)(2,1)} %copy-done.5, bf16[256,512]{1,0:T(8,128)(2,1)} %collective-permute-done.12.refs_1_.refs_5_, bf16[256,512]{1,0:T(8,128)(2,1)} %collective-permute-done.14.refs_2_.refs_6_, ...), custom_call_target="tpu_custom_call" | custom-call | tf_op jit(solution)/shard_map/attention/pallas_call | solution.py:152
  78.3 7.3 %attention.7 = (bf16[256,512]{1,0:T(8,128)(2,1)}, f32[768,128]{1,0:T(8,128)}, bf16[2,64,256]{2,1,0:T(8,128)(2,1)}) custom-call(bf16[256,512]{1,0:T(8,128)(2,1)} %copy-done.4, bf16[256,512]{1,0:T(8,128)(2,1)} %copy-done.8, bf16[256,512]{1,0:T(8,128)(2,1)} %collective-permute-done.18.refs_2_.refs_6_, bf16[256,512]{1,0:T(8,128)(2,1)} %copy-done.6, ...), custom_call_target="tpu_custom_call" | custom-call | tf_op jit(solution)/shard_map/attention/pallas_call | solution.py:152
  91.0 4.4 %collective-permute-done.20.refs_2_ = bf16[256,128]{1,0:T(8,128)(2,1)S(1)} collective-permute-done((bf16[256,128]{1,0:T(8,128)(2,1)S(1)}, bf16[256,128]{1,0:T(8,128)(2,1)S(1)}, u32[]{:S(2)}, u32[]{:S(2)}) %collective-permute-start.20) | collective-permute-done | bytes 65568 | tf_op jit(solution)/shard_map/ppermute | solution.py:26
  95.4 3.4 %collective-permute-done.21.refs_3_ = bf16[256,128]{1,0:T(8,128)(2,1)S(1)} collective-permute-done((bf16[256,128]{1,0:T(8,128)(2,1)S(1)}, bf16[256,128]{1,0:T(8,128)(2,1)S(1)}, u32[]{:S(2)}, u32[]{:S(2)}) %collective-permute-start.21) | collective-permute-done | bytes 65568 | tf_op jit(solution)/shard_map/ppermute | solution.py:26
  99.4 3.9 %product.1 = (bf16[400,8,128]{2,1,0:T(8,128)(2,1)}, bf16[400,8,128]{2,1,0:T(8,128)(2,1)}) custom-call(s32[1]{0:T(128)} %bitcast.16.refs_0_, f32[256,128]{1,0:T(8,128)} %slice.85.refs_1_, bf16[256,128]{1,0:T(8,128)(2,1)} %copy-done.20, bf16[256,128]{1,0:T(8,128)(2,1)} %copy-done.21, f32[256,128]{1,0:T(8,128)} %compare_select_fusion.refs_4_, ...), custom_call_target="tpu_custom_call" | custom-call | tf_op jit(solution)/shard_map/product/pallas_call | solution.py:372
  103.3 2.5 %collective-permute-done.22 = bf16[400,8,128]{2,1,0:T(8,128)(2,1)S(1)} collective-permute-done((bf16[400,8,128]{2,1,0:T(8,128)(2,1)}, bf16[400,8,128]{2,1,0:T(8,128)(2,1)S(1)}, u32[]{:S(2)}, u32[]{:S(2)}) %collective-permute-start.22) | collective-permute-done | bytes 819232 | tf_op jit(solution)/shard_map/ppermute | solution.py:31
  110.0 4.2 %collective-permute-done.31 = bf16[96,8,128]{2,1,0:T(8,128)(2,1)S(1)} collective-permute-done((bf16[96,8,128]{2,1,0:T(8,128)(2,1)S(1)}, bf16[96,8,128]{2,1,0:T(8,128)(2,1)S(1)}, u32[]{:S(2)}, u32[]{:S(2)}) %collective-permute-start.31) | collective-permute-done | bytes 196640 | tf_op jit(solution)/shard_map/ppermute | solution.py:36
  115.0 2.6 %collective-permute-done.23 = bf16[104,8,128]{2,1,0:T(8,128)(2,1)S(1)} collective-permute-done((bf16[104,8,128]{2,1,0:T(8,128)(2,1)S(1)}, bf16[104,8,128]{2,1,0:T(8,128)(2,1)S(1)}, u32[]{:S(2)}, u32[]{:S(2)}) %collective-permute-start.23) | collective-permute-done | bytes 213024 | tf_op jit(solution)/shard_map/ppermute | solution.py:36
  123.5 2.7 %collective-permute-start.34 = (bf16[12,8,128]{2,1,0:T(8,128)(2,1)S(1)}, bf16[12,8,128]{2,1,0:T(8,128)(2,1)S(1)}, u32[]{:S(2)}, u32[]{:S(2)}) collective-permute-start(bf16[12,8,128]{2,1,0:T(8,128)(2,1)S(1)} %constant_dynamic-slice_fusion), channel_id=1, source_target_pairs={{0,8},{2,10},{4,12},{6,14},{8,0},{10,2},{12,4},{14,6},{1,9},{3,11}... | collective-permute-start | bytes 73736 | tf_op jit(solution)/shard_map/ppermute | solution.py:36
  128.3 2.8 %collective-permute-start.35 = (bf16[12,8,128]{2,1,0:T(8,128)(2,1)S(1)}, bf16[12,8,128]{2,1,0:T(8,128)(2,1)S(1)}, u32[]{:S(2)}, u32[]{:S(2)}) collective-permute-start(bf16[12,8,128]{2,1,0:T(8,128)(2,1)S(1)} %get-tuple-element.36), channel_id=1, source_target_pairs={{0,8},{2,10},{4,12},{6,14},{8,0},{10,2},{12,4},{14,6},{1,9},{3,11}... | collective-permute-start | bytes 73736 | tf_op jit(solution)/shard_map/ppermute | solution.py:36
  136.5 4.4 %collective-permute-done.27 = bf16[13,8,128]{2,1,0:T(8,128)(2,1)S(1)} collective-permute-done((bf16[13,8,128]{2,1,0:T(8,128)(2,1)S(1)}, bf16[13,8,128]{2,1,0:T(8,128)(2,1)S(1)}, u32[]{:S(2)}, u32[]{:S(2)}) %collective-permute-start.27) | collective-permute-done | bytes 26656 | tf_op jit(solution)/shard_map/ppermute | solution.py:36
  141.5 3.7 %collective-permute-done.28 = bf16[26,8,128]{2,1,0:T(8,128)(2,1)S(1)} collective-permute-done((bf16[26,8,128]{2,1,0:T(8,128)(2,1)S(1)}, bf16[26,8,128]{2,1,0:T(8,128)(2,1)S(1)}, u32[]{:S(2)}, u32[]{:S(2)}) %collective-permute-start.28) | collective-permute-done | bytes 53280 | tf_op jit(solution)/shard_map/ppermute | solution.py:36
  150.4 5.5 %collective-permute-done.30 = bf16[104,8,128]{2,1,0:T(8,128)(2,1)S(1)} collective-permute-done((bf16[104,8,128]{2,1,0:T(8,128)(2,1)S(1)}, bf16[104,8,128]{2,1,0:T(8,128)(2,1)S(1)}, u32[]{:S(2)}, u32[]{:S(2)}) %collective-permute-start.30) | collective-permute-done | bytes 213024 | tf_op jit(solution)/shard_map/ppermute | solution.py:36
  160.9 3.4 %assemble.1 = (f32[128,5376]{1,0:T(8,128)}, f32[128,1024]{1,0:T(8,128)}) custom-call(s32[3]{0:T(128)} %pad_add_fusion.1.scalars_ref, bf16[16,13,8,128]{3,2,1,0:T(8,128)(2,1)} %bitcast.54, bf16[16,12,8,128]{3,2,1,0:T(8,128)(2,1)} %bitcast.55, bf16[16,13,8,128]{3,2,1,0:T(8,128)(2,1)} %bitcast.56, bf16[16,12,8,128]{3,2,1,0:T(8,128)(2,1)} %bitcast.57), custom_call_target="tpu_custom_call" | custom-call | tf_op jit(solution)/shard_map/assemble/pallas_call | solution.py:397
  (182 shorter events, 58.2 us)
Async XLA Ops:
  2.9 33.1 %collective-permute-start.1 = (bf16[256,512]{1,0:T(8,128)(2,1)S(1)}, bf16[256,512]{1,0:T(8,128)(2,1)}, u32[]{:S(2)}, u32[]{:S(2)}) collective-permute-start(bf16[256,512]{1,0:T(8,128)(2,1)S(1)} %pad_maximum_fusion.2.refs_0_.refs_4_), channel_id=1, source_target_pairs={{0,4},{2,6},{4,8},{6,10},{8,12},{10,14},{1,5},{3,7},{5,9},{7,11},{... | collective-permute-start | bytes 786440 | tf_op jit(solution)/shard_map/ppermute | solution.py:26
  8.5 29.7 %collective-permute-start = (bf16[256,512]{1,0:T(8,128)(2,1)S(1)}, bf16[256,512]{1,0:T(8,128)(2,1)}, u32[]{:S(2)}, u32[]{:S(2)}) collective-permute-start(bf16[256,512]{1,0:T(8,128)(2,1)S(1)} %pad_maximum_fusion.2.refs_0_.refs_4_), channel_id=1, source_target_pairs={{0,2},{4,6},{8,10},{12,14},{1,3},{5,7},{9,11},{13,15},{16,18},{20,... | collective-permute-start | bytes 786440 | tf_op jit(solution)/shard_map/ppermute | solution.py:50
  16.1 8.9 %collective-permute-start.5 = (bf16[256,128]{1,0:T(8,128)(2,1)S(1)}, bf16[256,128]{1,0:T(8,128)(2,1)S(1)}, u32[]{:S(2)}, u32[]{:S(2)}) collective-permute-start(bf16[256,128]{1,0:T(8,128)(2,1)S(1)} %fusion), channel_id=1, source_target_pairs={{0,4},{2,6},{4,8},{6,10},{8,12},{10,14},{1,5},{3,7},{5,9},{7,11},{... | collective-permute-start | bytes 196616 | tf_op jit(solution)/shard_map/ppermute | solution.py:26
  19.0 32.6 %collective-permute-start.3 = (bf16[1,256,2048]{2,1,0:T(8,128)(2,1)S(1)}, bf16[1,256,2048]{2,1,0:T(8,128)(2,1)S(1)}, u32[]{:S(2)}, u32[]{:S(2)}) collective-permute-start(bf16[1,256,2048]{2,1,0:T(8,128)(2,1)S(1)} %copy-done.24), channel_id=1, source_target_pairs={{0,16},{16,0},{1,17},{17,1},{2,18},{18,2},{3,19},{19,3},{4,20},{20... | collective-permute-start | bytes 3145736 | tf_op jit(solution)/shard_map/ppermute | solution.py:31
  19.1 20.5 %collective-permute-start.9 = (bf16[256,512]{1,0:T(8,128)(2,1)S(1)}, bf16[256,512]{1,0:T(8,128)(2,1)}, u32[]{:S(2)}, u32[]{:S(2)}) collective-permute-start(bf16[256,512]{1,0:T(8,128)(2,1)S(1)} %pad_maximum_fusion.3.refs_0_.refs_4_), channel_id=1, source_target_pairs={{0,4},{2,6},{4,8},{6,10},{8,12},{10,14},{1,5},{3,7},{5,9},{7,11},{... | collective-permute-start | bytes 786440 | tf_op jit(solution)/shard_map/ppermute | solution.py:26
  28.2 6.1 %collective-permute-start.6 = (bf16[256,128]{1,0:T(8,128)(2,1)S(1)}, bf16[256,128]{1,0:T(8,128)(2,1)S(1)}, u32[]{:S(2)}, u32[]{:S(2)}) collective-permute-start(bf16[256,128]{1,0:T(8,128)(2,1)S(1)} %collective-permute-done.5), channel_id=1, source_target_pairs={{2,0},{6,4},{10,8},{14,12},{3,1},{7,5},{11,9},{15,13},{18,16},{22,... | collective-permute-start | bytes 196616 | tf_op jit(solution)/shard_map/ppermute | solution.py:51
  34.4 8.0 %collective-permute-start.8 = (bf16[256,512]{1,0:T(8,128)(2,1)S(1)}, bf16[256,512]{1,0:T(8,128)(2,1)S(1)}, u32[]{:S(2)}, u32[]{:S(2)}) collective-permute-start(bf16[256,512]{1,0:T(8,128)(2,1)S(1)} %pad_maximum_fusion.3.refs_0_.refs_4_), channel_id=1, source_target_pairs={{0,2},{4,6},{8,10},{12,14},{1,3},{5,7},{9,11},{13,15},{16,18},{20,... | collective-permute-start | bytes 786440 | tf_op jit(solution)/shard_map/ppermute | solution.py:50
  36.0 11.7 %collective-permute-start.13 = (bf16[256,512]{1,0:T(8,128)(2,1)S(1)}, bf16[256,512]{1,0:T(8,128)(2,1)}, u32[]{:S(2)}, u32[]{:S(2)}) collective-permute-start(bf16[256,512]{1,0:T(8,128)(2,1)S(1)} %pad_maximum_fusion.4.refs_0_.refs_4_), channel_id=1, source_target_pairs={{0,4},{2,6},{4,8},{6,10},{8,12},{10,14},{1,5},{3,7},{5,9},{7,11},{... | collective-permute-start | bytes 786440 | tf_op jit(solution)/shard_map/ppermute | solution.py:26
  38.2 10.8 %collective-permute-start.17 = (bf16[256,512]{1,0:T(8,128)(2,1)S(1)}, bf16[256,512]{1,0:T(8,128)(2,1)S(1)}, u32[]{:S(2)}, u32[]{:S(2)}) collective-permute-start(bf16[256,512]{1,0:T(8,128)(2,1)S(1)} %pad_maximum_fusion.5.refs_0_.refs_4_), channel_id=1, source_target_pairs={{0,4},{2,6},{4,8},{6,10},{8,12},{10,14},{1,5},{3,7},{5,9},{7,11},{... | collective-permute-start | bytes 786440 | tf_op jit(solution)/shard_map/ppermute | solution.py:26
  39.6 10.7 %collective-permute-start.2 = (bf16[256,512]{1,0:T(8,128)(2,1)}, bf16[256,512]{1,0:T(8,128)(2,1)S(1)}, u32[]{:S(2)}, u32[]{:S(2)}) collective-permute-start(bf16[256,512]{1,0:T(8,128)(2,1)} %collective-permute-done.1.refs_3_.refs_7_), channel_id=1, source_target_pairs={{2,0},{6,4},{10,8},{14,12},{3,1},{7,5},{11,9},{15,13},{18,16},{22,... | collective-permute-start | bytes 786440 | tf_op jit(solution)/shard_map/ppermute | solution.py:51
  42.4 27.9 %collective-permute-start.12 = (bf16[256,512]{1,0:T(8,128)(2,1)S(1)}, bf16[256,512]{1,0:T(8,128)(2,1)}, u32[]{:S(2)}, u32[]{:S(2)}) collective-permute-start(bf16[256,512]{1,0:T(8,128)(2,1)S(1)} %pad_maximum_fusion.4.refs_0_.refs_4_), channel_id=1, source_target_pairs={{0,2},{4,6},{8,10},{12,14},{1,3},{5,7},{9,11},{13,15},{16,18},{20,... | collective-permute-start | bytes 786440 | tf_op jit(solution)/shard_map/ppermute | solution.py:50
  47.7 29.9 %collective-permute-start.16 = (bf16[256,512]{1,0:T(8,128)(2,1)S(1)}, bf16[256,512]{1,0:T(8,128)(2,1)S(1)}, u32[]{:S(2)}, u32[]{:S(2)}) collective-permute-start(bf16[256,512]{1,0:T(8,128)(2,1)S(1)} %pad_maximum_fusion.5.refs_0_.refs_4_), channel_id=1, source_target_pairs={{0,2},{4,6},{8,10},{12,14},{1,3},{5,7},{9,11},{13,15},{16,18},{20,... | collective-permute-start | bytes 786440 | tf_op jit(solution)/shard_map/ppermute | solution.py:50
  49.0 14.1 %collective-permute-start.10 = (bf16[256,512]{1,0:T(8,128)(2,1)}, bf16[256,512]{1,0:T(8,128)(2,1)}, u32[]{:S(2)}, u32[]{:S(2)}) collective-permute-start(bf16[256,512]{1,0:T(8,128)(2,1)} %collective-permute-done.9.refs_3_.refs_7_), channel_id=1, source_target_pairs={{2,0},{6,4},{10,8},{14,12},{3,1},{7,5},{11,9},{15,13},{18,16},{22,... | collective-permute-start | bytes 786440 | tf_op jit(solution)/shard_map/ppermute | solution.py:51
  50.3 20.0 %collective-permute-start.14 = (bf16[256,512]{1,0:T(8,128)(2,1)}, bf16[256,512]{1,0:T(8,128)(2,1)}, u32[]{:S(2)}, u32[]{:S(2)}) collective-permute-start(bf16[256,512]{1,0:T(8,128)(2,1)} %collective-permute-done.13.refs_3_.refs_7_), channel_id=1, source_target_pairs={{2,0},{6,4},{10,8},{14,12},{3,1},{7,5},{11,9},{15,13},{18,16},{22,... | collective-permute-start | bytes 786440 | tf_op jit(solution)/shard_map/ppermute | solution.py:51
  51.6 26.0 %collective-permute-start.18 = (bf16[256,512]{1,0:T(8,128)(2,1)S(1)}, bf16[256,512]{1,0:T(8,128)(2,1)}, u32[]{:S(2)}, u32[]{:S(2)}) collective-permute-start(bf16[256,512]{1,0:T(8,128)(2,1)S(1)} %collective-permute-done.17.refs_3_.refs_7_), channel_id=1, source_target_pairs={{2,0},{6,4},{10,8},{14,12},{3,1},{7,5},{11,9},{15,13},{18,16},{22,... | collective-permute-start | bytes 786440 | tf_op jit(solution)/shard_map/ppermute | solution.py:51
  86.7 8.7 %collective-permute-start.20 = (bf16[256,128]{1,0:T(8,128)(2,1)S(1)}, bf16[256,128]{1,0:T(8,128)(2,1)S(1)}, u32[]{:S(2)}, u32[]{:S(2)}) collective-permute-start(bf16[256,128]{1,0:T(8,128)(2,1)S(1)} %get-tuple-element.52), channel_id=1, source_target_pairs={{2,0},{4,2},{6,4},{8,6},{10,8},{12,10},{14,12},{3,1},{5,3},{7,5},{... | collective-permute-start | bytes 196616 | tf_op jit(solution)/shard_map/ppermute | solution.py:26
  88.0 10.7 %collective-permute-start.21 = (bf16[256,128]{1,0:T(8,128)(2,1)S(1)}, bf16[256,128]{1,0:T(8,128)(2,1)S(1)}, u32[]{:S(2)}, u32[]{:S(2)}) collective-permute-start(bf16[256,128]{1,0:T(8,128)(2,1)S(1)} %get-tuple-element.51), channel_id=1, source_target_pairs={{4,0},{6,2},{8,4},{10,6},{12,8},{14,10},{5,1},{7,3},{9,5},{11,7},{... | collective-permute-start | bytes 196616 | tf_op jit(solution)/shard_map/ppermute | solution.py:26
  107.2 7.0 %collective-permute-start.31 = (bf16[96,8,128]{2,1,0:T(8,128)(2,1)S(1)}, bf16[96,8,128]{2,1,0:T(8,128)(2,1)S(1)}, u32[]{:S(2)}, u32[]{:S(2)}) collective-permute-start(bf16[96,8,128]{2,1,0:T(8,128)(2,1)S(1)} %constant_dynamic-slice_fusion.3), channel_id=1, source_target_pairs={{0,1},{1,0},{2,3},{3,2},{4,5},{5,4},{6,7},{7,6},{8,9},{9,8},{10,11... | collective-permute-start | bytes 589832 | tf_op jit(solution)/shard_map/ppermute | solution.py:36
  108.8 47.8 %collective-permute-start.7 = (bf16[256,512]{1,0:T(8,128)(2,1)}, bf16[256,512]{1,0:T(8,128)(2,1)S(1)}, u32[]{:S(2)}, u32[]{:S(2)}) collective-permute-start(bf16[256,512]{1,0:T(8,128)(2,1)} %get-tuple-element.19), channel_id=1, source_target_pairs={{0,16},{16,0},{1,17},{17,1},{2,18},{18,2},{3,19},{19,3},{4,20},{20... | collective-permute-start | bytes 786440 | tf_op jit(solution)/shard_map/ppermute | solution.py:31
  108.8 48.5 %collective-permute-start.11 = (bf16[256,512]{1,0:T(8,128)(2,1)}, bf16[256,512]{1,0:T(8,128)(2,1)S(1)}, u32[]{:S(2)}, u32[]{:S(2)}) collective-permute-start(bf16[256,512]{1,0:T(8,128)(2,1)} %get-tuple-element.20), channel_id=1, source_target_pairs={{0,16},{16,0},{1,17},{17,1},{2,18},{18,2},{3,19},{19,3},{4,20},{20... | collective-permute-start | bytes 786440 | tf_op jit(solution)/shard_map/ppermute | solution.py:31
  109.3 48.0 %collective-permute-start.15 = (bf16[256,512]{1,0:T(8,128)(2,1)}, bf16[256,512]{1,0:T(8,128)(2,1)}, u32[]{:S(2)}, u32[]{:S(2)}) collective-permute-start(bf16[256,512]{1,0:T(8,128)(2,1)} %get-tuple-element.21), channel_id=1, source_target_pairs={{0,16},{16,0},{1,17},{17,1},{2,18},{18,2},{3,19},{19,3},{4,20},{20... | collective-permute-start | bytes 786440 | tf_op jit(solution)/shard_map/ppermute | solution.py:31
  109.4 8.2 %collective-permute-start.23 = (bf16[104,8,128]{2,1,0:T(8,128)(2,1)S(1)}, bf16[104,8,128]{2,1,0:T(8,128)(2,1)S(1)}, u32[]{:S(2)}, u32[]{:S(2)}) collective-permute-start(bf16[104,8,128]{2,1,0:T(8,128)(2,1)S(1)} %constant_dynamic-slice_fusion.7), channel_id=1, source_target_pairs={{0,2},{2,0},{4,6},{6,4},{8,10},{10,8},{12,14},{14,12},{1,3},{3,1},... | collective-permute-start | bytes 638984 | tf_op jit(solution)/shard_map/ppermute | solution.py:36
  133.2 7.9 %collective-permute-start.36 = (bf16[24,8,128]{2,1,0:T(8,128)(2,1)S(1)}, bf16[24,8,128]{2,1,0:T(8,128)(2,1)S(1)}, u32[]{:S(2)}, u32[]{:S(2)}) collective-permute-start(bf16[24,8,128]{2,1,0:T(8,128)(2,1)S(1)} %pad_maximum_fusion.12), channel_id=1, source_target_pairs={{0,4},{2,6},{4,0},{6,2},{8,12},{10,14},{12,8},{14,10},{1,5},{3,7},... | collective-permute-start | bytes 147464 | tf_op jit(solution)/shard_map/ppermute | solution.py:36
  146.6 9.4 %collective-permute-start.38 = (bf16[96,8,128]{2,1,0:T(8,128)(2,1)S(1)}, bf16[96,8,128]{2,1,0:T(8,128)(2,1)S(1)}, u32[]{:S(2)}, u32[]{:S(2)}) collective-permute-start(bf16[96,8,128]{2,1,0:T(8,128)(2,1)S(1)} %pad_maximum_fusion.8), channel_id=1, source_target_pairs={{0,1},{1,0},{2,3},{3,2},{4,5},{5,4},{6,7},{7,6},{8,9},{9,8},{10,11... | collective-permute-start | bytes 589832 | tf_op jit(solution)/shard_map/ppermute | solution.py:36
  (42 other events, 312.6 us)

commit v2 on v1

--- a/solution.py
+++ b/solution.py
@@ -10,7 +10,7 @@
 HD = 128
 WINDOW = 1024
 SUB = 8
-SPLITS = 4
+PIECES = (2, 3, 3)
 
 query_scale = 168.0 ** (-0.5)
 adapter_scale = 0.5
@@ -37,21 +37,15 @@
 
 
 def window_blocks(own, steps):
-    count = lax.axis_size("ctx")
-    even_to_odd = [(i, i + 1) for i in range(0, count - 1, 2)]
-    odd_to_even = [(i + 1, i) for i in range(0, count - 1, 2)]
+    even = lax.axis_index("ctx") % 2 == 0
     chain = [own]
     for _ in range(steps):
         chain.append(permute_by(chain[-1], "ctx", 2))
     blocks = []
     for i in range(steps):
-        blocks.append(
-            [
-                lax.ppermute(chain[i], "ctx", even_to_odd),
-                lax.ppermute(chain[i + 1], "ctx", odd_to_even),
-            ]
-        )
-        blocks.append([chain[i + 1]])
+        payload = jnp.where(even, chain[i], chain[i + 1])
+        blocks.append(permute_xor(payload, "ctx", 1))
+        blocks.append(chain[i + 1])
     return blocks
 
 
@@ -60,66 +54,85 @@
     return jnp.sum((doc_ends[None, :] <= positions[:, None]).astype(jnp.int32), axis=1)
 
 
-def attention_kernel(*refs, counts, tok, group):
-    n_in = sum(counts)
-    k_refs, v_refs = refs[:n_in], refs[n_in : 2 * n_in]
-    q_ref, g_ref, spread_ref, up_ref, bias_ref, cos_ref, sin_ref = refs[2 * n_in : 2 * n_in + 7]
-    out_ref, lg_ref, u_ref = refs[2 * n_in + 7 :]
+def attention_kernel(*refs, n_blocks, tok, group, sub, chained):
+    k_refs, v_refs = refs[:n_blocks], refs[n_blocks : 2 * n_blocks]
+    at = 2 * n_blocks
+    q_ref, g_ref, spread_ref, up_ref, bias_ref, cos_ref, sin_ref = refs[at : at + 7]
+    at += 7
+    if chained:
+        lg_in_ref = refs[at]
+        at += 3
+    out_ref, u_ref, lg_ref = refs[at : at + 3]
+    lg_low_refs = refs[at + 3 :]
+    step = pl.program_id(0)
     up = up_ref[0]
     spread = spread_ref[...]
     shift = adapter_scale * jnp.dot(spread, up, preferred_element_type=f32)
-
-    def stacked(block_refs):
-        rows, at = [], 0
-        for n in counts:
-            block = block_refs[at][...].astype(f32)
-            for extra in block_refs[at + 1 : at + n]:
-                block = block + extra[...].astype(f32)
-            rows.append(block)
-            at += n
-        return jnp.concatenate(rows, axis=0)
-
     cos, sin = cos_ref[...], sin_ref[...]
-    key = stacked(k_refs) + shift[:, :HD]
+    key = jnp.concatenate([r[...] for r in k_refs], axis=0).astype(f32) + shift[:, :HD]
     key = (key * cos + pltpu.roll(key, HD // 2, 1) * sin).astype(bf16)
-    val = (stacked(v_refs) + shift[:, HD:]).astype(bf16)
-    cos_q, sin_q = cos[:tok], sin[:tok]
+    val = jnp.concatenate([r[...] for r in v_refs], axis=0).astype(f32) + shift[:, HD:]
+    val = val.astype(bf16)
+    span = key.shape[0]
+    cos_q, sin_q = cos[span - tok :], sin[span - tok :]
     queries, grads = [], []
     for h in range(group):
         q = q_ref[:, h * HD : (h + 1) * HD].astype(f32)
         queries.append((q * cos_q + pltpu.roll(q, HD // 2, 1) * sin_q).astype(bf16))
         grads.append(g_ref[:, h * HD : (h + 1) * HD])
-    q = jnp.concatenate(queries, axis=0)
-    g = jnp.concatenate(grads, axis=0)
     dot = partial(lax.dot_general, preferred_element_type=f32)
     last, first = (((1,), (1,)), ((), ())), (((0,), (0,)), ((), ()))
-    bias = jnp.concatenate([bias_ref[...]] * group, axis=1)
-    scores = dot(key, q, last) * query_scale + bias
-    top = jnp.max(scores, axis=0, keepdims=True)
-    probs = jnp.exp(scores - top)
-    total = jnp.sum(probs, axis=0, keepdims=True)
-    probs = probs * (1.0 / total)
-    low_probs = probs.astype(bf16)
-    out_t = dot(val, low_probs, first)
-    out = out_t.T.astype(bf16)
-    for h in range(group):
-        out_ref[:, h * HD : (h + 1) * HD] = out[h * tok : (h + 1) * tok]
-    drift = jnp.sum(out_t.astype(bf16).astype(f32) * g.astype(f32).T, axis=0, keepdims=True)
-    dprob = dot(val, g, last)
-    dscore = (probs * (dprob - drift)).astype(bf16)
-    dkey = query_scale * jnp.dot(dscore, q, preferred_element_type=f32)
-    dval = jnp.dot(low_probs, g, preferred_element_type=f32)
+    length = span - tok + sub
+    dkeys, dvals = [], []
+    for i in range(tok // sub):
+        cut = slice(i * sub, (i + 1) * sub)
+        rows = slice(i * sub, i * sub + length)
+        q = jnp.concatenate([x[cut] for x in queries], axis=0)
+        g = jnp.concatenate([x[cut] for x in grads], axis=0)
+        bias = jnp.concatenate([bias_ref[rows, cut]] * group, axis=1)
+        scores = dot(key[rows], q, last) * query_scale + bias
+        top = jnp.max(scores, axis=0, keepdims=True)
+        probs = jnp.exp(scores - top)
+        total = jnp.sum(probs, axis=0, keepdims=True)
+        probs = probs * (1.0 / total)
+        low_probs = probs.astype(bf16)
+        out_t = dot(val[rows], low_probs, first).astype(bf16)
+        out = out_t.T
+        for h in range(group):
+            out_ref[cut, h * HD : (h + 1) * HD] = out[h * sub : (h + 1) * sub]
+        drift = jnp.sum(out_t.astype(f32) * g.T.astype(f32), axis=0, keepdims=True)
+        dprob = dot(val[rows], g, last)
+        dscore = (probs * (dprob - drift)).astype(bf16)
+        dkeys.append(jnp.dot(dscore, q, preferred_element_type=f32))
+        dvals.append(jnp.dot(low_probs, g, preferred_element_type=f32))
+
+    def overlapped(parts):
+        rows = []
+        for j in range(span // sub):
+            here = [p[(j - i) * sub : (j - i + 1) * sub] for i, p in enumerate(parts) if 0 <= j - i < length // sub]
+            rows.append(sum(here[1:], here[0]))
+        return jnp.concatenate(rows, axis=0)
+
+    dkey = query_scale * overlapped(dkeys)
+    dval = overlapped(dvals)
     dkey = dkey * cos - pltpu.roll(dkey, HD // 2, 1) * sin
     both = jnp.concatenate([dkey.astype(bf16), dval.astype(bf16)], axis=1)
     lg = dot(both, up, last)
 
-    @pl.when(pl.program_id(0) == 0)
+    @pl.when(step == 0)
     def _():
-        lg_ref[...] = lg
-
-    @pl.when(pl.program_id(0) != 0)
+        lg_ref[...] = lg_in_ref[...] + lg if chained else lg
+
+    @pl.when(step != 0)
     def _():
         lg_ref[...] += lg
+
+    if lg_low_refs:
+
+        @pl.when(step == pl.num_programs(0) - 1)
+        def _():
+            for j, ref in enumerate(lg_low_refs):
+                ref[...] = lg_ref[j * tok : (j + 1) * tok].astype(bf16)
 
     u = adapter_scale * dot(spread, both, first)
     half = spread.shape[1] // 2
@@ -127,20 +140,23 @@
     u_ref[1] = u[half:, HD:].astype(bf16)
 
 
-def attention(blocks, start, q_rows, g_rows, spread, up_cat, bias, cos, sin):
+def attention(blocks, start, carried, is_last, q_rows, g_rows, spread, up_cat, bias, cos, sin):
     tok = q_rows.shape[0]
-    heads = blocks[0][0].shape[1] // (2 * HD)
+    heads = blocks[0].shape[1] // (2 * HD)
     kv_heads, width, _ = up_cat.shape
     group = q_rows.shape[1] // (kv_heads * HD)
-    counts = tuple(len(b) for b in blocks)
-    flat = [a for b in blocks for a in b]
+    n_blocks = len(blocks)
     span = spread.shape[0]
     half = width // 2
+    sub = HD if tok % HD == 0 else tok
     whole = lambda shape: pl.BlockSpec(shape, lambda h: (0,) * len(shape))
+    any_space = pl.BlockSpec(memory_space=pl.ANY)
+    out_spec = pl.BlockSpec((tok, group * HD), lambda h: (0, h + start))
+    u_spec = pl.BlockSpec((2, half, HD), lambda h: (0, 0, h + start))
     in_specs = (
-        [pl.BlockSpec((tok, HD), lambda h: (0, h))] * len(flat)
-        + [pl.BlockSpec((tok, HD), lambda h: (0, h + heads))] * len(flat)
-        + [pl.BlockSpec((tok, group * HD), lambda h: (0, h + start))] * 2
+        [pl.BlockSpec((tok, HD), lambda h: (0, h))] * n_blocks
+        + [pl.BlockSpec((tok, HD), lambda h: (0, h + heads))] * n_blocks
+        + [out_spec] * 2
         + [
             whole((span, width)),
             pl.BlockSpec((1, width, 2 * HD), lambda h: (h + start, 0, 0)),
@@ -149,31 +165,44 @@
             whole((span, HD)),
         ]
     )
+    extra, aliases = [], {}
+    if carried is not None:
+        out, u, lg = carried
+        at = len(in_specs)
+        extra, aliases = [lg, out, u], {at + 1: 0, at + 2: 1}
+        in_specs = in_specs + [whole((span, width)), any_space, any_space]
+    low_count = n_blocks - 1 if is_last else 0
+    work = heads * group * tok * (span - tok + sub) * HD * 2 * 6
     return pl.pallas_call(
-        partial(attention_kernel, counts=counts, tok=tok, group=group),
+        partial(
+            attention_kernel,
+            n_blocks=n_blocks,
+            tok=tok,
+            group=group,
+            sub=sub,
+            chained=carried is not None,
+        ),
         grid=(heads,),
         in_specs=in_specs,
-        out_specs=[
-            pl.BlockSpec((tok, group * HD), lambda h: (0, h)),
-            whole((span, width)),
-            pl.BlockSpec((2, half, HD), lambda h: (0, 0, h)),
-        ],
+        out_specs=[out_spec, u_spec, whole((span, width))] + [whole((tok, width))] * low_count,
         out_shape=[
-            jax.ShapeDtypeStruct((tok, heads * group * HD), bf16),
+            jax.ShapeDtypeStruct(q_rows.shape, bf16),
+            jax.ShapeDtypeStruct((2, half, kv_heads * HD), bf16),
             jax.ShapeDtypeStruct((span, width), f32),
-            jax.ShapeDtypeStruct((2, half, heads * HD), bf16),
-        ],
+        ]
+        + [jax.ShapeDtypeStruct((tok, width), bf16)] * low_count,
+        input_output_aliases=aliases,
         compiler_params=pltpu.CompilerParams(dimension_semantics=("arbitrary",)),
+        cost_estimate=pl.CostEstimate(flops=work, transcendentals=0, bytes_accessed=heads * tok * HD * 20),
         name="attention",
-    )(*flat, *flat, q_rows, g_rows, spread, up_cat, bias, cos, sin)
-
-
-def product_kernel(*refs, n_recv, n_up, cols, up_cols):
+    )(*blocks, *blocks, q_rows, g_rows, spread, up_cat, bias, cos, sin, *extra)
+
+
+def product_kernel(*refs, n_recv, cols, up_cols):
     side_ref, lg_ref = refs[:2]
     recv = refs[2 : 2 + n_recv]
     mask_ref, hidden_ref = refs[2 + n_recv : 4 + n_recv]
-    ups = refs[4 + n_recv : 4 + n_recv + n_up]
-    keep_ref, send_ref = refs[4 + n_recv + n_up :]
+    up_ref, keep_ref, send_ref = refs[4 + n_recv :]
     side = side_ref[0]
     total = lg_ref[...]
     for r in recv:
@@ -197,14 +226,11 @@
                 tile = w[:, j * HD : (j + 1) * HD]
                 keep_ref[r * per_row + c + j] = tile[r * SUB : (r + 1) * SUB]
                 send_ref[r * per_row + c + j] = tile[half + r * SUB : half + (r + 1) * SUB]
-    at = cols
-    for up in ups:
-        for h in range(up.shape[2] // HD):
-            for r in range(rows):
-                where = (slice(r * SUB, (r + 1) * SUB), slice(h * HD, (h + 1) * HD))
-                keep_ref[r * per_row + at] = up[(side,) + where]
-                send_ref[r * per_row + at] = up[(1 - side,) + where]
-            at += 1
+    for h in range(up_cols):
+        for r in range(rows):
+            where = (slice(r * SUB, (r + 1) * SUB), slice(h * HD, (h + 1) * HD))
+            keep_ref[r * per_row + cols + h] = up_ref[(side,) + where]
+            send_ref[r * per_row + cols + h] = up_ref[(1 - side,) + where]
     used = rows * per_row
     if keep_ref.shape[0] > used:
         rest = keep_ref.shape[0] - used
@@ -248,6 +274,30 @@
     return ((lax.axis_index(axis) & bit) != 0).astype(jnp.int32)
 
 
+def direct_peers(axis, bits):
+    masks = [0]
+    for bit in bits:
+        masks = masks + [m | bit for m in masks]
+    me = jnp.int32(0)
+    for bit in reversed(bits):
+        me = me * 2 + bit_of((axis, bit))
+    return masks, me
+
+
+def direct_scatter(tiles, axis, bits):
+    masks, me = direct_peers(axis, bits)
+    total = lax.dynamic_index_in_dim(tiles, me, 0, keepdims=False).astype(f32)
+    for j in range(1, len(masks)):
+        part = lax.dynamic_index_in_dim(tiles, me ^ j, 0, keepdims=False)
+        total = total + permute_xor(part, axis, masks[j]).astype(f32)
+    return total.astype(bf16)
+
+
+def direct_gather(tiles, axis, bits):
+    masks, _ = direct_peers(axis, bits)
+    return jnp.stack([tiles] + [permute_xor(tiles, axis, m) for m in masks[1:]])
+
+
 def scatter_stage(tiles, stage):
     n = tiles.shape[0] // 2
     bit = bit_of(stage)
@@ -283,20 +333,20 @@
     reach = min(-(-(min(WINDOW, longest) - 1) // tok), ctx_size - 1)
     steps = (reach + 1) // 2
 
-    splits = SPLITS if kv_heads % SPLITS == 0 else 1
-    per = kv_heads // splits
+    pieces = PIECES if sum(PIECES) == kv_heads else (kv_heads,)
+    starts = [sum(pieces[:i]) for i in range(len(pieces))]
     keys, vals = frozen_key_rows[0], frozen_value_rows[0]
     parts = []
-    for i in range(splits):
-        cut = slice(i * per * HD, (i + 1) * per * HD)
+    for first, count in zip(starts, pieces):
+        cut = slice(first * HD, (first + count) * HD)
         own = jnp.concatenate([keys[:, cut], vals[:, cut]], axis=1)
-        parts.append([[own]] + window_blocks(own, steps))
+        parts.append(window_blocks(own, steps)[::-1] + [own])
     returned = permute_cyclic(next_output_gradient, "section", -1)
 
-    block_starts = jnp.stack([(ctx_index - d) * tok for d in range(2 * steps + 1)])
+    block_starts = jnp.stack([(ctx_index - d) * tok for d in range(2 * steps, -1, -1)])
     key_pos = (block_starts[:, None] + jnp.arange(tok, dtype=jnp.int32)[None, :]).reshape(-1)
     key_docs = doc_index(document_lengths[0], key_pos)
-    positions, docs = key_pos[:tok], key_docs[:tok]
+    positions, docs = key_pos[-tok:], key_docs[-tok:]
     picked = docs[:, None] == jnp.arange(document_lengths.shape[1], dtype=jnp.int32)[None, :]
     tenant = jnp.sum(picked.astype(jnp.int32) * document_adapter[0][None, :], axis=1)
     lane_adapter = (jnp.arange(width, dtype=jnp.int32) // rank) % adapters
@@ -319,11 +369,7 @@
         hidden[0], adapter_down_maps.reshape(model_width, width), preferred_element_type=f32
     )
     spread_own = (low * mask).astype(bf16)
-    spread = jnp.concatenate(
-        [spread_own]
-        + [sum(b[1:], b[0]) for b in window_blocks(spread_own, steps)],
-        axis=0,
-    )
+    spread = jnp.concatenate(window_blocks(spread_own, steps)[::-1] + [spread_own], axis=0)
     up_flat = adapter_up_maps.reshape(2, half, kv_heads, HD)
     zero = jnp.zeros((kv_heads, half, HD), bf16)
     up_heads = jnp.moveaxis(up_flat, 2, 1)
@@ -335,11 +381,13 @@
         axis=1,
     )
 
-    outs, lgs, ups = [], [], []
-    for i in range(splits):
-        out, lg, u = attention(
+    carried = None
+    for i in range(len(pieces)):
+        result = attention(
             parts[i],
-            i * per,
+            starts[i],
+            carried,
+            i == len(pieces) - 1,
             frozen_query_rows[0],
             returned[0],
             spread,
@@ -348,19 +396,16 @@
             cos,
             sin,
         )
-        outs.append(permute_cyclic(out, "section", 1))
-        lgs.append(lg)
-        ups.append(u)
-    handed = jnp.concatenate(outs, axis=1)[None]
-
-    lg = sum(lgs[1:], lgs[0]).reshape(2 * steps + 1, tok, width)
-    received = [permute_by(lg[d].astype(bf16), "ctx", -d) for d in range(1, 2 * steps + 1)]
+        carried = result[:3]
+    out, ups, lg = carried
+    received = [permute_by(low, "ctx", j - 2 * steps) for j, low in enumerate(result[3:])]
+    handed = permute_cyclic(out, "section", 1)[None]
 
     other = (
         axis_bits("ctx")[:1] + axis_bits("dp"),
         axis_bits("dp") + axis_bits("ctx")[:1],
     )
-    tail = axis_bits("ctx")[1:]
+    tail = [bit for _, bit in axis_bits("ctx")[1:]]
     group = lax.axis_size("ctx") * lax.axis_size("dp")
     cols, up_cols, rows = model_width // HD, kv_heads, half // SUB
     units = -(-(rows * (cols + up_cols)) // group)
@@ -371,27 +416,43 @@
     vmem = pl.BlockSpec(memory_space=pltpu.VMEM)
     keep, send = pl.pallas_call(
         partial(
-            product_kernel, n_recv=len(received), n_up=len(ups), cols=cols, up_cols=up_cols
+            product_kernel, n_recv=len(received), cols=cols, up_cols=up_cols
         ),
-        in_specs=[smem] + [vmem] * (3 + len(received) + len(ups)),
+        in_specs=[smem] + [pl.BlockSpec((tok, width), lambda i: (2 * steps, 0))] + [vmem] * (3 + len(received)),
+        grid=(1,),
         out_specs=[vmem, vmem],
         out_shape=[jax.ShapeDtypeStruct((units * group, SUB, HD), bf16)] * 2,
         name="product",
-    )(side[None], lg[0], *received, adapter_scale * mask, hidden[0], *ups)
+    )(side[None], lg, *received, adapter_scale * mask, hidden[0], ups)
     recv = permute_cyclic(send, "section", 1)
     tiles = (keep.astype(f32) + recv.astype(f32)).astype(bf16)
     colours = [tiles[: a * group], tiles[a * group :]]
+    for k in range(len(other[0])):
+        colours = [scatter_stage(colours[c], other[c][k]) for c in range(2)]
+    rounds = [tail[k : k + 2] for k in range(0, len(tail), 2)]
+    members = group >> len(other[0])
+    joined = jnp.concatenate([c.reshape(members, -1, SUB, HD) for c in colours], axis=1)
+    for bits in rounds:
+        joined = joined.reshape(2 ** len(bits), -1, a + b, SUB, HD)
+        joined = direct_scatter(joined, "ctx", bits)
+    joined = joined.reshape(a + b, SUB, HD)
     ids = []
-    stages = [list(other[c]) + list(tail) for c in range(2)]
-    for k in range(len(stages[0])):
-        colours = [scatter_stage(colours[c], stages[c][k]) for c in range(2)]
     for c in range(2):
         me = jnp.int32(0)
-        for stage in stages[c]:
+        for stage in other[c]:
             me = me * 2 + bit_of(stage)
+        for bits in rounds:
+            me = me * 2 ** len(bits) + direct_peers("ctx", bits)[1]
         ids.append(me)
-    for k in reversed(range(len(stages[0]))):
-        colours = [gather_stage(colours[c], stages[c][k]) for c in range(2)]
+    joined = joined[None]
+    for bits in reversed(rounds):
+        joined = direct_gather(joined, "ctx", bits).reshape(-1, a + b, SUB, HD)
+    colours = [
+        joined[:, :a].reshape(-1, SUB, HD),
+        joined[:, a:].reshape(-1, SUB, HD),
+    ]
+    for k in reversed(range(len(other[0]))):
+        colours = [gather_stage(colours[c], other[c][k]) for c in range(2)]
     theirs = [permute_cyclic(t, "section", 1) for t in colours]
     shapes = [(group, a, SUB, HD), (group, b, SUB, HD)]
     w, u = pl.pallas_call(

time: 165 us -> 145 us (0.88)
  waiting for transfers between devices: 48.2 us -> 32.2 us
  starting transfers between devices: 57.5 us -> 47.6 us
  local copies, waits for them, and re-layouts: 5.63 us -> 9.23 us
    ppermute x10 -> x0, starting transfers between devices: 20.2 us -> none  [the longest x5 13.5 us: window_blocks(): lax.ppermute(chain[i], 'ctx', even_to_odd)]
    ppermute x16 -> x18, starting transfers between devices: 16.9 us -> 29.7 us  [permute_xor(): return lax.ppermute(value, axis, [(i, i ^ bit) for i in range(count)])]
    ppermute x16 -> x18, waiting for transfers between devices: 30.6 us -> 22.3 us  [permute_xor(): return lax.ppermute(value, axis, [(i, i ^ bit) for i in range(count)])]
    ppermute x10 -> x0, waiting for transfers between devices: 6.77 us -> none  [the longest x5 4.81 us: window_blocks(): lax.ppermute(chain[i + 1], 'ctx', odd_to_even)]
    unnamed x57 -> x52, local copies, waits for them, and re-layouts: 2.41 us -> 5.48 us
    select_n x0 -> x4, other arithmetic: none -> 3 us  [window_blocks(): payload = jnp.where(even, chain[i], chain[i + 1])]
    broadcast_in_dim x1 -> x0, other arithmetic: 2.13 us -> none  [body(): handed = jnp.concatenate(outs, axis=1)[None]]
    ppermute x7 -> x6, waiting for transfers between devices: 7.82 us -> 6.12 us  [permute_by(): lax.ppermute(value, axis, [(i, i + steps) for i in range(first, last)])]
  transfers between devices with their start and end apart: 41 -> 29, of which waited for: 18 -> 16; matrix products, arithmetic and copies ran while one was open for 8% -> 12% of each run, Pallas kernels for 13% -> 13%
where the time goes in v2:
time: 145 us; the launch traced here: 144 us
  starting transfers between devices  47.6 us (33%)
  Pallas kernels  37.3 us (26%)
  waiting for transfers between devices  32.2 us (22%)
  other arithmetic  13.7 us (9%)
  local copies, waits for them, and re-layouts  9.23 us (6%)
  matrix products  2.73 us (2%)
    pallas_call x3, Pallas kernels, attention(): pl.pallas_call(partial(attention_kernel, n_blocks=n_blocks, tok=tok, grou...  30.1 us
    ppermute x18, starting transfers between devices, permute_xor(): return lax.ppermute(value, axis, [(i, i ^ bit) for i in range(count)])  29.7 us
    ppermute x18, waiting for transfers between devices, permute_xor(): return lax.ppermute(value, axis, [(i, i ^ bit) for i in range(count)])  22.3 us
    ppermute x6, starting transfers between devices, permute_by(): lax.ppermute(value, axis, [(i, i + steps) for i in range(first, last)])  17.8 us
    ppermute x6, waiting for transfers between devices, permute_by(): lax.ppermute(value, axis, [(i, i + steps) for i in range(first, last)])  6.12 us
    unnamed x52, local copies, waits for them, and re-layouts  5.48 us
    ppermute x5, waiting for transfers between devices, permute_cyclic(): lax.ppermute(value, axis, [(i, (i + by) % count) for i in range(count)])  3.81 us
    pallas_call x1, Pallas kernels, body(): pl.pallas_call(partial(product_kernel, n_recv=len(received), cols=cols, u...  3.81 us
  transfers between devices with their start and end apart: 29, of which 16 were waited for; matrix products, arithmetic and copies ran while one was open for 12% of the time, Pallas kernels for 13%

profile of v2, /device:TPU:0, one launch (start us, length us, event | category | flops | bytes accessed | tf_op | source)
XLA Modules:
  0.0 143.9 jit_solution(10471114035629784084)
XLA Ops:
  3.3 5.7 %collective-permute-start.7 = (bf16[256,512]{1,0:T(8,128)(2,1)S(1)}, bf16[256,512]{1,0:T(8,128)(2,1)}, u32[]{:S(2)}, u32[]{:S(2)}) collective-permute-start(bf16[256,512]{1,0:T(8,128)(2,1)S(1)} %pad_maximum_fusion.6.refs_2_.refs_5_), channel_id=1, source_target_pairs={{0,4},{2,6},{4,8},{6,10},{8,12},{10,14},{1,5},{3,7},{5,9},{7,11},{... | collective-permute-start | bytes 786440 | tf_op jit(solution)/shard_map/ppermute | solution.py:26
  10.9 2.7 %fusion = bf16[256,128]{1,0:T(8,128)(2,1)S(1)} fusion(bf16[5376,128]{0,1:T(8,128)(2,1)S(1)} %bitcast.49, s32[128]{0:T(128)S(1)} %and_select_fusion, s32[256]{0:T(256)S(1)} %select_reduce_fusion, bf16[1,256,5376]{2,1,0:T(8,128)(2,1)} %param.9), kind=kOutput, calls=%fused_computation.4 | convolution fusion | flops 352419840 | bytes 4195840 | tf_op jit(solution)/shard_map/dot_general | solution.py:368
  13.7 3.6 %collective-permute-start.3 = (bf16[256,128]{1,0:T(8,128)(2,1)S(1)}, bf16[256,128]{1,0:T(8,128)(2,1)}, u32[]{:S(2)}, u32[]{:S(2)}) collective-permute-start(bf16[256,128]{1,0:T(8,128)(2,1)S(1)} %fusion), channel_id=1, source_target_pairs={{0,4},{2,6},{4,8},{6,10},{8,12},{10,14},{1,5},{3,7},{5,9},{7,11},{... | collective-permute-start | bytes 196616 | tf_op jit(solution)/shard_map/ppermute | solution.py:26
  17.4 3.7 %collective-permute-start.5 = (bf16[256,768]{1,0:T(8,128)(2,1)S(1)}, bf16[256,768]{1,0:T(8,128)(2,1)}, u32[]{:S(2)}, u32[]{:S(2)}) collective-permute-start(bf16[256,768]{1,0:T(8,128)(2,1)S(1)} %pad_maximum_fusion.4.refs_2_.refs_5_), channel_id=1, source_target_pairs={{0,4},{2,6},{4,8},{6,10},{8,12},{10,14},{1,5},{3,7},{5,9},{7,11},{... | collective-permute-start | bytes 1179656 | tf_op jit(solution)/shard_map/ppermute | solution.py:26
  28.3 2.4 %collective-permute-start.4 = (bf16[256,128]{1,0:T(8,128)(2,1)S(1)}, bf16[256,128]{1,0:T(8,128)(2,1)S(1)}, u32[]{:S(2)}, u32[]{:S(2)}) collective-permute-start(bf16[256,128]{1,0:T(8,128)(2,1)S(1)} %broadcast_select_fusion.3), channel_id=1, source_target_pairs={{0,2},{2,0},{4,6},{6,4},{8,10},{10,8},{12,14},{14,12},{1,3},{3,1},... | collective-permute-start | bytes 196616 | tf_op jit(solution)/shard_map/ppermute | solution.py:36
  37.9 2.5 %collective-permute-start.1 = (bf16[256,768]{1,0:T(8,128)(2,1)S(1)}, bf16[256,768]{1,0:T(8,128)(2,1)S(1)}, u32[]{:S(2)}, u32[]{:S(2)}) collective-permute-start(bf16[256,768]{1,0:T(8,128)(2,1)S(1)} %broadcast_select_fusion.1), channel_id=1, source_target_pairs={{0,2},{2,0},{4,6},{6,4},{8,10},{10,8},{12,14},{14,12},{1,3},{3,1},... | collective-permute-start | bytes 1179656 | tf_op jit(solution)/shard_map/ppermute | solution.py:36
  43.9 8.0 %attention.3 = (bf16[256,2048]{1,0:T(8,128)(2,1)}, bf16[2,64,1024]{2,1,0:T(8,128)(2,1)}, f32[768,128]{1,0:T(8,128)}) custom-call(bf16[256,512]{1,0:T(8,128)(2,1)} %collective-permute-done.7.refs_0_.refs_3_, bf16[256,512]{1,0:T(8,128)(2,1)} %copy-done.17, bf16[256,512]{1,0:T(8,128)(2,1)} %copy-done.5, ...), custom_call_target="tpu_custom_call" | custom-call | flops 1006632960 | bytes 1310720 | tf_op jit(solution)/shard_map/attention/pallas_call | solution.py:176
  51.9 11.1 %attention.4 = (bf16[256,2048]{1,0:T(8,128)(2,1)}, bf16[2,64,1024]{2,1,0:T(8,128)(2,1)}, f32[768,128]{1,0:T(8,128)}) custom-call(bf16[256,768]{1,0:T(8,128)(2,1)} %collective-permute-done.5.refs_0_.refs_3_, bf16[256,768]{1,0:T(8,128)(2,1)} %collective-permute-done.6.refs_1_.refs_4_, ...), custom_call_target="tpu_custom_call", output_to_operand_aliasing={{0}: (14, {}), {1}: (15, {})} | custom-call | flops 1509949440 | bytes 1966080 | tf_op jit(solution)/shard_map/attention/pallas_call | solution.py:176
  63.7 11.0 %attention.5 = (bf16[256,2048]{1,0:T(8,128)(2,1)}, bf16[2,64,1024]{2,1,0:T(8,128)(2,1)}, f32[768,128]{1,0:T(8,128)}, bf16[256,128]{1,0:T(8,128)(2,1)}, bf16[256,128]{1,0:T(8,128)(2,1)}) custom-call(bf16[256,768]{1,0:T(8,128)(2,1)} %collective-permute-done.refs_0_.refs_3_, ...), custom_call_target="tpu_custom_call", output_to_operand_aliasing={{0}: (14, {}), {1}: (15, {})} | custom-call | flops 1509949440 | bytes 1966080 | tf_op jit(solution)/shard_map/attention/pallas_call | solution.py:176
  78.3 3.5 %collective-permute-done.10.refs_2_ = bf16[256,128]{1,0:T(8,128)(2,1)S(1)} collective-permute-done((bf16[256,128]{1,0:T(8,128)(2,1)}, bf16[256,128]{1,0:T(8,128)(2,1)S(1)}, u32[]{:S(2)}, u32[]{:S(2)}) %collective-permute-start.10) | collective-permute-done | bytes 65568 | tf_op jit(solution)/shard_map/ppermute | solution.py:26
  83.1 3.8 %product.1 = (bf16[400,8,128]{2,1,0:T(8,128)(2,1)}, bf16[400,8,128]{2,1,0:T(8,128)(2,1)}) custom-call(s32[1]{0:T(128)} %bitcast.16.refs_0_, f32[768,128]{1,0:T(8,128)} %get-tuple-element.25.refs_1_, bf16[256,128]{1,0:T(8,128)(2,1)} %copy-done.23, bf16[256,128]{1,0:T(8,128)(2,1)} %copy-done.24, f32[256,128]{1,0:T(8,128)} %compare_select_fusion.refs_4_, ...), custom_call_target="tpu_custom_call" | custom-call | tf_op jit(solution)/shard_map/product/pallas_call | solution.py:417
  86.9 2.5 %collective-permute-done.12 = bf16[400,8,128]{2,1,0:T(8,128)(2,1)S(1)} collective-permute-done((bf16[400,8,128]{2,1,0:T(8,128)(2,1)}, bf16[400,8,128]{2,1,0:T(8,128)(2,1)S(1)}, u32[]{:S(2)}, u32[]{:S(2)}) %collective-permute-start.12) | collective-permute-done | bytes 819232 | tf_op jit(solution)/shard_map/ppermute | solution.py:31
  92.5 2.7 %collective-permute-start.13 = (bf16[104,8,128]{2,1,0:T(8,128)(2,1)S(1)}, bf16[104,8,128]{2,1,0:T(8,128)(2,1)S(1)}, u32[]{:S(2)}, u32[]{:S(2)}) collective-permute-start(bf16[104,8,128]{2,1,0:T(8,128)(2,1)S(1)} %constant_dynamic-slice_fusion.3), channel_id=1, source_target_pairs={{0,2},{2,0},{4,6},{6,4},{8,10},{10,8},{12,14},{14,12},{1,3},{3,1},... | collective-permute-start | bytes 638984 | tf_op jit(solution)/shard_map/ppermute | solution.py:36
  95.2 2.6 %collective-permute-done.15 = bf16[96,8,128]{2,1,0:T(8,128)(2,1)S(1)} collective-permute-done((bf16[96,8,128]{2,1,0:T(8,128)(2,1)S(1)}, bf16[96,8,128]{2,1,0:T(8,128)(2,1)S(1)}, u32[]{:S(2)}, u32[]{:S(2)}) %collective-permute-start.15) | collective-permute-done | bytes 196640 | tf_op jit(solution)/shard_map/ppermute | solution.py:36
  97.9 2.7 %collective-permute-start.16 = (bf16[48,8,128]{2,1,0:T(8,128)(2,1)S(1)}, bf16[48,8,128]{2,1,0:T(8,128)(2,1)S(1)}, u32[]{:S(2)}, u32[]{:S(2)}) collective-permute-start(bf16[48,8,128]{2,1,0:T(8,128)(2,1)S(1)} %constant_dynamic-slice_fusion), channel_id=1, source_target_pairs={{0,2},{2,0},{4,6},{6,4},{8,10},{10,8},{12,14},{14,12},{1,3},{3,1},... | collective-permute-start | bytes 294920 | tf_op jit(solution)/shard_map/ppermute | solution.py:36
  103.3 2.2 %collective-permute-done.14 = bf16[52,8,128]{2,1,0:T(8,128)(2,1)S(1)} collective-permute-done((bf16[52,8,128]{2,1,0:T(8,128)(2,1)S(1)}, bf16[52,8,128]{2,1,0:T(8,128)(2,1)S(1)}, u32[]{:S(2)}, u32[]{:S(2)}) %collective-permute-start.14) | collective-permute-done | bytes 106528 | tf_op jit(solution)/shard_map/ppermute | solution.py:36
  105.6 2.2 %collective-permute-start.17 = (bf16[1,25,8,128]{3,2,1,0:T(8,128)(2,1)S(1)}, bf16[1,25,8,128]{3,2,1,0:T(8,128)(2,1)S(1)}, u32[]{:S(2)}, u32[]{:S(2)}) collective-permute-start(bf16[1,25,8,128]{3,2,1,0:T(8,128)(2,1)S(1)} %get-tuple-element.39), channel_id=1, source_target_pairs={{0,4},{2,6},{4,0},{6,2},{8,12},{10,14},{12,8},{14,10},{1,5},{3,7},... | collective-permute-start | bytes 153608 | tf_op jit(solution)/shard_map/ppermute | solution.py:36
  112.8 2.7 %collective-permute-done.19 = bf16[1,25,8,128]{3,2,1,0:T(8,128)(2,1)S(1)} collective-permute-done((bf16[1,25,8,128]{3,2,1,0:T(8,128)(2,1)S(1)}, bf16[1,25,8,128]{3,2,1,0:T(8,128)(2,1)S(1)}, u32[]{:S(2)}, u32[]{:S(2)}) %collective-permute-start.19) | collective-permute-done | bytes 51232 | tf_op jit(solution)/shard_map/ppermute | solution.py:36
  117.4 2.6 %collective-permute-start.22 = (bf16[1,25,8,128]{3,2,1,0:T(8,128)(2,1)S(1)}, bf16[1,25,8,128]{3,2,1,0:T(8,128)(2,1)S(1)}, u32[]{:S(2)}, u32[]{:S(2)}) collective-permute-start(bf16[1,25,8,128]{3,2,1,0:T(8,128)(2,1)S(1)} %add_convert_fusion.5), channel_id=1, source_target_pairs={{0,12},{2,14},{4,8},{6,10},{8,4},{10,6},{12,0},{14,2},{1,13},{3,15... | collective-permute-start | bytes 153608 | tf_op jit(solution)/shard_map/ppermute | solution.py:36
  120.7 2.6 %collective-permute-done.22 = bf16[1,25,8,128]{3,2,1,0:T(8,128)(2,1)S(1)} collective-permute-done((bf16[1,25,8,128]{3,2,1,0:T(8,128)(2,1)S(1)}, bf16[1,25,8,128]{3,2,1,0:T(8,128)(2,1)S(1)}, u32[]{:S(2)}, u32[]{:S(2)}) %collective-permute-start.22) | collective-permute-done | bytes 51232 | tf_op jit(solution)/shard_map/ppermute | solution.py:36
  125.5 2.6 %collective-permute-done.23 = bf16[52,8,128]{2,1,0:T(8,128)(2,1)S(1)} collective-permute-done((bf16[52,8,128]{2,1,0:T(8,128)(2,1)S(1)}, bf16[52,8,128]{2,1,0:T(8,128)(2,1)S(1)}, u32[]{:S(2)}, u32[]{:S(2)}) %collective-permute-start.23) | collective-permute-done | bytes 106528 | tf_op jit(solution)/shard_map/ppermute | solution.py:36
  131.3 3.0 %collective-permute-done.24 = bf16[104,8,128]{2,1,0:T(8,128)(2,1)S(1)} collective-permute-done((bf16[104,8,128]{2,1,0:T(8,128)(2,1)S(1)}, bf16[104,8,128]{2,1,0:T(8,128)(2,1)S(1)}, u32[]{:S(2)}, u32[]{:S(2)}) %collective-permute-start.24) | collective-permute-done | bytes 213024 | tf_op jit(solution)/shard_map/ppermute | solution.py:36
  138.2 3.4 %assemble.1 = (f32[128,5376]{1,0:T(8,128)}, f32[128,1024]{1,0:T(8,128)}) custom-call(s32[3]{0:T(128)} %pad_add_fusion.1.scalars_ref, bf16[16,13,8,128]{3,2,1,0:T(8,128)(2,1)} %bitcast.57, bf16[16,12,8,128]{3,2,1,0:T(8,128)(2,1)} %bitcast.58, bf16[16,13,8,128]{3,2,1,0:T(8,128)(2,1)} %bitcast.30.ra_ref, bf16[16,12,8,128]{3,2,1,0:T(8,128)(2,1)} %bitcast.31.rb_ref), custom_call_target="tpu_custom_call" | custom-call | tf_op jit(solution)/shard_map/assemble/pallas_call | solution.py:458
  141.6 2.3 %copy.29 = bf16[1,256,2048]{2,1,0:T(8,128)(2,1)} copy(bf16[1,256,2048]{2,1,0:T(8,128)(2,1)} %bitcast.15) | data formatting | bytes 2097152
  (145 shorter events, 50.4 us)
Async XLA Ops:
  3.3 27.4 %collective-permute-start.7 = (bf16[256,512]{1,0:T(8,128)(2,1)S(1)}, bf16[256,512]{1,0:T(8,128)(2,1)}, u32[]{:S(2)}, u32[]{:S(2)}) collective-permute-start(bf16[256,512]{1,0:T(8,128)(2,1)S(1)} %pad_maximum_fusion.6.refs_2_.refs_5_), channel_id=1, source_target_pairs={{0,4},{2,6},{4,8},{6,10},{8,12},{10,14},{1,5},{3,7},{5,9},{7,11},{... | collective-permute-start | bytes 786440 | tf_op jit(solution)/shard_map/ppermute | solution.py:26
  13.7 14.6 %collective-permute-start.3 = (bf16[256,128]{1,0:T(8,128)(2,1)S(1)}, bf16[256,128]{1,0:T(8,128)(2,1)}, u32[]{:S(2)}, u32[]{:S(2)}) collective-permute-start(bf16[256,128]{1,0:T(8,128)(2,1)S(1)} %fusion), channel_id=1, source_target_pairs={{0,4},{2,6},{4,8},{6,10},{8,12},{10,14},{1,5},{3,7},{5,9},{7,11},{... | collective-permute-start | bytes 196616 | tf_op jit(solution)/shard_map/ppermute | solution.py:26
  17.2 25.6 %collective-permute-start.2 = (bf16[1,256,2048]{2,1,0:T(8,128)(2,1)}, bf16[1,256,2048]{2,1,0:T(8,128)(2,1)S(1)}, u32[]{:S(2)}, u32[]{:S(2)}) collective-permute-start(bf16[1,256,2048]{2,1,0:T(8,128)(2,1)} %param.13), channel_id=1, source_target_pairs={{0,16},{16,0},{1,17},{17,1},{2,18},{18,2},{3,19},{19,3},{4,20},{20... | collective-permute-start | bytes 3145736 | tf_op jit(solution)/shard_map/ppermute | solution.py:31
  17.4 14.5 %collective-permute-start.5 = (bf16[256,768]{1,0:T(8,128)(2,1)S(1)}, bf16[256,768]{1,0:T(8,128)(2,1)}, u32[]{:S(2)}, u32[]{:S(2)}) collective-permute-start(bf16[256,768]{1,0:T(8,128)(2,1)S(1)} %pad_maximum_fusion.4.refs_2_.refs_5_), channel_id=1, source_target_pairs={{0,4},{2,6},{4,8},{6,10},{8,12},{10,14},{1,5},{3,7},{5,9},{7,11},{... | collective-permute-start | bytes 1179656 | tf_op jit(solution)/shard_map/ppermute | solution.py:26
  21.2 16.6 %collective-permute-start = (bf16[256,768]{1,0:T(8,128)(2,1)S(1)}, bf16[256,768]{1,0:T(8,128)(2,1)}, u32[]{:S(2)}, u32[]{:S(2)}) collective-permute-start(bf16[256,768]{1,0:T(8,128)(2,1)S(1)} %pad_maximum_fusion.1.refs_2_.refs_5_), channel_id=1, source_target_pairs={{0,4},{2,6},{4,8},{6,10},{8,12},{10,14},{1,5},{3,7},{5,9},{7,11},{... | collective-permute-start | bytes 1179656 | tf_op jit(solution)/shard_map/ppermute | solution.py:26
  28.3 13.0 %collective-permute-start.4 = (bf16[256,128]{1,0:T(8,128)(2,1)S(1)}, bf16[256,128]{1,0:T(8,128)(2,1)S(1)}, u32[]{:S(2)}, u32[]{:S(2)}) collective-permute-start(bf16[256,128]{1,0:T(8,128)(2,1)S(1)} %broadcast_select_fusion.3), channel_id=1, source_target_pairs={{0,2},{2,0},{4,6},{6,4},{8,10},{10,8},{12,14},{14,12},{1,3},{3,1},... | collective-permute-start | bytes 196616 | tf_op jit(solution)/shard_map/ppermute | solution.py:36
  31.8 11.1 %collective-permute-start.8 = (bf16[256,512]{1,0:T(8,128)(2,1)S(1)}, bf16[256,512]{1,0:T(8,128)(2,1)S(1)}, u32[]{:S(2)}, u32[]{:S(2)}) collective-permute-start(bf16[256,512]{1,0:T(8,128)(2,1)S(1)} %broadcast_select_fusion.2), channel_id=1, source_target_pairs={{0,2},{2,0},{4,6},{6,4},{8,10},{10,8},{12,14},{14,12},{1,3},{3,1},... | collective-permute-start | bytes 786440 | tf_op jit(solution)/shard_map/ppermute | solution.py:36
  33.8 18.1 %collective-permute-start.6 = (bf16[256,768]{1,0:T(8,128)(2,1)}, bf16[256,768]{1,0:T(8,128)(2,1)}, u32[]{:S(2)}, u32[]{:S(2)}) collective-permute-start(bf16[256,768]{1,0:T(8,128)(2,1)} %broadcast_select_fusion), channel_id=1, source_target_pairs={{0,2},{2,0},{4,6},{6,4},{8,10},{10,8},{12,14},{14,12},{1,3},{3,1},... | collective-permute-start | bytes 1179656 | tf_op jit(solution)/shard_map/ppermute | solution.py:36
  37.9 25.1 %collective-permute-start.1 = (bf16[256,768]{1,0:T(8,128)(2,1)S(1)}, bf16[256,768]{1,0:T(8,128)(2,1)S(1)}, u32[]{:S(2)}, u32[]{:S(2)}) collective-permute-start(bf16[256,768]{1,0:T(8,128)(2,1)S(1)} %broadcast_select_fusion.1), channel_id=1, source_target_pairs={{0,2},{2,0},{4,6},{6,4},{8,10},{10,8},{12,14},{14,12},{1,3},{3,1},... | collective-permute-start | bytes 1179656 | tf_op jit(solution)/shard_map/ppermute | solution.py:36
  74.8 7.1 %collective-permute-start.10 = (bf16[256,128]{1,0:T(8,128)(2,1)}, bf16[256,128]{1,0:T(8,128)(2,1)S(1)}, u32[]{:S(2)}, u32[]{:S(2)}) collective-permute-start(bf16[256,128]{1,0:T(8,128)(2,1)} %get-tuple-element.26), channel_id=1, source_target_pairs={{4,0},{6,2},{8,4},{10,6},{12,8},{14,10},{5,1},{7,3},{9,5},{11,7},{... | collective-permute-start | bytes 196616 | tf_op jit(solution)/shard_map/ppermute | solution.py:26
  76.1 6.4 %collective-permute-start.11 = (bf16[256,128]{1,0:T(8,128)(2,1)}, bf16[256,128]{1,0:T(8,128)(2,1)S(1)}, u32[]{:S(2)}, u32[]{:S(2)}) collective-permute-start(bf16[256,128]{1,0:T(8,128)(2,1)} %get-tuple-element.27), channel_id=1, source_target_pairs={{2,0},{4,2},{6,4},{8,6},{10,8},{12,10},{14,12},{3,1},{5,3},{7,5},{... | collective-permute-start | bytes 196616 | tf_op jit(solution)/shard_map/ppermute | solution.py:26
  90.8 7.0 %collective-permute-start.15 = (bf16[96,8,128]{2,1,0:T(8,128)(2,1)S(1)}, bf16[96,8,128]{2,1,0:T(8,128)(2,1)S(1)}, u32[]{:S(2)}, u32[]{:S(2)}) collective-permute-start(bf16[96,8,128]{2,1,0:T(8,128)(2,1)S(1)} %constant_dynamic-slice_fusion.1), channel_id=1, source_target_pairs={{0,1},{1,0},{2,3},{3,2},{4,5},{5,4},{6,7},{7,6},{8,9},{9,8},{10,11... | collective-permute-start | bytes 589832 | tf_op jit(solution)/shard_map/ppermute | solution.py:36
  92.5 8.2 %collective-permute-start.13 = (bf16[104,8,128]{2,1,0:T(8,128)(2,1)S(1)}, bf16[104,8,128]{2,1,0:T(8,128)(2,1)S(1)}, u32[]{:S(2)}, u32[]{:S(2)}) collective-permute-start(bf16[104,8,128]{2,1,0:T(8,128)(2,1)S(1)} %constant_dynamic-slice_fusion.3), channel_id=1, source_target_pairs={{0,2},{2,0},{4,6},{6,4},{8,10},{10,8},{12,14},{14,12},{1,3},{3,1},... | collective-permute-start | bytes 638984 | tf_op jit(solution)/shard_map/ppermute | solution.py:36
  97.9 5.3 %collective-permute-start.16 = (bf16[48,8,128]{2,1,0:T(8,128)(2,1)S(1)}, bf16[48,8,128]{2,1,0:T(8,128)(2,1)S(1)}, u32[]{:S(2)}, u32[]{:S(2)}) collective-permute-start(bf16[48,8,128]{2,1,0:T(8,128)(2,1)S(1)} %constant_dynamic-slice_fusion), channel_id=1, source_target_pairs={{0,2},{2,0},{4,6},{6,4},{8,10},{10,8},{12,14},{14,12},{1,3},{3,1},... | collective-permute-start | bytes 294920 | tf_op jit(solution)/shard_map/ppermute | solution.py:36
  100.8 4.8 %collective-permute-start.14 = (bf16[52,8,128]{2,1,0:T(8,128)(2,1)S(1)}, bf16[52,8,128]{2,1,0:T(8,128)(2,1)S(1)}, u32[]{:S(2)}, u32[]{:S(2)}) collective-permute-start(bf16[52,8,128]{2,1,0:T(8,128)(2,1)S(1)} %constant_dynamic-slice_fusion.2), channel_id=1, source_target_pairs={{0,1},{1,0},{2,3},{3,2},{4,5},{5,4},{6,7},{7,6},{8,9},{9,8},{10,11... | collective-permute-start | bytes 319496 | tf_op jit(solution)/shard_map/ppermute | solution.py:36
  105.6 5.1 %collective-permute-start.17 = (bf16[1,25,8,128]{3,2,1,0:T(8,128)(2,1)S(1)}, bf16[1,25,8,128]{3,2,1,0:T(8,128)(2,1)S(1)}, u32[]{:S(2)}, u32[]{:S(2)}) collective-permute-start(bf16[1,25,8,128]{3,2,1,0:T(8,128)(2,1)S(1)} %get-tuple-element.39), channel_id=1, source_target_pairs={{0,4},{2,6},{4,0},{6,2},{8,12},{10,14},{12,8},{14,10},{1,5},{3,7},... | collective-permute-start | bytes 153608 | tf_op jit(solution)/shard_map/ppermute | solution.py:36
  107.8 5.0 %collective-permute-start.18 = (bf16[1,25,8,128]{3,2,1,0:T(8,128)(2,1)S(1)}, bf16[1,25,8,128]{3,2,1,0:T(8,128)(2,1)S(1)}, u32[]{:S(2)}, u32[]{:S(2)}) collective-permute-start(bf16[1,25,8,128]{3,2,1,0:T(8,128)(2,1)S(1)} %get-tuple-element.40), channel_id=1, source_target_pairs={{0,8},{2,10},{4,12},{6,14},{8,0},{10,2},{12,4},{14,6},{1,9},{3,11}... | collective-permute-start | bytes 153608 | tf_op jit(solution)/shard_map/ppermute | solution.py:36
  109.5 6.0 %collective-permute-start.19 = (bf16[1,25,8,128]{3,2,1,0:T(8,128)(2,1)S(1)}, bf16[1,25,8,128]{3,2,1,0:T(8,128)(2,1)S(1)}, u32[]{:S(2)}, u32[]{:S(2)}) collective-permute-start(bf16[1,25,8,128]{3,2,1,0:T(8,128)(2,1)S(1)} %get-tuple-element.41), channel_id=1, source_target_pairs={{0,12},{2,14},{4,8},{6,10},{8,4},{10,6},{12,0},{14,2},{1,13},{3,15... | collective-permute-start | bytes 153608 | tf_op jit(solution)/shard_map/ppermute | solution.py:36
  115.6 5.1 %collective-permute-start.21 = (bf16[1,25,8,128]{3,2,1,0:T(8,128)(2,1)S(1)}, bf16[1,25,8,128]{3,2,1,0:T(8,128)(2,1)S(1)}, u32[]{:S(2)}, u32[]{:S(2)}) collective-permute-start(bf16[1,25,8,128]{3,2,1,0:T(8,128)(2,1)S(1)} %add_convert_fusion.5), channel_id=1, source_target_pairs={{0,8},{2,10},{4,12},{6,14},{8,0},{10,2},{12,4},{14,6},{1,9},{3,11}... | collective-permute-start | bytes 153608 | tf_op jit(solution)/shard_map/ppermute | solution.py:36
  117.4 5.9 %collective-permute-start.22 = (bf16[1,25,8,128]{3,2,1,0:T(8,128)(2,1)S(1)}, bf16[1,25,8,128]{3,2,1,0:T(8,128)(2,1)S(1)}, u32[]{:S(2)}, u32[]{:S(2)}) collective-permute-start(bf16[1,25,8,128]{3,2,1,0:T(8,128)(2,1)S(1)} %add_convert_fusion.5), channel_id=1, source_target_pairs={{0,12},{2,14},{4,8},{6,10},{8,4},{10,6},{12,0},{14,2},{1,13},{3,15... | collective-permute-start | bytes 153608 | tf_op jit(solution)/shard_map/ppermute | solution.py:36
  124.4 12.5 %collective-permute-start.9 = (bf16[256,2048]{1,0:T(8,128)(2,1)S(1)}, bf16[256,2048]{1,0:T(8,128)(2,1)}, u32[]{:S(2)}, u32[]{:S(2)}) collective-permute-start(bf16[256,2048]{1,0:T(8,128)(2,1)S(1)} %copy-done.2), channel_id=1, source_target_pairs={{0,16},{16,0},{1,17},{17,1},{2,18},{18,2},{3,19},{19,3},{4,20},{20... | collective-permute-start | bytes 3145736 | tf_op jit(solution)/shard_map/ppermute | solution.py:31
  124.5 5.7 %collective-permute-start.25 = (bf16[48,8,128]{2,1,0:T(8,128)(2,1)S(1)}, bf16[48,8,128]{2,1,0:T(8,128)(2,1)S(1)}, u32[]{:S(2)}, u32[]{:S(2)}) collective-permute-start(bf16[48,8,128]{2,1,0:T(8,128)(2,1)S(1)} %bitcast.66), channel_id=1, source_target_pairs={{0,2},{2,0},{4,6},{6,4},{8,10},{10,8},{12,14},{14,12},{1,3},{3,1},... | collective-permute-start | bytes 294920 | tf_op jit(solution)/shard_map/ppermute | solution.py:36
  128.2 6.1 %collective-permute-start.24 = (bf16[104,8,128]{2,1,0:T(8,128)(2,1)S(1)}, bf16[104,8,128]{2,1,0:T(8,128)(2,1)S(1)}, u32[]{:S(2)}, u32[]{:S(2)}) collective-permute-start(bf16[104,8,128]{2,1,0:T(8,128)(2,1)S(1)} %pad_maximum_fusion.7), channel_id=1, source_target_pairs={{0,2},{2,0},{4,6},{6,4},{8,10},{10,8},{12,14},{14,12},{1,3},{3,1},... | collective-permute-start | bytes 638984 | tf_op jit(solution)/shard_map/ppermute | solution.py:36
  130.2 6.0 %collective-permute-start.26 = (bf16[96,8,128]{2,1,0:T(8,128)(2,1)S(1)}, bf16[96,8,128]{2,1,0:T(8,128)(2,1)S(1)}, u32[]{:S(2)}, u32[]{:S(2)}) collective-permute-start(bf16[96,8,128]{2,1,0:T(8,128)(2,1)S(1)} %pad_maximum_fusion.9), channel_id=1, source_target_pairs={{0,1},{1,0},{2,3},{3,2},{4,5},{5,4},{6,7},{7,6},{8,9},{9,8},{10,11... | collective-permute-start | bytes 589832 | tf_op jit(solution)/shard_map/ppermute | solution.py:36
  (30 other events, 190.4 us)

commit v3 on v2

--- a/solution.py
+++ b/solution.py
@@ -10,10 +10,11 @@
 HD = 128
 WINDOW = 1024
 SUB = 8
-PIECES = (2, 3, 3)
+PIECES = 2
 
 query_scale = 168.0 ** (-0.5)
 adapter_scale = 0.5
+log2e = 1.4426950408889634
 rope_base = 10000.0
 masked_score = -1e30
 f32 = jnp.float32
@@ -54,57 +55,71 @@
     return jnp.sum((doc_ends[None, :] <= positions[:, None]).astype(jnp.int32), axis=1)
 
 
-def attention_kernel(*refs, n_blocks, tok, group, sub, chained):
-    k_refs, v_refs = refs[:n_blocks], refs[n_blocks : 2 * n_blocks]
-    at = 2 * n_blocks
-    q_ref, g_ref, spread_ref, up_ref, bias_ref, cos_ref, sin_ref = refs[at : at + 7]
-    at += 7
+def attention_kernel(*refs, n_blocks, heads, tok, group, sub, chained, is_last):
+    m_refs = refs[:n_blocks]
+    q_ref, g_ref, spread_ref, up_ref, bias_ref, cos_ref, sin_ref = refs[n_blocks : n_blocks + 7]
+    at = n_blocks + 7
+    if is_last:
+        mask_ref = refs[at]
+        at += 1
     if chained:
         lg_in_ref = refs[at]
         at += 3
     out_ref, u_ref, lg_ref = refs[at : at + 3]
     lg_low_refs = refs[at + 3 :]
-    step = pl.program_id(0)
-    up = up_ref[0]
     spread = spread_ref[...]
-    shift = adapter_scale * jnp.dot(spread, up, preferred_element_type=f32)
+    span = spread.shape[0]
+    half = spread.shape[1] // 2
     cos, sin = cos_ref[...], sin_ref[...]
-    key = jnp.concatenate([r[...] for r in k_refs], axis=0).astype(f32) + shift[:, :HD]
-    key = (key * cos + pltpu.roll(key, HD // 2, 1) * sin).astype(bf16)
-    val = jnp.concatenate([r[...] for r in v_refs], axis=0).astype(f32) + shift[:, HD:]
-    val = val.astype(bf16)
-    span = key.shape[0]
-    cos_q, sin_q = cos[span - tok :], sin[span - tok :]
-    queries, grads = [], []
-    for h in range(group):
-        q = q_ref[:, h * HD : (h + 1) * HD].astype(f32)
-        queries.append((q * cos_q + pltpu.roll(q, HD // 2, 1) * sin_q).astype(bf16))
-        grads.append(g_ref[:, h * HD : (h + 1) * HD])
     dot = partial(lax.dot_general, preferred_element_type=f32)
     last, first = (((1,), (1,)), ((), ())), (((0,), (0,)), ((), ()))
     length = span - tok + sub
-    dkeys, dvals = [], []
-    for i in range(tok // sub):
+    subs = tok // sub
+
+    def prepare(h):
+        shift = adapter_scale * jnp.dot(spread, up_ref[h], preferred_element_type=f32)
+        kc, vc = slice(h * HD, (h + 1) * HD), slice((heads + h) * HD, (heads + h + 1) * HD)
+        key = jnp.concatenate([r[:, kc] for r in m_refs], axis=0).astype(f32) + shift[:, :HD]
+        key = (key * cos + pltpu.roll(key, HD // 2, 1) * sin).astype(bf16)
+        val = jnp.concatenate([r[:, vc] for r in m_refs], axis=0).astype(f32) + shift[:, HD:]
+        return key, val.astype(bf16)
+
+    def scored(h, i, key):
         cut = slice(i * sub, (i + 1) * sub)
         rows = slice(i * sub, i * sub + length)
-        q = jnp.concatenate([x[cut] for x in queries], axis=0)
-        g = jnp.concatenate([x[cut] for x in grads], axis=0)
+        cq, sq = cos[span - tok + i * sub : span - tok + (i + 1) * sub], sin[span - tok + i * sub : span - tok + (i + 1) * sub]
+        queries = []
+        for j in range(group):
+            q = q_ref[cut, (h * group + j) * HD : (h * group + j + 1) * HD].astype(f32)
+            q = q * cq + pltpu.roll(q, HD // 2, 1) * sq
+            queries.append((q * (query_scale * log2e)).astype(bf16))
+        q = jnp.concatenate(queries, axis=0)
         bias = jnp.concatenate([bias_ref[rows, cut]] * group, axis=1)
-        scores = dot(key[rows], q, last) * query_scale + bias
+        return q, dot(key[rows], q, last) + bias
+
+    def forward(h, i, scores, val):
+        cut = slice(i * sub, (i + 1) * sub)
+        rows = slice(i * sub, i * sub + length)
         top = jnp.max(scores, axis=0, keepdims=True)
-        probs = jnp.exp(scores - top)
-        total = jnp.sum(probs, axis=0, keepdims=True)
-        probs = probs * (1.0 / total)
+        probs = jnp.exp2(scores - top)
+        scale = 1.0 / jnp.sum(probs, axis=0, keepdims=True)
         low_probs = probs.astype(bf16)
-        out_t = dot(val[rows], low_probs, first).astype(bf16)
+        out_t = (dot(val[rows], low_probs, first) * scale).astype(bf16)
         out = out_t.T
-        for h in range(group):
-            out_ref[cut, h * HD : (h + 1) * HD] = out[h * sub : (h + 1) * sub]
-        drift = jnp.sum(out_t.astype(f32) * g.T.astype(f32), axis=0, keepdims=True)
-        dprob = dot(val[rows], g, last)
+        gs = []
+        for j in range(group):
+            lanes = slice((h * group + j) * HD, (h * group + j + 1) * HD)
+            out_ref[cut, lanes] = out[j * sub : (j + 1) * sub]
+            gs.append(g_ref[cut, lanes])
+        g_t = (jnp.concatenate(gs, axis=0).T.astype(f32) * scale).astype(bf16)
+        drift = jnp.sum(out_t.astype(f32) * g_t.astype(f32), axis=0, keepdims=True)
+        dprob = jnp.dot(val[rows], g_t, preferred_element_type=f32)
+        return probs, low_probs, g_t, drift, dprob
+
+    def backward(q, state):
+        probs, low_probs, g_t, drift, dprob = state
         dscore = (probs * (dprob - drift)).astype(bf16)
-        dkeys.append(jnp.dot(dscore, q, preferred_element_type=f32))
-        dvals.append(jnp.dot(low_probs, g, preferred_element_type=f32))
+        return jnp.dot(dscore, q, preferred_element_type=f32), dot(low_probs, g_t, last)
 
     def overlapped(parts):
         rows = []
@@ -113,34 +128,43 @@
             rows.append(sum(here[1:], here[0]))
         return jnp.concatenate(rows, axis=0)
 
-    dkey = query_scale * overlapped(dkeys)
-    dval = overlapped(dvals)
-    dkey = dkey * cos - pltpu.roll(dkey, HD // 2, 1) * sin
-    both = jnp.concatenate([dkey.astype(bf16), dval.astype(bf16)], axis=1)
-    lg = dot(both, up, last)
-
-    @pl.when(step == 0)
-    def _():
-        lg_ref[...] = lg_in_ref[...] + lg if chained else lg
-
-    @pl.when(step != 0)
-    def _():
-        lg_ref[...] += lg
-
-    if lg_low_refs:
-
-        @pl.when(step == pl.num_programs(0) - 1)
-        def _():
-            for j, ref in enumerate(lg_low_refs):
-                ref[...] = lg_ref[j * tok : (j + 1) * tok].astype(bf16)
-
-    u = adapter_scale * dot(spread, both, first)
-    half = spread.shape[1] // 2
-    u_ref[0] = u[:half, :HD].astype(bf16)
-    u_ref[1] = u[half:, HD:].astype(bf16)
-
-
-def attention(blocks, start, carried, is_last, q_rows, g_rows, spread, up_cat, bias, cos, sin):
+    def finish(h, parts):
+        dkey = (1.0 / log2e) * overlapped([p[0] for p in parts])
+        dval = overlapped([p[1] for p in parts])
+        dkey = dkey * cos - pltpu.roll(dkey, HD // 2, 1) * sin
+        both = jnp.concatenate([dkey.astype(bf16), dval.astype(bf16)], axis=1)
+        lg = dot(both, up_ref[h], last)
+        if h > 0:
+            lg_ref[...] += lg
+        else:
+            lg_ref[...] = lg_in_ref[...] + lg if chained else lg
+        u = adapter_scale * dot(spread, both, first)
+        u_ref[0, :, h * HD : (h + 1) * HD] = u[:half, :HD].astype(bf16)
+        u_ref[1, :, h * HD : (h + 1) * HD] = u[half:, HD:].astype(bf16)
+
+    units = [(h, i) for h in range(heads) for i in range(subs)]
+    prepared, scores, states, grads = {}, {}, {}, {}
+    for t in range(len(units) + 2):
+        if t < len(units):
+            h, i = units[t]
+            if i == 0:
+                prepared[h] = prepare(h)
+            scores[h, i] = scored(h, i, prepared[h][0])
+        if 0 <= t - 1 < len(units):
+            h, i = units[t - 1]
+            states[h, i] = forward(h, i, scores[h, i][1], prepared[h][1])
+        if 0 <= t - 2 < len(units):
+            h, i = units[t - 2]
+            grads.setdefault(h, []).append(backward(scores[h, i][0], states[h, i]))
+            if i == subs - 1:
+                finish(h, grads[h])
+    if is_last:
+        lg_ref[...] *= mask_ref[...]
+    for j, ref in enumerate(lg_low_refs):
+        ref[...] = lg_ref[j * tok : (j + 1) * tok].astype(bf16)
+
+
+def attention(blocks, piece, carried, mask, q_rows, g_rows, spread, up_cat, bias, cos, sin):
     tok = q_rows.shape[0]
     heads = blocks[0].shape[1] // (2 * HD)
     kv_heads, width, _ = up_cat.shape
@@ -151,25 +175,28 @@
     sub = HD if tok % HD == 0 else tok
     whole = lambda shape: pl.BlockSpec(shape, lambda h: (0,) * len(shape))
     any_space = pl.BlockSpec(memory_space=pl.ANY)
-    out_spec = pl.BlockSpec((tok, group * HD), lambda h: (0, h + start))
-    u_spec = pl.BlockSpec((2, half, HD), lambda h: (0, 0, h + start))
+    out_spec = pl.BlockSpec((tok, heads * group * HD), lambda i: (0, piece))
+    u_spec = pl.BlockSpec((2, half, heads * HD), lambda i: (0, 0, piece))
     in_specs = (
-        [pl.BlockSpec((tok, HD), lambda h: (0, h))] * n_blocks
-        + [pl.BlockSpec((tok, HD), lambda h: (0, h + heads))] * n_blocks
+        [whole((tok, 2 * heads * HD))] * n_blocks
         + [out_spec] * 2
         + [
             whole((span, width)),
-            pl.BlockSpec((1, width, 2 * HD), lambda h: (h + start, 0, 0)),
+            pl.BlockSpec((heads, width, 2 * HD), lambda i: (piece, 0, 0)),
             whole((span, tok)),
             whole((span, HD)),
             whole((span, HD)),
         ]
     )
     extra, aliases = [], {}
+    is_last = mask is not None
+    if is_last:
+        extra = [mask]
+        in_specs = in_specs + [whole((span, width))]
     if carried is not None:
         out, u, lg = carried
         at = len(in_specs)
-        extra, aliases = [lg, out, u], {at + 1: 0, at + 2: 1}
+        extra, aliases = extra + [lg, out, u], {at + 1: 0, at + 2: 1}
         in_specs = in_specs + [whole((span, width)), any_space, any_space]
     low_count = n_blocks - 1 if is_last else 0
     work = heads * group * tok * (span - tok + sub) * HD * 2 * 6
@@ -177,12 +204,14 @@
         partial(
             attention_kernel,
             n_blocks=n_blocks,
+            heads=heads,
             tok=tok,
             group=group,
             sub=sub,
             chained=carried is not None,
+            is_last=is_last,
         ),
-        grid=(heads,),
+        grid=(1,),
         in_specs=in_specs,
         out_specs=[out_spec, u_spec, whole((span, width))] + [whole((tok, width))] * low_count,
         out_shape=[
@@ -195,19 +224,17 @@
         compiler_params=pltpu.CompilerParams(dimension_semantics=("arbitrary",)),
         cost_estimate=pl.CostEstimate(flops=work, transcendentals=0, bytes_accessed=heads * tok * HD * 20),
         name="attention",
-    )(*blocks, *blocks, q_rows, g_rows, spread, up_cat, bias, cos, sin, *extra)
+    )(*blocks, q_rows, g_rows, spread, up_cat, bias, cos, sin, *extra)
 
 
 def product_kernel(*refs, n_recv, cols, up_cols):
     side_ref, lg_ref = refs[:2]
     recv = refs[2 : 2 + n_recv]
-    mask_ref, hidden_ref = refs[2 + n_recv : 4 + n_recv]
-    up_ref, keep_ref, send_ref = refs[4 + n_recv :]
+    hidden_ref, up_ref, keep_ref, send_ref = refs[2 + n_recv :]
     side = side_ref[0]
     total = lg_ref[...]
     for r in recv:
         total = total + r[...].astype(f32)
-    total = total * mask_ref[...]
     width = total.shape[1]
     half = width // 2
     total = jnp.where(side == 0, total, pltpu.roll(total, half, 1)).astype(bf16)
@@ -238,7 +265,9 @@
         send_ref[pl.ds(used, rest)] = jnp.zeros((rest, SUB, HD), bf16)
 
 
-def assemble_kernel(scalars_ref, ma_ref, mb_ref, ra_ref, rb_ref, w_ref, u_ref, *, cols, rows):
+def assemble_kernel(
+    scalars_ref, ma_ref, mb_ref, ra_ref, rb_ref, handed_ref, w_ref, u_ref, same_ref, *, cols, rows
+):
     side, me_a, me_b = scalars_ref[0], scalars_ref[1], scalars_ref[2]
     n_a, a = ma_ref.shape[:2]
     b = mb_ref.shape[1]
@@ -333,12 +362,12 @@
     reach = min(-(-(min(WINDOW, longest) - 1) // tok), ctx_size - 1)
     steps = (reach + 1) // 2
 
-    pieces = PIECES if sum(PIECES) == kv_heads else (kv_heads,)
-    starts = [sum(pieces[:i]) for i in range(len(pieces))]
+    pieces = PIECES if kv_heads % PIECES == 0 else 1
+    count = kv_heads // pieces
     keys, vals = frozen_key_rows[0], frozen_value_rows[0]
     parts = []
-    for first, count in zip(starts, pieces):
-        cut = slice(first * HD, (first + count) * HD)
+    for i in range(pieces):
+        cut = slice(i * count * HD, (i + 1) * count * HD)
         own = jnp.concatenate([keys[:, cut], vals[:, cut]], axis=1)
         parts.append(window_blocks(own, steps)[::-1] + [own])
     returned = permute_cyclic(next_output_gradient, "section", -1)
@@ -347,10 +376,11 @@
     key_pos = (block_starts[:, None] + jnp.arange(tok, dtype=jnp.int32)[None, :]).reshape(-1)
     key_docs = doc_index(document_lengths[0], key_pos)
     positions, docs = key_pos[-tok:], key_docs[-tok:]
-    picked = docs[:, None] == jnp.arange(document_lengths.shape[1], dtype=jnp.int32)[None, :]
+    picked = key_docs[:, None] == jnp.arange(document_lengths.shape[1], dtype=jnp.int32)[None, :]
     tenant = jnp.sum(picked.astype(jnp.int32) * document_adapter[0][None, :], axis=1)
     lane_adapter = (jnp.arange(width, dtype=jnp.int32) // rank) % adapters
-    mask = (tenant[:, None] == lane_adapter[None, :]).astype(f32)
+    span_mask = jnp.where(tenant[:, None] == lane_adapter[None, :], adapter_scale, 0.0).astype(f32)
+    mask = (tenant[-tok:, None] == lane_adapter[None, :]).astype(f32)
     gap = positions[None, :] - key_pos[:, None]
     allowed = (
         (key_docs[:, None] == docs[None, :])
@@ -382,12 +412,12 @@
     )
 
     carried = None
-    for i in range(len(pieces)):
+    for i in range(pieces):
         result = attention(
             parts[i],
-            starts[i],
+            i,
             carried,
-            i == len(pieces) - 1,
+            span_mask if i == pieces - 1 else None,
             frozen_query_rows[0],
             returned[0],
             spread,
@@ -418,12 +448,12 @@
         partial(
             product_kernel, n_recv=len(received), cols=cols, up_cols=up_cols
         ),
-        in_specs=[smem] + [pl.BlockSpec((tok, width), lambda i: (2 * steps, 0))] + [vmem] * (3 + len(received)),
+        in_specs=[smem] + [pl.BlockSpec((tok, width), lambda i: (2 * steps, 0))] + [vmem] * (2 + len(received)),
         grid=(1,),
         out_specs=[vmem, vmem],
         out_shape=[jax.ShapeDtypeStruct((units * group, SUB, HD), bf16)] * 2,
         name="product",
-    )(side[None], lg, *received, adapter_scale * mask, hidden[0], ups)
+    )(side[None], lg, *received, hidden[0], ups)
     recv = permute_cyclic(send, "section", 1)
     tiles = (keep.astype(f32) + recv.astype(f32)).astype(bf16)
     colours = [tiles[: a * group], tiles[a * group :]]
@@ -455,13 +485,16 @@
         colours = [gather_stage(colours[c], other[c][k]) for c in range(2)]
     theirs = [permute_cyclic(t, "section", 1) for t in colours]
     shapes = [(group, a, SUB, HD), (group, b, SUB, HD)]
-    w, u = pl.pallas_call(
+    any_space = pl.BlockSpec(memory_space=pl.ANY)
+    w, u, handed = pl.pallas_call(
         partial(assemble_kernel, cols=cols, rows=rows),
-        in_specs=[smem] + [vmem] * 4,
-        out_specs=[vmem, vmem],
+        in_specs=[smem] + [vmem] * 4 + [any_space],
+        out_specs=[vmem, vmem, any_space],
+        input_output_aliases={5: 2},
         out_shape=[
             jax.ShapeDtypeStruct((width, model_width), f32),
             jax.ShapeDtypeStruct((width, kv_width), f32),
+            jax.ShapeDtypeStruct(handed.shape, bf16),
         ],
         name="assemble",
     )(
@@ -470,6 +503,7 @@
         colours[1].reshape(shapes[1]),
         theirs[0].reshape(shapes[0]),
         theirs[1].reshape(shapes[1]),
+        handed,
     )
     down_map_gradient = w.T.reshape(model_width, 2, adapters, rank)
     up_map_gradient = u.reshape(2, adapters, rank, kv_width)

time: 145 us -> 147 us (1.014)
  waiting for transfers between devices: 32.2 us -> 52.5 us
  Pallas kernels: 37.3 us -> 25.9 us
  starting transfers between devices: 47.6 us -> 43 us
    ppermute x18 -> x17, waiting for transfers between devices: 22.3 us -> 42 us  [permute_xor(): return lax.ppermute(value, axis, [(i, i ^ bit) for i in range(count)])]
    pallas_call x3 -> x2, Pallas kernels: 30.1 us -> 18.8 us  [attention(): pl.pallas_call(partial(attention_kernel, n_blocks=n_blocks, heads=heads,...]
    ppermute x6 -> x5, starting transfers between devices: 17.8 us -> 14.6 us  [permute_by(): lax.ppermute(value, axis, [(i, i + steps) for i in range(first, last)])]
    select_n x4 -> x3, other arithmetic: 3 us -> 0.33 us  [window_blocks(): payload = jnp.where(even, chain[i], chain[i + 1])]
    ppermute x18 -> x17, starting transfers between devices: 29.7 us -> 28.2 us  [permute_xor(): return lax.ppermute(value, axis, [(i, i ^ bit) for i in range(count)])]
    ppermute x6 -> x5, waiting for transfers between devices: 6.12 us -> 6.69 us  [permute_by(): lax.ppermute(value, axis, [(i, i + steps) for i in range(first, last)])]
    unnamed x52 -> x36, local copies, waits for them, and re-layouts: 5.48 us -> 5.59 us
  transfers between devices with their start and end apart: 29 -> 27, of which waited for: 16 -> 18; matrix products, arithmetic and copies ran while one was open for 12% -> 11% of each run, Pallas kernels for 13% -> 6%
where the time goes in v3:
time: 147 us
  waiting for transfers between devices  52.5 us (36%)
  starting transfers between devices  43 us (29%)
  Pallas kernels  25.9 us (18%)
  other arithmetic  13.3 us (9%)
  local copies, waits for them, and re-layouts  8.39 us (6%)
  matrix products  2.64 us (2%)
    ppermute x17, waiting for transfers between devices, permute_xor(): return lax.ppermute(value, axis, [(i, i ^ bit) for i in range(count)])  42 us
    ppermute x17, starting transfers between devices, permute_xor(): return lax.ppermute(value, axis, [(i, i ^ bit) for i in range(count)])  28.2 us
    pallas_call x2, Pallas kernels, attention(): pl.pallas_call(partial(attention_kernel, n_blocks=n_blocks, heads=heads,...  18.8 us
    ppermute x5, starting transfers between devices, permute_by(): lax.ppermute(value, axis, [(i, i + steps) for i in range(first, last)])  14.6 us
    ppermute x5, waiting for transfers between devices, permute_by(): lax.ppermute(value, axis, [(i, i + steps) for i in range(first, last)])  6.69 us
    unnamed x36, local copies, waits for them, and re-layouts  5.59 us
    ppermute x5, waiting for transfers between devices, permute_cyclic(): lax.ppermute(value, axis, [(i, (i + by) % count) for i in range(count)])  3.76 us
    pallas_call x1, Pallas kernels, body(): pl.pallas_call(partial(product_kernel, n_recv=len(received), cols=cols, u...  3.69 us
  transfers between devices with their start and end apart: 27, of which 18 were waited for; matrix products, arithmetic and copies ran while one was open for 11% of the time, Pallas kernels for 6%

profile of v3, /device:TPU:0, one launch (start us, length us, event | category | flops | bytes accessed | tf_op | source)
XLA Modules:
  0.0 146.7 jit_solution(12011806882510404837)
XLA Ops:
  2.9 5.7 %collective-permute-start.5 = (bf16[256,1024]{1,0:T(8,128)(2,1)}, bf16[256,1024]{1,0:T(8,128)(2,1)}, u32[]{:S(2)}, u32[]{:S(2)}) collective-permute-start(bf16[256,1024]{1,0:T(8,128)(2,1)} %pad_maximum_fusion.1.refs_2_), channel_id=1, source_target_pairs={{0,4},{2,6},{4,8},{6,10},{8,12},{10,14},{1,5},{3,7},{5,9},{7,11},{... | collective-permute-start | bytes 1572872 | tf_op jit(solution)/shard_map/ppermute | solution.py:27
  9.3 2.6 %fusion = bf16[256,128]{1,0:T(8,128)(2,1)S(1)} fusion(bf16[5376,128]{0,1:T(8,128)(2,1)S(1)} %bitcast.49, s32[128]{0:T(128)S(1)} %and_select_fusion, s32[256]{0:T(256)S(1)} %slice.42, bf16[1,256,5376]{2,1,0:T(8,128)(2,1)} %param.9), kind=kOutput, calls=%fused_computation.4 | convolution fusion | flops 352419840 | bytes 4195840 | tf_op jit(solution)/shard_map/dot_general | solution.py:398
  11.9 3.3 %collective-permute-start.3 = (bf16[256,128]{1,0:T(8,128)(2,1)S(1)}, bf16[256,128]{1,0:T(8,128)(2,1)}, u32[]{:S(2)}, u32[]{:S(2)}) collective-permute-start(bf16[256,128]{1,0:T(8,128)(2,1)S(1)} %fusion), channel_id=1, source_target_pairs={{0,4},{2,6},{4,8},{6,10},{8,12},{10,14},{1,5},{3,7},{5,9},{7,11},{... | collective-permute-start | bytes 196616 | tf_op jit(solution)/shard_map/ppermute | solution.py:27
  15.4 3.0 %collective-permute-start = (bf16[256,1024]{1,0:T(8,128)(2,1)S(1)}, bf16[256,1024]{1,0:T(8,128)(2,1)S(1)}, u32[]{:S(2)}, u32[]{:S(2)}) collective-permute-start(bf16[256,1024]{1,0:T(8,128)(2,1)S(1)} %pad_maximum_fusion.refs_2_), channel_id=1, source_target_pairs={{0,4},{2,6},{4,8},{6,10},{8,12},{10,14},{1,5},{3,7},{5,9},{7,11},{... | collective-permute-start | bytes 1572872 | tf_op jit(solution)/shard_map/ppermute | solution.py:27
  21.7 2.1 %fusion.8 = (f32[768,64]{1,0:T(8,128)S(1)}, f32[768,64]{1,0:T(8,128)S(1)}, f32[768,64]{1,0:T(8,128)S(1)}) fusion(f32[64]{0:T(128)} %multiply_power_fusion, f32[768]{0:T(1024)S(1)} %convert_element_type.102), kind=kLoop, calls=%fused_computation.44 | loop fusion | flops 98304 | bytes 593152 | tf_op jit(solution)/shard_map/neg | solution.py:396
  27.6 2.6 %collective-permute-start.6 = (bf16[256,1024]{1,0:T(8,128)(2,1)S(1)}, bf16[256,1024]{1,0:T(8,128)(2,1)S(1)}, u32[]{:S(2)}, u32[]{:S(2)}) collective-permute-start(bf16[256,1024]{1,0:T(8,128)(2,1)S(1)} %broadcast_select_fusion), channel_id=1, source_target_pairs={{0,2},{2,0},{4,6},{6,4},{8,10},{10,8},{12,14},{14,12},{1,3},{3,1},... | collective-permute-start | bytes 1572872 | tf_op jit(solution)/shard_map/ppermute | solution.py:37
  35.9 19.3 %collective-permute-done.4 = bf16[256,128]{1,0:T(8,128)(2,1)S(1)} collective-permute-done((bf16[256,128]{1,0:T(8,128)(2,1)S(1)}, bf16[256,128]{1,0:T(8,128)(2,1)S(1)}, u32[]{:S(2)}, u32[]{:S(2)}) %collective-permute-start.4) | collective-permute-done | bytes 65568 | tf_op jit(solution)/shard_map/ppermute | solution.py:37
  57.5 9.2 %attention.2 = (bf16[256,2048]{1,0:T(8,128)(2,1)}, bf16[2,64,1024]{2,1,0:T(8,128)(2,1)}, f32[768,128]{1,0:T(8,128)}) custom-call(bf16[256,1024]{1,0:T(8,128)(2,1)} %collective-permute-done.5.refs_0_, bf16[256,1024]{1,0:T(8,128)(2,1)} %copy-done.16, bf16[256,1024]{1,0:T(8,128)(2,1)} %pad_maximum_fusion.1.refs_2_, bf16[256,2048]{1,0:T(8,128)(2,1)} %bitcast.54, ...), custom_call_target="tpu_custom_call" | custom-call | flops 2013265920 | bytes 2621440 | tf_op jit(solution)/shard_map/attention/pallas_call | solution.py:203
  67.5 9.6 %attention.3 = (bf16[256,2048]{1,0:T(8,128)(2,1)}, bf16[2,64,1024]{2,1,0:T(8,128)(2,1)}, f32[768,128]{1,0:T(8,128)}, bf16[256,128]{1,0:T(8,128)(2,1)}, bf16[256,128]{1,0:T(8,128)(2,1)}) custom-call(bf16[256,1024]{1,0:T(8,128)(2,1)} %copy-done.3, bf16[256,1024]{1,0:T(8,128)(2,1)} %copy-done.6, ...), custom_call_target="tpu_custom_call", output_to_operand_aliasing={{0}: (12, {}), {1}: (13, {})} | custom-call | flops 2013265920 | bytes 2621440 | tf_op jit(solution)/shard_map/attention/pallas_call | solution.py:203
  79.7 3.8 %collective-permute-done.7.refs_2_ = bf16[256,128]{1,0:T(8,128)(2,1)S(1)} collective-permute-done((bf16[256,128]{1,0:T(8,128)(2,1)}, bf16[256,128]{1,0:T(8,128)(2,1)S(1)}, u32[]{:S(2)}, u32[]{:S(2)}) %collective-permute-start.7) | collective-permute-done | bytes 65568 | tf_op jit(solution)/shard_map/ppermute | solution.py:27
  85.4 3.7 %product.1 = (bf16[400,8,128]{2,1,0:T(8,128)(2,1)}, bf16[400,8,128]{2,1,0:T(8,128)(2,1)}) custom-call(s32[1]{0:T(128)} %bitcast.refs_0_, f32[768,128]{1,0:T(8,128)} %get-tuple-element.19.refs_1_, bf16[256,128]{1,0:T(8,128)(2,1)} %copy-done.7, bf16[256,128]{1,0:T(8,128)(2,1)} %copy-done.8, bf16[256,5376]{1,0:T(8,128)(2,1)} %bitcast.50, ...), custom_call_target="tpu_custom_call" | custom-call | tf_op jit(solution)/shard_map/product/pallas_call | solution.py:447
  89.1 2.5 %collective-permute-done.9 = bf16[400,8,128]{2,1,0:T(8,128)(2,1)S(1)} collective-permute-done((bf16[400,8,128]{2,1,0:T(8,128)(2,1)}, bf16[400,8,128]{2,1,0:T(8,128)(2,1)S(1)}, u32[]{:S(2)}, u32[]{:S(2)}) %collective-permute-start.9) | collective-permute-done | bytes 819232 | tf_op jit(solution)/shard_map/ppermute | solution.py:32
  94.7 2.7 %collective-permute-start.10 = (bf16[104,8,128]{2,1,0:T(8,128)(2,1)S(1)}, bf16[104,8,128]{2,1,0:T(8,128)(2,1)S(1)}, u32[]{:S(2)}, u32[]{:S(2)}) collective-permute-start(bf16[104,8,128]{2,1,0:T(8,128)(2,1)S(1)} %constant_dynamic-slice_fusion.3), channel_id=1, source_target_pairs={{0,2},{2,0},{4,6},{6,4},{8,10},{10,8},{12,14},{14,12},{1,3},{3,1},... | collective-permute-start | bytes 638984 | tf_op jit(solution)/shard_map/ppermute | solution.py:37
  97.4 2.7 %collective-permute-done.12 = bf16[96,8,128]{2,1,0:T(8,128)(2,1)S(1)} collective-permute-done((bf16[96,8,128]{2,1,0:T(8,128)(2,1)S(1)}, bf16[96,8,128]{2,1,0:T(8,128)(2,1)S(1)}, u32[]{:S(2)}, u32[]{:S(2)}) %collective-permute-start.12) | collective-permute-done | bytes 196640 | tf_op jit(solution)/shard_map/ppermute | solution.py:37
  100.2 2.7 %collective-permute-start.13 = (bf16[48,8,128]{2,1,0:T(8,128)(2,1)S(1)}, bf16[48,8,128]{2,1,0:T(8,128)(2,1)S(1)}, u32[]{:S(2)}, u32[]{:S(2)}) collective-permute-start(bf16[48,8,128]{2,1,0:T(8,128)(2,1)S(1)} %constant_dynamic-slice_fusion), channel_id=1, source_target_pairs={{0,2},{2,0},{4,6},{6,4},{8,10},{10,8},{12,14},{14,12},{1,3},{3,1},... | collective-permute-start | bytes 294920 | tf_op jit(solution)/shard_map/ppermute | solution.py:37
  105.5 2.2 %collective-permute-done.11 = bf16[52,8,128]{2,1,0:T(8,128)(2,1)S(1)} collective-permute-done((bf16[52,8,128]{2,1,0:T(8,128)(2,1)S(1)}, bf16[52,8,128]{2,1,0:T(8,128)(2,1)S(1)}, u32[]{:S(2)}, u32[]{:S(2)}) %collective-permute-start.11) | collective-permute-done | bytes 106528 | tf_op jit(solution)/shard_map/ppermute | solution.py:37
  107.8 2.7 %collective-permute-start.14 = (bf16[1,25,8,128]{3,2,1,0:T(8,128)(2,1)S(1)}, bf16[1,25,8,128]{3,2,1,0:T(8,128)(2,1)S(1)}, u32[]{:S(2)}, u32[]{:S(2)}) collective-permute-start(bf16[1,25,8,128]{3,2,1,0:T(8,128)(2,1)S(1)} %get-tuple-element.35), channel_id=1, source_target_pairs={{0,4},{2,6},{4,0},{6,2},{8,12},{10,14},{12,8},{14,10},{1,5},{3,7},... | collective-permute-start | bytes 153608 | tf_op jit(solution)/shard_map/ppermute | solution.py:37
  110.5 2.4 %collective-permute-start.16 = (bf16[1,25,8,128]{3,2,1,0:T(8,128)(2,1)S(1)}, bf16[1,25,8,128]{3,2,1,0:T(8,128)(2,1)S(1)}, u32[]{:S(2)}, u32[]{:S(2)}) collective-permute-start(bf16[1,25,8,128]{3,2,1,0:T(8,128)(2,1)S(1)} %get-tuple-element.37), channel_id=1, source_target_pairs={{0,12},{2,14},{4,8},{6,10},{8,4},{10,6},{12,0},{14,2},{1,13},{3,15... | collective-permute-start | bytes 153608 | tf_op jit(solution)/shard_map/ppermute | solution.py:37
  117.3 2.3 %collective-permute-start.18 = (bf16[1,25,8,128]{3,2,1,0:T(8,128)(2,1)S(1)}, bf16[1,25,8,128]{3,2,1,0:T(8,128)(2,1)S(1)}, u32[]{:S(2)}, u32[]{:S(2)}) collective-permute-start(bf16[1,25,8,128]{3,2,1,0:T(8,128)(2,1)S(1)} %add_convert_fusion.5), channel_id=1, source_target_pairs={{0,8},{2,10},{4,12},{6,14},{8,0},{10,2},{12,4},{14,6},{1,9},{3,11}... | collective-permute-start | bytes 153608 | tf_op jit(solution)/shard_map/ppermute | solution.py:37
  122.3 3.2 %collective-permute-done.19 = bf16[1,25,8,128]{3,2,1,0:T(8,128)(2,1)S(1)} collective-permute-done((bf16[1,25,8,128]{3,2,1,0:T(8,128)(2,1)S(1)}, bf16[1,25,8,128]{3,2,1,0:T(8,128)(2,1)S(1)}, u32[]{:S(2)}, u32[]{:S(2)}) %collective-permute-start.19) | collective-permute-done | bytes 51232 | tf_op jit(solution)/shard_map/ppermute | solution.py:37
  127.8 2.5 %collective-permute-done.20 = bf16[52,8,128]{2,1,0:T(8,128)(2,1)S(1)} collective-permute-done((bf16[52,8,128]{2,1,0:T(8,128)(2,1)S(1)}, bf16[52,8,128]{2,1,0:T(8,128)(2,1)S(1)}, u32[]{:S(2)}, u32[]{:S(2)}) %collective-permute-start.20) | collective-permute-done | bytes 106528 | tf_op jit(solution)/shard_map/ppermute | solution.py:37
  133.5 3.6 %collective-permute-done.21 = bf16[104,8,128]{2,1,0:T(8,128)(2,1)S(1)} collective-permute-done((bf16[104,8,128]{2,1,0:T(8,128)(2,1)S(1)}, bf16[104,8,128]{2,1,0:T(8,128)(2,1)S(1)}, u32[]{:S(2)}, u32[]{:S(2)}) %collective-permute-start.21) | collective-permute-done | bytes 213024 | tf_op jit(solution)/shard_map/ppermute | solution.py:37
  141.0 3.4 %assemble.1 = (f32[128,5376]{1,0:T(8,128)}, f32[128,1024]{1,0:T(8,128)}, bf16[1,256,2048]{2,1,0:T(8,128)(2,1)}) custom-call(s32[3]{0:T(128)} %pad_add_fusion.scalars_ref, bf16[16,13,8,128]{3,2,1,0:T(8,128)(2,1)} %bitcast.52, bf16[16,12,8,128]{3,2,1,0:T(8,128)(2,1)} %bitcast.53, ...), custom_call_target="tpu_custom_call", output_to_operand_aliasing={{2}: (5, {})} | custom-call | tf_op jit(solution)/shard_map/assemble/pallas_call | solution.py:489
  144.4 2.3 %copy.27 = bf16[1,256,2048]{2,1,0:T(8,128)(2,1)} copy(bf16[1,256,2048]{2,1,0:T(8,128)(2,1)} %get-tuple-element.48) | data formatting | bytes 2097152
  (121 shorter events, 45.5 us)
Async XLA Ops:
  2.9 24.6 %collective-permute-start.5 = (bf16[256,1024]{1,0:T(8,128)(2,1)}, bf16[256,1024]{1,0:T(8,128)(2,1)}, u32[]{:S(2)}, u32[]{:S(2)}) collective-permute-start(bf16[256,1024]{1,0:T(8,128)(2,1)} %pad_maximum_fusion.1.refs_2_), channel_id=1, source_target_pairs={{0,4},{2,6},{4,8},{6,10},{8,12},{10,14},{1,5},{3,7},{5,9},{7,11},{... | collective-permute-start | bytes 1572872 | tf_op jit(solution)/shard_map/ppermute | solution.py:27
  11.9 21.7 %collective-permute-start.3 = (bf16[256,128]{1,0:T(8,128)(2,1)S(1)}, bf16[256,128]{1,0:T(8,128)(2,1)}, u32[]{:S(2)}, u32[]{:S(2)}) collective-permute-start(bf16[256,128]{1,0:T(8,128)(2,1)S(1)} %fusion), channel_id=1, source_target_pairs={{0,4},{2,6},{4,8},{6,10},{8,12},{10,14},{1,5},{3,7},{5,9},{7,11},{... | collective-permute-start | bytes 196616 | tf_op jit(solution)/shard_map/ppermute | solution.py:27
  15.3 42.2 %collective-permute-start.2 = (bf16[1,256,2048]{2,1,0:T(8,128)(2,1)}, bf16[1,256,2048]{2,1,0:T(8,128)(2,1)}, u32[]{:S(2)}, u32[]{:S(2)}) collective-permute-start(bf16[1,256,2048]{2,1,0:T(8,128)(2,1)} %param.13), channel_id=1, source_target_pairs={{0,16},{16,0},{1,17},{17,1},{2,18},{18,2},{3,19},{19,3},{4,20},{20... | collective-permute-start | bytes 3145736 | tf_op jit(solution)/shard_map/ppermute | solution.py:32
  15.4 16.5 %collective-permute-start = (bf16[256,1024]{1,0:T(8,128)(2,1)S(1)}, bf16[256,1024]{1,0:T(8,128)(2,1)S(1)}, u32[]{:S(2)}, u32[]{:S(2)}) collective-permute-start(bf16[256,1024]{1,0:T(8,128)(2,1)S(1)} %pad_maximum_fusion.refs_2_), channel_id=1, source_target_pairs={{0,4},{2,6},{4,8},{6,10},{8,12},{10,14},{1,5},{3,7},{5,9},{7,11},{... | collective-permute-start | bytes 1572872 | tf_op jit(solution)/shard_map/ppermute | solution.py:27
  27.6 29.1 %collective-permute-start.6 = (bf16[256,1024]{1,0:T(8,128)(2,1)S(1)}, bf16[256,1024]{1,0:T(8,128)(2,1)S(1)}, u32[]{:S(2)}, u32[]{:S(2)}) collective-permute-start(bf16[256,1024]{1,0:T(8,128)(2,1)S(1)} %broadcast_select_fusion), channel_id=1, source_target_pairs={{0,2},{2,0},{4,6},{6,4},{8,10},{10,8},{12,14},{14,12},{1,3},{3,1},... | collective-permute-start | bytes 1572872 | tf_op jit(solution)/shard_map/ppermute | solution.py:37
  32.0 34.6 %collective-permute-start.1 = (bf16[256,1024]{1,0:T(8,128)(2,1)S(1)}, bf16[256,1024]{1,0:T(8,128)(2,1)S(1)}, u32[]{:S(2)}, u32[]{:S(2)}) collective-permute-start(bf16[256,1024]{1,0:T(8,128)(2,1)S(1)} %broadcast_select_fusion.1), channel_id=1, source_target_pairs={{0,2},{2,0},{4,6},{6,4},{8,10},{10,8},{12,14},{14,12},{1,3},{3,1},... | collective-permute-start | bytes 1572872 | tf_op jit(solution)/shard_map/ppermute | solution.py:37
  33.6 21.6 %collective-permute-start.4 = (bf16[256,128]{1,0:T(8,128)(2,1)S(1)}, bf16[256,128]{1,0:T(8,128)(2,1)S(1)}, u32[]{:S(2)}, u32[]{:S(2)}) collective-permute-start(bf16[256,128]{1,0:T(8,128)(2,1)S(1)} %broadcast_select_fusion.2), channel_id=1, source_target_pairs={{0,2},{2,0},{4,6},{6,4},{8,10},{10,8},{12,14},{14,12},{1,3},{3,1},... | collective-permute-start | bytes 196616 | tf_op jit(solution)/shard_map/ppermute | solution.py:37
  77.1 6.4 %collective-permute-start.7 = (bf16[256,128]{1,0:T(8,128)(2,1)}, bf16[256,128]{1,0:T(8,128)(2,1)S(1)}, u32[]{:S(2)}, u32[]{:S(2)}) collective-permute-start(bf16[256,128]{1,0:T(8,128)(2,1)} %get-tuple-element.20), channel_id=1, source_target_pairs={{4,0},{6,2},{8,4},{10,6},{12,8},{14,10},{5,1},{7,3},{9,5},{11,7},{... | collective-permute-start | bytes 196616 | tf_op jit(solution)/shard_map/ppermute | solution.py:27
  78.4 6.4 %collective-permute-start.8 = (bf16[256,128]{1,0:T(8,128)(2,1)}, bf16[256,128]{1,0:T(8,128)(2,1)S(1)}, u32[]{:S(2)}, u32[]{:S(2)}) collective-permute-start(bf16[256,128]{1,0:T(8,128)(2,1)} %get-tuple-element.21), channel_id=1, source_target_pairs={{2,0},{4,2},{6,4},{8,6},{10,8},{12,10},{14,12},{3,1},{5,3},{7,5},{... | collective-permute-start | bytes 196616 | tf_op jit(solution)/shard_map/ppermute | solution.py:27
  93.1 7.0 %collective-permute-start.12 = (bf16[96,8,128]{2,1,0:T(8,128)(2,1)S(1)}, bf16[96,8,128]{2,1,0:T(8,128)(2,1)S(1)}, u32[]{:S(2)}, u32[]{:S(2)}) collective-permute-start(bf16[96,8,128]{2,1,0:T(8,128)(2,1)S(1)} %constant_dynamic-slice_fusion.1), channel_id=1, source_target_pairs={{0,1},{1,0},{2,3},{3,2},{4,5},{5,4},{6,7},{7,6},{8,9},{9,8},{10,11... | collective-permute-start | bytes 589832 | tf_op jit(solution)/shard_map/ppermute | solution.py:37
  94.7 8.1 %collective-permute-start.10 = (bf16[104,8,128]{2,1,0:T(8,128)(2,1)S(1)}, bf16[104,8,128]{2,1,0:T(8,128)(2,1)S(1)}, u32[]{:S(2)}, u32[]{:S(2)}) collective-permute-start(bf16[104,8,128]{2,1,0:T(8,128)(2,1)S(1)} %constant_dynamic-slice_fusion.3), channel_id=1, source_target_pairs={{0,2},{2,0},{4,6},{6,4},{8,10},{10,8},{12,14},{14,12},{1,3},{3,1},... | collective-permute-start | bytes 638984 | tf_op jit(solution)/shard_map/ppermute | solution.py:37
  100.2 5.3 %collective-permute-start.13 = (bf16[48,8,128]{2,1,0:T(8,128)(2,1)S(1)}, bf16[48,8,128]{2,1,0:T(8,128)(2,1)S(1)}, u32[]{:S(2)}, u32[]{:S(2)}) collective-permute-start(bf16[48,8,128]{2,1,0:T(8,128)(2,1)S(1)} %constant_dynamic-slice_fusion), channel_id=1, source_target_pairs={{0,2},{2,0},{4,6},{6,4},{8,10},{10,8},{12,14},{14,12},{1,3},{3,1},... | collective-permute-start | bytes 294920 | tf_op jit(solution)/shard_map/ppermute | solution.py:37
  102.9 4.8 %collective-permute-start.11 = (bf16[52,8,128]{2,1,0:T(8,128)(2,1)S(1)}, bf16[52,8,128]{2,1,0:T(8,128)(2,1)S(1)}, u32[]{:S(2)}, u32[]{:S(2)}) collective-permute-start(bf16[52,8,128]{2,1,0:T(8,128)(2,1)S(1)} %constant_dynamic-slice_fusion.2), channel_id=1, source_target_pairs={{0,1},{1,0},{2,3},{3,2},{4,5},{5,4},{6,7},{7,6},{8,9},{9,8},{10,11... | collective-permute-start | bytes 319496 | tf_op jit(solution)/shard_map/ppermute | solution.py:37
  107.8 5.9 %collective-permute-start.14 = (bf16[1,25,8,128]{3,2,1,0:T(8,128)(2,1)S(1)}, bf16[1,25,8,128]{3,2,1,0:T(8,128)(2,1)S(1)}, u32[]{:S(2)}, u32[]{:S(2)}) collective-permute-start(bf16[1,25,8,128]{3,2,1,0:T(8,128)(2,1)S(1)} %get-tuple-element.35), channel_id=1, source_target_pairs={{0,4},{2,6},{4,0},{6,2},{8,12},{10,14},{12,8},{14,10},{1,5},{3,7},... | collective-permute-start | bytes 153608 | tf_op jit(solution)/shard_map/ppermute | solution.py:37
  110.5 5.1 %collective-permute-start.15 = (bf16[1,25,8,128]{3,2,1,0:T(8,128)(2,1)S(1)}, bf16[1,25,8,128]{3,2,1,0:T(8,128)(2,1)S(1)}, u32[]{:S(2)}, u32[]{:S(2)}) collective-permute-start(bf16[1,25,8,128]{3,2,1,0:T(8,128)(2,1)S(1)} %get-tuple-element.36), channel_id=1, source_target_pairs={{0,8},{2,10},{4,12},{6,14},{8,0},{10,2},{12,4},{14,6},{1,9},{3,11}... | collective-permute-start | bytes 153608 | tf_op jit(solution)/shard_map/ppermute | solution.py:37
  110.5 6.0 %collective-permute-start.16 = (bf16[1,25,8,128]{3,2,1,0:T(8,128)(2,1)S(1)}, bf16[1,25,8,128]{3,2,1,0:T(8,128)(2,1)S(1)}, u32[]{:S(2)}, u32[]{:S(2)}) collective-permute-start(bf16[1,25,8,128]{3,2,1,0:T(8,128)(2,1)S(1)} %get-tuple-element.37), channel_id=1, source_target_pairs={{0,12},{2,14},{4,8},{6,10},{8,4},{10,6},{12,0},{14,2},{1,13},{3,15... | collective-permute-start | bytes 153608 | tf_op jit(solution)/shard_map/ppermute | solution.py:37
  116.5 4.5 %collective-permute-start.17 = (bf16[1,25,8,128]{3,2,1,0:T(8,128)(2,1)S(1)}, bf16[1,25,8,128]{3,2,1,0:T(8,128)(2,1)S(1)}, u32[]{:S(2)}, u32[]{:S(2)}) collective-permute-start(bf16[1,25,8,128]{3,2,1,0:T(8,128)(2,1)S(1)} %add_convert_fusion.5), channel_id=1, source_target_pairs={{0,4},{2,6},{4,0},{6,2},{8,12},{10,14},{12,8},{14,10},{1,5},{3,7},... | collective-permute-start | bytes 153608 | tf_op jit(solution)/shard_map/ppermute | solution.py:37
  117.3 5.0 %collective-permute-start.18 = (bf16[1,25,8,128]{3,2,1,0:T(8,128)(2,1)S(1)}, bf16[1,25,8,128]{3,2,1,0:T(8,128)(2,1)S(1)}, u32[]{:S(2)}, u32[]{:S(2)}) collective-permute-start(bf16[1,25,8,128]{3,2,1,0:T(8,128)(2,1)S(1)} %add_convert_fusion.5), channel_id=1, source_target_pairs={{0,8},{2,10},{4,12},{6,14},{8,0},{10,2},{12,4},{14,6},{1,9},{3,11}... | collective-permute-start | bytes 153608 | tf_op jit(solution)/shard_map/ppermute | solution.py:37
  119.6 5.9 %collective-permute-start.19 = (bf16[1,25,8,128]{3,2,1,0:T(8,128)(2,1)S(1)}, bf16[1,25,8,128]{3,2,1,0:T(8,128)(2,1)S(1)}, u32[]{:S(2)}, u32[]{:S(2)}) collective-permute-start(bf16[1,25,8,128]{3,2,1,0:T(8,128)(2,1)S(1)} %add_convert_fusion.5), channel_id=1, source_target_pairs={{0,12},{2,14},{4,8},{6,10},{8,4},{10,6},{12,0},{14,2},{1,13},{3,15... | collective-permute-start | bytes 153608 | tf_op jit(solution)/shard_map/ppermute | solution.py:37
  125.6 4.8 %collective-permute-start.20 = (bf16[52,8,128]{2,1,0:T(8,128)(2,1)S(1)}, bf16[52,8,128]{2,1,0:T(8,128)(2,1)S(1)}, u32[]{:S(2)}, u32[]{:S(2)}) collective-permute-start(bf16[52,8,128]{2,1,0:T(8,128)(2,1)S(1)} %bitcast.60), channel_id=1, source_target_pairs={{0,1},{1,0},{2,3},{3,2},{4,5},{5,4},{6,7},{7,6},{8,9},{9,8},{10,11... | collective-permute-start | bytes 319496 | tf_op jit(solution)/shard_map/ppermute | solution.py:37
  127.2 12.6 %collective-permute-start.26 = (bf16[256,2048]{1,0:T(8,128)(2,1)}, bf16[256,2048]{1,0:T(8,128)(2,1)S(1)}, u32[]{:S(2)}, u32[]{:S(2)}) collective-permute-start(bf16[256,2048]{1,0:T(8,128)(2,1)} %get-tuple-element.25), channel_id=1, source_target_pairs={{0,16},{16,0},{1,17},{17,1},{2,18},{18,2},{3,19},{19,3},{4,20},{20... | collective-permute-start | bytes 3145736 | tf_op jit(solution)/shard_map/ppermute | solution.py:32
  127.2 5.7 %collective-permute-start.22 = (bf16[48,8,128]{2,1,0:T(8,128)(2,1)S(1)}, bf16[48,8,128]{2,1,0:T(8,128)(2,1)S(1)}, u32[]{:S(2)}, u32[]{:S(2)}) collective-permute-start(bf16[48,8,128]{2,1,0:T(8,128)(2,1)S(1)} %bitcast.63), channel_id=1, source_target_pairs={{0,2},{2,0},{4,6},{6,4},{8,10},{10,8},{12,14},{14,12},{1,3},{3,1},... | collective-permute-start | bytes 294920 | tf_op jit(solution)/shard_map/ppermute | solution.py:37
  130.3 6.7 %collective-permute-start.21 = (bf16[104,8,128]{2,1,0:T(8,128)(2,1)S(1)}, bf16[104,8,128]{2,1,0:T(8,128)(2,1)S(1)}, u32[]{:S(2)}, u32[]{:S(2)}) collective-permute-start(bf16[104,8,128]{2,1,0:T(8,128)(2,1)S(1)} %pad_maximum_fusion.6), channel_id=1, source_target_pairs={{0,2},{2,0},{4,6},{6,4},{8,10},{10,8},{12,14},{14,12},{1,3},{3,1},... | collective-permute-start | bytes 638984 | tf_op jit(solution)/shard_map/ppermute | solution.py:37
  133.0 6.0 %collective-permute-start.23 = (bf16[96,8,128]{2,1,0:T(8,128)(2,1)S(1)}, bf16[96,8,128]{2,1,0:T(8,128)(2,1)S(1)}, u32[]{:S(2)}, u32[]{:S(2)}) collective-permute-start(bf16[96,8,128]{2,1,0:T(8,128)(2,1)S(1)} %pad_maximum_fusion.8), channel_id=1, source_target_pairs={{0,1},{1,0},{2,3},{3,2},{4,5},{5,4},{6,7},{7,6},{8,9},{9,8},{10,11... | collective-permute-start | bytes 589832 | tf_op jit(solution)/shard_map/ppermute | solution.py:37
  (20 other events, 107.7 us)

commit v4 on v3

--- a/solution.py
+++ b/solution.py
@@ -55,7 +55,11 @@
     return jnp.sum((doc_ends[None, :] <= positions[:, None]).astype(jnp.int32), axis=1)
 
 
-def attention_kernel(*refs, n_blocks, heads, tok, group, sub, chained, is_last):
+def in_vmem(value):
+    return pltpu.with_memory_space_constraint(value, pltpu.VMEM)
+
+
+def attention_kernel(*refs, n_blocks, piece, heads, tok, group, sub, chained, is_last):
     m_refs = refs[:n_blocks]
     q_ref, g_ref, spread_ref, up_ref, bias_ref, cos_ref, sin_ref = refs[n_blocks : n_blocks + 7]
     at = n_blocks + 7
@@ -67,6 +71,7 @@
         at += 3
     out_ref, u_ref, lg_ref = refs[at : at + 3]
     lg_low_refs = refs[at + 3 :]
+    first_head = piece * heads
     spread = spread_ref[...]
     span = spread.shape[0]
     half = spread.shape[1] // 2
@@ -76,8 +81,12 @@
     length = span - tok + sub
     subs = tok // sub
 
+    def lanes_of(query_head):
+        at = first_head * group + query_head
+        return slice(at * HD, (at + 1) * HD)
+
     def prepare(h):
-        shift = adapter_scale * jnp.dot(spread, up_ref[h], preferred_element_type=f32)
+        shift = adapter_scale * jnp.dot(spread, up_ref[first_head + h], preferred_element_type=f32)
         kc, vc = slice(h * HD, (h + 1) * HD), slice((heads + h) * HD, (heads + h + 1) * HD)
         key = jnp.concatenate([r[:, kc] for r in m_refs], axis=0).astype(f32) + shift[:, :HD]
         key = (key * cos + pltpu.roll(key, HD // 2, 1) * sin).astype(bf16)
@@ -90,7 +99,7 @@
         cq, sq = cos[span - tok + i * sub : span - tok + (i + 1) * sub], sin[span - tok + i * sub : span - tok + (i + 1) * sub]
         queries = []
         for j in range(group):
-            q = q_ref[cut, (h * group + j) * HD : (h * group + j + 1) * HD].astype(f32)
+            q = q_ref[cut, lanes_of(h * group + j)].astype(f32)
             q = q * cq + pltpu.roll(q, HD // 2, 1) * sq
             queries.append((q * (query_scale * log2e)).astype(bf16))
         q = jnp.concatenate(queries, axis=0)
@@ -108,7 +117,7 @@
         out = out_t.T
         gs = []
         for j in range(group):
-            lanes = slice((h * group + j) * HD, (h * group + j + 1) * HD)
+            lanes = lanes_of(h * group + j)
             out_ref[cut, lanes] = out[j * sub : (j + 1) * sub]
             gs.append(g_ref[cut, lanes])
         g_t = (jnp.concatenate(gs, axis=0).T.astype(f32) * scale).astype(bf16)
@@ -133,14 +142,15 @@
         dval = overlapped([p[1] for p in parts])
         dkey = dkey * cos - pltpu.roll(dkey, HD // 2, 1) * sin
         both = jnp.concatenate([dkey.astype(bf16), dval.astype(bf16)], axis=1)
-        lg = dot(both, up_ref[h], last)
+        lg = dot(both, up_ref[first_head + h], last)
         if h > 0:
             lg_ref[...] += lg
         else:
             lg_ref[...] = lg_in_ref[...] + lg if chained else lg
         u = adapter_scale * dot(spread, both, first)
-        u_ref[0, :, h * HD : (h + 1) * HD] = u[:half, :HD].astype(bf16)
-        u_ref[1, :, h * HD : (h + 1) * HD] = u[half:, HD:].astype(bf16)
+        head_lanes = slice((first_head + h) * HD, (first_head + h + 1) * HD)
+        u_ref[0, :, head_lanes] = u[:half, :HD].astype(bf16)
+        u_ref[1, :, head_lanes] = u[half:, HD:].astype(bf16)
 
     units = [(h, i) for h in range(heads) for i in range(subs)]
     prepared, scores, states, grads = {}, {}, {}, {}
@@ -173,37 +183,23 @@
     span = spread.shape[0]
     half = width // 2
     sub = HD if tok % HD == 0 else tok
-    whole = lambda shape: pl.BlockSpec(shape, lambda h: (0,) * len(shape))
-    any_space = pl.BlockSpec(memory_space=pl.ANY)
-    out_spec = pl.BlockSpec((tok, heads * group * HD), lambda i: (0, piece))
-    u_spec = pl.BlockSpec((2, half, heads * HD), lambda i: (0, 0, piece))
-    in_specs = (
-        [whole((tok, 2 * heads * HD))] * n_blocks
-        + [out_spec] * 2
-        + [
-            whole((span, width)),
-            pl.BlockSpec((heads, width, 2 * HD), lambda i: (piece, 0, 0)),
-            whole((span, tok)),
-            whole((span, HD)),
-            whole((span, HD)),
-        ]
-    )
-    extra, aliases = [], {}
+    operands = [*blocks, q_rows, g_rows, spread, up_cat, bias, cos, sin]
+    aliases = {}
     is_last = mask is not None
     if is_last:
-        extra = [mask]
-        in_specs = in_specs + [whole((span, width))]
+        operands.append(mask)
     if carried is not None:
         out, u, lg = carried
-        at = len(in_specs)
-        extra, aliases = extra + [lg, out, u], {at + 1: 0, at + 2: 1}
-        in_specs = in_specs + [whole((span, width)), any_space, any_space]
+        at = len(operands)
+        operands += [lg, out, u]
+        aliases = {at: 2, at + 1: 0, at + 2: 1}
     low_count = n_blocks - 1 if is_last else 0
     work = heads * group * tok * (span - tok + sub) * HD * 2 * 6
     return pl.pallas_call(
         partial(
             attention_kernel,
             n_blocks=n_blocks,
+            piece=piece,
             heads=heads,
             tok=tok,
             group=group,
@@ -211,28 +207,35 @@
             chained=carried is not None,
             is_last=is_last,
         ),
-        grid=(1,),
-        in_specs=in_specs,
-        out_specs=[out_spec, u_spec, whole((span, width))] + [whole((tok, width))] * low_count,
+        in_specs=[pl.BlockSpec(memory_space=pltpu.VMEM)] * len(operands),
+        out_specs=[pl.BlockSpec(memory_space=pltpu.VMEM)] * (3 + low_count),
         out_shape=[
-            jax.ShapeDtypeStruct(q_rows.shape, bf16),
-            jax.ShapeDtypeStruct((2, half, kv_heads * HD), bf16),
-            jax.ShapeDtypeStruct((span, width), f32),
+            pltpu.VMEM(q_rows.shape, bf16),
+            pltpu.VMEM((2, half, kv_heads * HD), bf16),
+            pltpu.VMEM((span, width), f32),
         ]
-        + [jax.ShapeDtypeStruct((tok, width), bf16)] * low_count,
+        + [pltpu.VMEM((tok, width), bf16)] * low_count,
         input_output_aliases=aliases,
-        compiler_params=pltpu.CompilerParams(dimension_semantics=("arbitrary",)),
+        compiler_params=pltpu.CompilerParams(vmem_limit_bytes=28 << 20),
         cost_estimate=pl.CostEstimate(flops=work, transcendentals=0, bytes_accessed=heads * tok * HD * 20),
         name="attention",
-    )(*blocks, q_rows, g_rows, spread, up_cat, bias, cos, sin, *extra)
-
-
-def product_kernel(*refs, n_recv, cols, up_cols):
+    )(*[in_vmem(x) for x in operands])
+
+
+def product_kernel(*refs, n_recv, tok, cols, up_cols, chunk):
     side_ref, lg_ref = refs[:2]
     recv = refs[2 : 2 + n_recv]
-    hidden_ref, up_ref, keep_ref, send_ref = refs[2 + n_recv :]
+    up_ref, hidden_hbm, handed_hbm, keep_ref, send_ref, handed_out, hidden_ref, sems = refs[2 + n_recv :]
+    loads = []
+    for k, c in enumerate(range(0, cols, chunk)):
+        lanes = slice(c * HD, min(c + chunk, cols) * HD)
+        loads.append(pltpu.make_async_copy(hidden_hbm.at[:, lanes], hidden_ref.at[:, lanes], sems.at[k]))
+    handing = pltpu.make_async_copy(handed_hbm, handed_out, sems.at[len(loads)])
+    for load in loads:
+        load.start()
+    handing.start()
     side = side_ref[0]
-    total = lg_ref[...]
+    total = lg_ref[lg_ref.shape[0] - tok :]
     for r in recv:
         total = total + r[...].astype(f32)
     width = total.shape[1]
@@ -240,8 +243,20 @@
     total = jnp.where(side == 0, total, pltpu.roll(total, half, 1)).astype(bf16)
     per_row = cols + up_cols
     rows = half // SUB
-    step = 2 if cols % 2 == 0 else 1
+    for h in range(up_cols):
+        for r in range(rows):
+            where = (slice(r * SUB, (r + 1) * SUB), slice(h * HD, (h + 1) * HD))
+            keep_ref[r * per_row + cols + h] = up_ref[(side,) + where]
+            send_ref[r * per_row + cols + h] = up_ref[(1 - side,) + where]
+    used = rows * per_row
+    if keep_ref.shape[0] > used:
+        rest = keep_ref.shape[0] - used
+        keep_ref[pl.ds(used, rest)] = jnp.zeros((rest, SUB, HD), bf16)
+        send_ref[pl.ds(used, rest)] = jnp.zeros((rest, SUB, HD), bf16)
+    step = 2 if cols % 2 == 0 and chunk % 2 == 0 else 1
     for c in range(0, cols, step):
+        if c % chunk == 0:
+            loads[c // chunk].wait()
         w = lax.dot_general(
             total,
             hidden_ref[:, c * HD : (c + step) * HD],
@@ -253,27 +268,20 @@
                 tile = w[:, j * HD : (j + 1) * HD]
                 keep_ref[r * per_row + c + j] = tile[r * SUB : (r + 1) * SUB]
                 send_ref[r * per_row + c + j] = tile[half + r * SUB : half + (r + 1) * SUB]
-    for h in range(up_cols):
-        for r in range(rows):
-            where = (slice(r * SUB, (r + 1) * SUB), slice(h * HD, (h + 1) * HD))
-            keep_ref[r * per_row + cols + h] = up_ref[(side,) + where]
-            send_ref[r * per_row + cols + h] = up_ref[(1 - side,) + where]
-    used = rows * per_row
-    if keep_ref.shape[0] > used:
-        rest = keep_ref.shape[0] - used
-        keep_ref[pl.ds(used, rest)] = jnp.zeros((rest, SUB, HD), bf16)
-        send_ref[pl.ds(used, rest)] = jnp.zeros((rest, SUB, HD), bf16)
+    handing.wait()
 
 
 def assemble_kernel(
-    scalars_ref, ma_ref, mb_ref, ra_ref, rb_ref, handed_ref, w_ref, u_ref, same_ref, *, cols, rows
+    scalars_ref, ma_ref, mb_ref, ra_ref, rb_ref, w_hbm, u_hbm, w_ref, u_ref, sems, *, cols, rows
 ):
     side, me_a, me_b = scalars_ref[0], scalars_ref[1], scalars_ref[2]
     n_a, a = ma_ref.shape[:2]
     b = mb_ref.shape[1]
     up_cols = u_ref.shape[1] // HD
     per_row = cols + up_cols
+    stores = []
     for r in range(rows):
+        starts = [pl.multiple_of((m * rows + r) * SUB, SUB) for m in (side, 1 - side)]
         for c in range(per_row):
             t = r * per_row + c
             if t < n_a * a:
@@ -281,13 +289,20 @@
             else:
                 t -= n_a * a
                 mine, theirs, piece, off = mb_ref, rb_ref, (t // b) ^ me_b, t % b
-            for src, m in ((mine, side), (theirs, 1 - side)):
-                at = pl.multiple_of((m * rows + r) * SUB, SUB)
+            for src, at in zip((mine, theirs), starts):
                 tile = src[piece, off].astype(f32)
                 if c < cols:
                     w_ref[pl.ds(at, SUB), c * HD : (c + 1) * HD] = tile
                 else:
                     u_ref[pl.ds(at, SUB), (c - cols) * HD : (c - cols + 1) * HD] = tile
+        for at in starts:
+            band = pl.ds(at, SUB)
+            stores.append(pltpu.make_async_copy(w_ref.at[band], w_hbm.at[band], sems.at[len(stores)]))
+            stores[-1].start()
+    stores.append(pltpu.make_async_copy(u_ref, u_hbm, sems.at[len(stores)]))
+    stores[-1].start()
+    for store in stores:
+        store.wait()
 
 
 def axis_bits(axis):
@@ -340,7 +355,7 @@
     return jnp.concatenate([tiles, permute_xor(tiles, *stage)], axis=0)
 
 
-def body(
+def step(
     hidden,
     frozen_query_rows,
     frozen_key_rows,
@@ -444,16 +459,28 @@
     side = lax.axis_index("section").astype(jnp.int32)
     smem = pl.BlockSpec(memory_space=pltpu.SMEM)
     vmem = pl.BlockSpec(memory_space=pltpu.VMEM)
-    keep, send = pl.pallas_call(
+    any_space = pl.BlockSpec(memory_space=pl.ANY)
+    chunk = -(-cols // 6)
+    chunk += chunk % 2
+    tile_shape = (units * group, SUB, HD)
+    keep, send, handed = pl.pallas_call(
         partial(
-            product_kernel, n_recv=len(received), cols=cols, up_cols=up_cols
+            product_kernel, n_recv=len(received), tok=tok, cols=cols, up_cols=up_cols, chunk=chunk
         ),
-        in_specs=[smem] + [pl.BlockSpec((tok, width), lambda i: (2 * steps, 0))] + [vmem] * (2 + len(received)),
-        grid=(1,),
-        out_specs=[vmem, vmem],
-        out_shape=[jax.ShapeDtypeStruct((units * group, SUB, HD), bf16)] * 2,
+        in_specs=[smem] + [vmem] * (2 + len(received)) + [any_space] * 2,
+        out_specs=[vmem, vmem, any_space],
+        out_shape=[
+            pltpu.VMEM(tile_shape, bf16),
+            pltpu.VMEM(tile_shape, bf16),
+            jax.ShapeDtypeStruct(handed.shape, bf16),
+        ],
+        scratch_shapes=[
+            pltpu.VMEM((tok, model_width), bf16),
+            pltpu.SemaphoreType.DMA((-(-cols // chunk) + 1,)),
+        ],
+        compiler_params=pltpu.CompilerParams(vmem_limit_bytes=16 << 20),
         name="product",
-    )(side[None], lg, *received, hidden[0], ups)
+    )(side[None], in_vmem(lg), *[in_vmem(r) for r in received], in_vmem(ups), hidden[0], handed)
     recv = permute_cyclic(send, "section", 1)
     tiles = (keep.astype(f32) + recv.astype(f32)).astype(bf16)
     colours = [tiles[: a * group], tiles[a * group :]]
@@ -485,25 +512,27 @@
         colours = [gather_stage(colours[c], other[c][k]) for c in range(2)]
     theirs = [permute_cyclic(t, "section", 1) for t in colours]
     shapes = [(group, a, SUB, HD), (group, b, SUB, HD)]
-    any_space = pl.BlockSpec(memory_space=pl.ANY)
-    w, u, handed = pl.pallas_call(
+    w, u = pl.pallas_call(
         partial(assemble_kernel, cols=cols, rows=rows),
-        in_specs=[smem] + [vmem] * 4 + [any_space],
-        out_specs=[vmem, vmem, any_space],
-        input_output_aliases={5: 2},
+        in_specs=[smem] + [vmem] * 4,
+        out_specs=[any_space, any_space],
         out_shape=[
             jax.ShapeDtypeStruct((width, model_width), f32),
             jax.ShapeDtypeStruct((width, kv_width), f32),
-            jax.ShapeDtypeStruct(handed.shape, bf16),
         ],
+        scratch_shapes=[
+            pltpu.VMEM((width, model_width), f32),
+            pltpu.VMEM((width, kv_width), f32),
+            pltpu.SemaphoreType.DMA((2 * rows + 1,)),
+        ],
+        compiler_params=pltpu.CompilerParams(vmem_limit_bytes=16 << 20),
         name="assemble",
     )(
         jnp.stack([side, ids[0], ids[1]]),
-        colours[0].reshape(shapes[0]),
-        colours[1].reshape(shapes[1]),
-        theirs[0].reshape(shapes[0]),
-        theirs[1].reshape(shapes[1]),
-        handed,
+        in_vmem(colours[0].reshape(shapes[0])),
+        in_vmem(colours[1].reshape(shapes[1])),
+        in_vmem(theirs[0].reshape(shapes[0])),
+        in_vmem(theirs[1].reshape(shapes[1])),
     )
     down_map_gradient = w.T.reshape(model_width, 2, adapters, rank)
     up_map_gradient = u.reshape(2, adapters, rank, kv_width)
@@ -512,7 +541,7 @@
 
 def solution(mesh):
     return jax.shard_map(
-        body,
+        step,
         mesh=mesh,
         in_specs=(
             P(("section", "dp"), "ctx", None),

time: 147 us -> 140 us (0.952)
  other arithmetic: 13.3 us -> 8.42 us
  Pallas kernels: 25.9 us -> 21.7 us
  local copies, waits for them, and re-layouts: 8.39 us -> 9.95 us
    pallas_call x4, Pallas kernels: 25.9 us -> 21.7 us  [the longest x2 16.6 us: attention(): pl.pallas_call(partial(attention_kernel, n_blocks=n_blocks, piece=piece,...]
    ppermute x17, waiting for transfers between devices: 42 us -> 39.2 us  [permute_xor(): return lax.ppermute(value, axis, [(i, i ^ bit) for i in range(count)])]
    concatenate x6, other arithmetic: 4.48 us -> 2.11 us  [the longest x2 0.92 us: step(): own = jnp.concatenate([keys[:, cut], vals[:, cut]], axis=1)]
    ppermute x5, waiting for transfers between devices: 6.69 us -> 8.98 us  [permute_by(): lax.ppermute(value, axis, [(i, i + steps) for i in range(first, last)])]
    select_n x3, other arithmetic: 2.41 us -> 0.54 us  [the longest x1 0.37 us: step(): bias = jnp.where(allowed, 0.0, masked_score).astype(f32)]
    unnamed x36 -> x43, local copies, waits for them, and re-layouts: 5.59 us -> 7.1 us
  transfers between devices with their start and end apart: 27 -> 27, of which waited for: 18 -> 17; matrix products, arithmetic and copies ran while one was open for 11% -> 8% of each run, Pallas kernels for 6% -> 6%
where the time goes in v4:
time: 140 us; the launch traced here: 139 us
  waiting for transfers between devices  52.4 us (37%)
  starting transfers between devices  43 us (31%)
  Pallas kernels  21.7 us (16%)
  local copies, waits for them, and re-layouts  9.95 us (7%)
  other arithmetic  8.42 us (6%)
  matrix products  2.65 us (2%)
    ppermute x17, waiting for transfers between devices, permute_xor(): return lax.ppermute(value, axis, [(i, i ^ bit) for i in range(count)])  39.2 us
    ppermute x17, starting transfers between devices, permute_xor(): return lax.ppermute(value, axis, [(i, i ^ bit) for i in range(count)])  28 us
    pallas_call x2, Pallas kernels, attention(): pl.pallas_call(partial(attention_kernel, n_blocks=n_blocks, piece=piece,...  16.6 us
    ppermute x5, starting transfers between devices, permute_by(): lax.ppermute(value, axis, [(i, i + steps) for i in range(first, last)])  14.7 us
    ppermute x5, waiting for transfers between devices, permute_by(): lax.ppermute(value, axis, [(i, i + steps) for i in range(first, last)])  8.98 us
    unnamed x43, local copies, waits for them, and re-layouts  7.1 us
    ppermute x5, waiting for transfers between devices, permute_cyclic(): lax.ppermute(value, axis, [(i, (i + by) % count) for i in range(count)])  4.18 us
  transfers between devices with their start and end apart: 27, of which 17 were waited for; matrix products, arithmetic and copies ran while one was open for 8% of the time, Pallas kernels for 6%

profile of v4, /device:TPU:0, one launch (start us, length us, event | category | flops | bytes accessed | tf_op | source)
XLA Modules:
  0.0 139.4 jit_solution(1038910935176970919)
XLA Ops:
  3.6 5.7 %collective-permute-start.5 = (bf16[256,1024]{1,0:T(8,128)(2,1)}, bf16[256,1024]{1,0:T(8,128)(2,1)}, u32[]{:S(2)}, u32[]{:S(2)}) collective-permute-start(bf16[256,1024]{1,0:T(8,128)(2,1)} %pad_maximum_fusion.1.refs_2_), channel_id=1, source_target_pairs={{0,4},{2,6},{4,8},{6,10},{8,12},{10,14},{1,5},{3,7},{5,9},{7,11},{... | collective-permute-start | bytes 1572872 | tf_op jit(solution)/shard_map/ppermute | solution.py:27
  10.0 2.6 %fusion = bf16[256,128]{1,0:T(8,128)(2,1)S(1)} fusion(bf16[5376,128]{0,1:T(8,128)(2,1)S(1)} %bitcast.49, s32[128]{0:T(128)S(1)} %and_select_fusion, s32[256]{0:T(256)S(1)} %slice.42, bf16[1,256,5376]{2,1,0:T(8,128)(2,1)} %param.9), kind=kOutput, calls=%fused_computation.4 | convolution fusion | flops 352419840 | bytes 4195840 | tf_op jit(solution)/shard_map/dot_general | solution.py:413
  12.6 3.3 %collective-permute-start.3 = (bf16[256,128]{1,0:T(8,128)(2,1)S(1)}, bf16[256,128]{1,0:T(8,128)(2,1)}, u32[]{:S(2)}, u32[]{:S(2)}) collective-permute-start(bf16[256,128]{1,0:T(8,128)(2,1)S(1)} %fusion), channel_id=1, source_target_pairs={{0,4},{2,6},{4,8},{6,10},{8,12},{10,14},{1,5},{3,7},{5,9},{7,11},{... | collective-permute-start | bytes 196616 | tf_op jit(solution)/shard_map/ppermute | solution.py:27
  16.1 3.0 %collective-permute-start = (bf16[256,1024]{1,0:T(8,128)(2,1)S(1)}, bf16[256,1024]{1,0:T(8,128)(2,1)S(1)}, u32[]{:S(2)}, u32[]{:S(2)}) collective-permute-start(bf16[256,1024]{1,0:T(8,128)(2,1)S(1)} %pad_maximum_fusion.refs_2_), channel_id=1, source_target_pairs={{0,4},{2,6},{4,8},{6,10},{8,12},{10,14},{1,5},{3,7},{5,9},{7,11},{... | collective-permute-start | bytes 1572872 | tf_op jit(solution)/shard_map/ppermute | solution.py:27
  22.4 2.0 %fusion.8 = (f32[768,64]{1,0:T(8,128)S(1)}, f32[768,64]{1,0:T(8,128)S(1)}, f32[768,64]{1,0:T(8,128)S(1)}) fusion(f32[64]{0:T(128)} %multiply_power_fusion, f32[768]{0:T(1024)S(1)} %convert_element_type.99), kind=kLoop, calls=%fused_computation.44 | loop fusion | flops 98304 | bytes 593152 | tf_op jit(solution)/shard_map/neg | solution.py:411
  26.1 2.6 %collective-permute-start.6 = (bf16[256,1024]{1,0:T(8,128)(2,1)S(1)}, bf16[256,1024]{1,0:T(8,128)(2,1)S(1)}, u32[]{:S(2)}, u32[]{:S(2)}) collective-permute-start(bf16[256,1024]{1,0:T(8,128)(2,1)S(1)} %broadcast_select_fusion), channel_id=1, source_target_pairs={{0,2},{2,0},{4,6},{6,4},{8,10},{10,8},{12,14},{14,12},{1,3},{3,1},... | collective-permute-start | bytes 1572872 | tf_op jit(solution)/shard_map/ppermute | solution.py:37
  28.7 3.9 %collective-permute-done.refs_0_ = bf16[256,1024]{1,0:T(8,128)(2,1)S(1)} collective-permute-done((bf16[256,1024]{1,0:T(8,128)(2,1)S(1)}, bf16[256,1024]{1,0:T(8,128)(2,1)S(1)}, u32[]{:S(2)}, u32[]{:S(2)}) %collective-permute-start) | collective-permute-done | bytes 524320 | tf_op jit(solution)/shard_map/ppermute | solution.py:27
  35.8 17.8 %collective-permute-done.4 = bf16[256,128]{1,0:T(8,128)(2,1)S(1)} collective-permute-done((bf16[256,128]{1,0:T(8,128)(2,1)S(1)}, bf16[256,128]{1,0:T(8,128)(2,1)S(1)}, u32[]{:S(2)}, u32[]{:S(2)}) %collective-permute-start.4) | collective-permute-done | bytes 65568 | tf_op jit(solution)/shard_map/ppermute | solution.py:37
  56.7 8.2 %attention.2 = (bf16[256,2048]{1,0:T(8,128)(2,1)}, bf16[2,64,1024]{2,1,0:T(8,128)(2,1)S(1)}, f32[768,128]{1,0:T(8,128)S(1)}) custom-call(bf16[256,1024]{1,0:T(8,128)(2,1)} %collective-permute-done.5.refs_0_, bf16[256,1024]{1,0:T(8,128)(2,1)S(1)} %collective-permute-done.6.refs_1_, bf16[256,1024]{1,0:T(8,128)(2,1)} %pad_maximum_fusion.1.refs_2_, ...), custom_call_target="tpu_custom_call" | custom-call | flops 2013265920 | bytes 2621440 | tf_op jit(solution)/shard_map/attention/pallas_call | solution.py:198
  64.9 8.4 %attention.3 = (bf16[256,2048]{1,0:T(8,128)(2,1)}, bf16[2,64,1024]{2,1,0:T(8,128)(2,1)S(1)}, f32[768,128]{1,0:T(8,128)S(1)}, bf16[256,128]{1,0:T(8,128)(2,1)S(1)}, bf16[256,128]{1,0:T(8,128)(2,1)S(1)}) custom-call(bf16[256,1024]{1,0:T(8,128)(2,1)S(1)} %collective-permute-done.refs_0_, ...), custom_call_target="tpu_custom_call", output_to_operand_aliasing={{2}: (11, {}), {0}: (12, {}), {1}: (13, {})} | custom-call | flops 2013265920 | bytes 2621440 | tf_op jit(solution)/shard_map/attention/pallas_call | solution.py:198
  76.0 3.8 %collective-permute-done.7.refs_2_ = bf16[256,128]{1,0:T(8,128)(2,1)S(1)} collective-permute-done((bf16[256,128]{1,0:T(8,128)(2,1)S(1)}, bf16[256,128]{1,0:T(8,128)(2,1)S(1)}, u32[]{:S(2)}, u32[]{:S(2)}) %collective-permute-start.7) | collective-permute-done | bytes 65568 | tf_op jit(solution)/shard_map/ppermute | solution.py:27
  82.8 2.6 %product.1 = (bf16[400,8,128]{2,1,0:T(8,128)(2,1)S(1)}, bf16[400,8,128]{2,1,0:T(8,128)(2,1)}, bf16[1,256,2048]{2,1,0:T(8,128)(2,1)}) custom-call(s32[1]{0:T(128)} %bitcast.refs_0_, f32[768,128]{1,0:T(8,128)S(1)} %get-tuple-element.19.refs_1_, bf16[256,128]{1,0:T(8,128)(2,1)S(1)} %collective-permute-done.7.refs_2_, ...), custom_call_target="tpu_custom_call" | custom-call | tf_op jit(solution)/shard_map/product/pallas_call | solution.py:466
  86.4 2.5 %collective-permute-done.10 = bf16[400,8,128]{2,1,0:T(8,128)(2,1)S(1)} collective-permute-done((bf16[400,8,128]{2,1,0:T(8,128)(2,1)}, bf16[400,8,128]{2,1,0:T(8,128)(2,1)S(1)}, u32[]{:S(2)}, u32[]{:S(2)}) %collective-permute-start.10) | collective-permute-done | bytes 819232 | tf_op jit(solution)/shard_map/ppermute | solution.py:32
  92.0 2.7 %collective-permute-start.11 = (bf16[104,8,128]{2,1,0:T(8,128)(2,1)S(1)}, bf16[104,8,128]{2,1,0:T(8,128)(2,1)S(1)}, u32[]{:S(2)}, u32[]{:S(2)}) collective-permute-start(bf16[104,8,128]{2,1,0:T(8,128)(2,1)S(1)} %constant_dynamic-slice_fusion.3), channel_id=1, source_target_pairs={{0,2},{2,0},{4,6},{6,4},{8,10},{10,8},{12,14},{14,12},{1,3},{3,1},... | collective-permute-start | bytes 638984 | tf_op jit(solution)/shard_map/ppermute | solution.py:37
  94.7 2.7 %collective-permute-done.13 = bf16[96,8,128]{2,1,0:T(8,128)(2,1)S(1)} collective-permute-done((bf16[96,8,128]{2,1,0:T(8,128)(2,1)S(1)}, bf16[96,8,128]{2,1,0:T(8,128)(2,1)S(1)}, u32[]{:S(2)}, u32[]{:S(2)}) %collective-permute-start.13) | collective-permute-done | bytes 196640 | tf_op jit(solution)/shard_map/ppermute | solution.py:37
  97.4 2.7 %collective-permute-start.14 = (bf16[48,8,128]{2,1,0:T(8,128)(2,1)S(1)}, bf16[48,8,128]{2,1,0:T(8,128)(2,1)S(1)}, u32[]{:S(2)}, u32[]{:S(2)}) collective-permute-start(bf16[48,8,128]{2,1,0:T(8,128)(2,1)S(1)} %constant_dynamic-slice_fusion), channel_id=1, source_target_pairs={{0,2},{2,0},{4,6},{6,4},{8,10},{10,8},{12,14},{14,12},{1,3},{3,1},... | collective-permute-start | bytes 294920 | tf_op jit(solution)/shard_map/ppermute | solution.py:37
  102.7 2.2 %collective-permute-done.12 = bf16[52,8,128]{2,1,0:T(8,128)(2,1)S(1)} collective-permute-done((bf16[52,8,128]{2,1,0:T(8,128)(2,1)S(1)}, bf16[52,8,128]{2,1,0:T(8,128)(2,1)S(1)}, u32[]{:S(2)}, u32[]{:S(2)}) %collective-permute-start.12) | collective-permute-done | bytes 106528 | tf_op jit(solution)/shard_map/ppermute | solution.py:37
  105.0 2.5 %collective-permute-start.15 = (bf16[1,25,8,128]{3,2,1,0:T(8,128)(2,1)S(1)}, bf16[1,25,8,128]{3,2,1,0:T(8,128)(2,1)S(1)}, u32[]{:S(2)}, u32[]{:S(2)}) collective-permute-start(bf16[1,25,8,128]{3,2,1,0:T(8,128)(2,1)S(1)} %get-tuple-element.35), channel_id=1, source_target_pairs={{0,4},{2,6},{4,0},{6,2},{8,12},{10,14},{12,8},{14,10},{1,5},{3,7},... | collective-permute-start | bytes 153608 | tf_op jit(solution)/shard_map/ppermute | solution.py:37
  107.5 2.4 %collective-permute-start.17 = (bf16[1,25,8,128]{3,2,1,0:T(8,128)(2,1)S(1)}, bf16[1,25,8,128]{3,2,1,0:T(8,128)(2,1)S(1)}, u32[]{:S(2)}, u32[]{:S(2)}) collective-permute-start(bf16[1,25,8,128]{3,2,1,0:T(8,128)(2,1)S(1)} %get-tuple-element.37), channel_id=1, source_target_pairs={{0,12},{2,14},{4,8},{6,10},{8,4},{10,6},{12,0},{14,2},{1,13},{3,15... | collective-permute-start | bytes 153608 | tf_op jit(solution)/shard_map/ppermute | solution.py:37
  114.3 2.3 %collective-permute-start.19 = (bf16[1,25,8,128]{3,2,1,0:T(8,128)(2,1)S(1)}, bf16[1,25,8,128]{3,2,1,0:T(8,128)(2,1)S(1)}, u32[]{:S(2)}, u32[]{:S(2)}) collective-permute-start(bf16[1,25,8,128]{3,2,1,0:T(8,128)(2,1)S(1)} %add_convert_fusion.5), channel_id=1, source_target_pairs={{0,8},{2,10},{4,12},{6,14},{8,0},{10,2},{12,4},{14,6},{1,9},{3,11}... | collective-permute-start | bytes 153608 | tf_op jit(solution)/shard_map/ppermute | solution.py:37
  119.4 3.2 %collective-permute-done.20 = bf16[1,25,8,128]{3,2,1,0:T(8,128)(2,1)S(1)} collective-permute-done((bf16[1,25,8,128]{3,2,1,0:T(8,128)(2,1)S(1)}, bf16[1,25,8,128]{3,2,1,0:T(8,128)(2,1)S(1)}, u32[]{:S(2)}, u32[]{:S(2)}) %collective-permute-start.20) | collective-permute-done | bytes 51232 | tf_op jit(solution)/shard_map/ppermute | solution.py:37
  124.8 3.6 %collective-permute-done.21 = bf16[52,8,128]{2,1,0:T(8,128)(2,1)S(1)} collective-permute-done((bf16[52,8,128]{2,1,0:T(8,128)(2,1)S(1)}, bf16[52,8,128]{2,1,0:T(8,128)(2,1)S(1)}, u32[]{:S(2)}, u32[]{:S(2)}) %collective-permute-start.21) | collective-permute-done | bytes 106528 | tf_op jit(solution)/shard_map/ppermute | solution.py:37
  130.8 3.6 %collective-permute-done.22 = bf16[104,8,128]{2,1,0:T(8,128)(2,1)S(1)} collective-permute-done((bf16[104,8,128]{2,1,0:T(8,128)(2,1)S(1)}, bf16[104,8,128]{2,1,0:T(8,128)(2,1)S(1)}, u32[]{:S(2)}, u32[]{:S(2)}) %collective-permute-start.22) | collective-permute-done | bytes 213024 | tf_op jit(solution)/shard_map/ppermute | solution.py:37
  136.8 2.4 %assemble.1 = (f32[128,5376]{1,0:T(8,128)}, f32[128,1024]{1,0:T(8,128)}) custom-call(s32[3]{0:T(128)S(1)} %pad_add_fusion.1.scalars_ref, bf16[16,13,8,128]{3,2,1,0:T(8,128)(2,1)S(1)} %bitcast.51, bf16[16,12,8,128]{3,2,1,0:T(8,128)(2,1)S(1)} %bitcast.52, bf16[16,13,8,128]{3,2,1,0:T(8,128)(2,1)S(1)} %bitcast.58, bf16[16,12,8,128]{3,2,1,0:T(8,128)(2,1)S(1)} %bitcast.59), custom_call_target="tpu_custom_call" | custom-call | tf_op jit(solution)/shard_map/assemble/pallas_call | solution.py:515
  (128 shorter events, 41.2 us)
Async XLA Ops:
  3.6 21.8 %collective-permute-start.5 = (bf16[256,1024]{1,0:T(8,128)(2,1)}, bf16[256,1024]{1,0:T(8,128)(2,1)}, u32[]{:S(2)}, u32[]{:S(2)}) collective-permute-start(bf16[256,1024]{1,0:T(8,128)(2,1)} %pad_maximum_fusion.1.refs_2_), channel_id=1, source_target_pairs={{0,4},{2,6},{4,8},{6,10},{8,12},{10,14},{1,5},{3,7},{5,9},{7,11},{... | collective-permute-start | bytes 1572872 | tf_op jit(solution)/shard_map/ppermute | solution.py:27
  12.6 21.7 %collective-permute-start.3 = (bf16[256,128]{1,0:T(8,128)(2,1)S(1)}, bf16[256,128]{1,0:T(8,128)(2,1)}, u32[]{:S(2)}, u32[]{:S(2)}) collective-permute-start(bf16[256,128]{1,0:T(8,128)(2,1)S(1)} %fusion), channel_id=1, source_target_pairs={{0,4},{2,6},{4,8},{6,10},{8,12},{10,14},{1,5},{3,7},{5,9},{7,11},{... | collective-permute-start | bytes 196616 | tf_op jit(solution)/shard_map/ppermute | solution.py:27
  16.0 38.5 %collective-permute-start.2 = (bf16[1,256,2048]{2,1,0:T(8,128)(2,1)}, bf16[1,256,2048]{2,1,0:T(8,128)(2,1)S(1)}, u32[]{:S(2)}, u32[]{:S(2)}) collective-permute-start(bf16[1,256,2048]{2,1,0:T(8,128)(2,1)} %param.13), channel_id=1, source_target_pairs={{0,16},{16,0},{1,17},{17,1},{2,18},{18,2},{3,19},{19,3},{4,20},{20... | collective-permute-start | bytes 3145736 | tf_op jit(solution)/shard_map/ppermute | solution.py:32
  16.1 16.5 %collective-permute-start = (bf16[256,1024]{1,0:T(8,128)(2,1)S(1)}, bf16[256,1024]{1,0:T(8,128)(2,1)S(1)}, u32[]{:S(2)}, u32[]{:S(2)}) collective-permute-start(bf16[256,1024]{1,0:T(8,128)(2,1)S(1)} %pad_maximum_fusion.refs_2_), channel_id=1, source_target_pairs={{0,4},{2,6},{4,8},{6,10},{8,12},{10,14},{1,5},{3,7},{5,9},{7,11},{... | collective-permute-start | bytes 1572872 | tf_op jit(solution)/shard_map/ppermute | solution.py:27
  26.1 28.4 %collective-permute-start.6 = (bf16[256,1024]{1,0:T(8,128)(2,1)S(1)}, bf16[256,1024]{1,0:T(8,128)(2,1)S(1)}, u32[]{:S(2)}, u32[]{:S(2)}) collective-permute-start(bf16[256,1024]{1,0:T(8,128)(2,1)S(1)} %broadcast_select_fusion), channel_id=1, source_target_pairs={{0,2},{2,0},{4,6},{6,4},{8,10},{10,8},{12,14},{14,12},{1,3},{3,1},... | collective-permute-start | bytes 1572872 | tf_op jit(solution)/shard_map/ppermute | solution.py:37
  32.8 32.2 %collective-permute-start.1 = (bf16[256,1024]{1,0:T(8,128)(2,1)S(1)}, bf16[256,1024]{1,0:T(8,128)(2,1)S(1)}, u32[]{:S(2)}, u32[]{:S(2)}) collective-permute-start(bf16[256,1024]{1,0:T(8,128)(2,1)S(1)} %broadcast_select_fusion.1), channel_id=1, source_target_pairs={{0,2},{2,0},{4,6},{6,4},{8,10},{10,8},{12,14},{14,12},{1,3},{3,1},... | collective-permute-start | bytes 1572872 | tf_op jit(solution)/shard_map/ppermute | solution.py:37
  34.3 19.3 %collective-permute-start.4 = (bf16[256,128]{1,0:T(8,128)(2,1)S(1)}, bf16[256,128]{1,0:T(8,128)(2,1)S(1)}, u32[]{:S(2)}, u32[]{:S(2)}) collective-permute-start(bf16[256,128]{1,0:T(8,128)(2,1)S(1)} %broadcast_select_fusion.2), channel_id=1, source_target_pairs={{0,2},{2,0},{4,6},{6,4},{8,10},{10,8},{12,14},{14,12},{1,3},{3,1},... | collective-permute-start | bytes 196616 | tf_op jit(solution)/shard_map/ppermute | solution.py:37
  73.4 7.7 %collective-permute-start.9 = (bf16[256,2048]{1,0:T(8,128)(2,1)}, bf16[256,2048]{1,0:T(8,128)(2,1)S(1)}, u32[]{:S(2)}, u32[]{:S(2)}) collective-permute-start(bf16[256,2048]{1,0:T(8,128)(2,1)} %get-tuple-element.23), channel_id=1, source_target_pairs={{0,16},{16,0},{1,17},{17,1},{2,18},{18,2},{3,19},{19,3},{4,20},{20... | collective-permute-start | bytes 3145736 | tf_op jit(solution)/shard_map/ppermute | solution.py:32
  73.4 6.4 %collective-permute-start.7 = (bf16[256,128]{1,0:T(8,128)(2,1)S(1)}, bf16[256,128]{1,0:T(8,128)(2,1)S(1)}, u32[]{:S(2)}, u32[]{:S(2)}) collective-permute-start(bf16[256,128]{1,0:T(8,128)(2,1)S(1)} %get-tuple-element.20), channel_id=1, source_target_pairs={{4,0},{6,2},{8,4},{10,6},{12,8},{14,10},{5,1},{7,3},{9,5},{11,7},{... | collective-permute-start | bytes 196616 | tf_op jit(solution)/shard_map/ppermute | solution.py:27
  74.6 6.4 %collective-permute-start.8 = (bf16[256,128]{1,0:T(8,128)(2,1)S(1)}, bf16[256,128]{1,0:T(8,128)(2,1)S(1)}, u32[]{:S(2)}, u32[]{:S(2)}) collective-permute-start(bf16[256,128]{1,0:T(8,128)(2,1)S(1)} %get-tuple-element.21), channel_id=1, source_target_pairs={{2,0},{4,2},{6,4},{8,6},{10,8},{12,10},{14,12},{3,1},{5,3},{7,5},{... | collective-permute-start | bytes 196616 | tf_op jit(solution)/shard_map/ppermute | solution.py:27
  90.3 7.0 %collective-permute-start.13 = (bf16[96,8,128]{2,1,0:T(8,128)(2,1)S(1)}, bf16[96,8,128]{2,1,0:T(8,128)(2,1)S(1)}, u32[]{:S(2)}, u32[]{:S(2)}) collective-permute-start(bf16[96,8,128]{2,1,0:T(8,128)(2,1)S(1)} %constant_dynamic-slice_fusion.1), channel_id=1, source_target_pairs={{0,1},{1,0},{2,3},{3,2},{4,5},{5,4},{6,7},{7,6},{8,9},{9,8},{10,11... | collective-permute-start | bytes 589832 | tf_op jit(solution)/shard_map/ppermute | solution.py:37
  92.0 8.1 %collective-permute-start.11 = (bf16[104,8,128]{2,1,0:T(8,128)(2,1)S(1)}, bf16[104,8,128]{2,1,0:T(8,128)(2,1)S(1)}, u32[]{:S(2)}, u32[]{:S(2)}) collective-permute-start(bf16[104,8,128]{2,1,0:T(8,128)(2,1)S(1)} %constant_dynamic-slice_fusion.3), channel_id=1, source_target_pairs={{0,2},{2,0},{4,6},{6,4},{8,10},{10,8},{12,14},{14,12},{1,3},{3,1},... | collective-permute-start | bytes 638984 | tf_op jit(solution)/shard_map/ppermute | solution.py:37
  97.4 5.3 %collective-permute-start.14 = (bf16[48,8,128]{2,1,0:T(8,128)(2,1)S(1)}, bf16[48,8,128]{2,1,0:T(8,128)(2,1)S(1)}, u32[]{:S(2)}, u32[]{:S(2)}) collective-permute-start(bf16[48,8,128]{2,1,0:T(8,128)(2,1)S(1)} %constant_dynamic-slice_fusion), channel_id=1, source_target_pairs={{0,2},{2,0},{4,6},{6,4},{8,10},{10,8},{12,14},{14,12},{1,3},{3,1},... | collective-permute-start | bytes 294920 | tf_op jit(solution)/shard_map/ppermute | solution.py:37
  100.2 4.8 %collective-permute-start.12 = (bf16[52,8,128]{2,1,0:T(8,128)(2,1)S(1)}, bf16[52,8,128]{2,1,0:T(8,128)(2,1)S(1)}, u32[]{:S(2)}, u32[]{:S(2)}) collective-permute-start(bf16[52,8,128]{2,1,0:T(8,128)(2,1)S(1)} %constant_dynamic-slice_fusion.2), channel_id=1, source_target_pairs={{0,1},{1,0},{2,3},{3,2},{4,5},{5,4},{6,7},{7,6},{8,9},{9,8},{10,11... | collective-permute-start | bytes 319496 | tf_op jit(solution)/shard_map/ppermute | solution.py:37
  105.0 5.6 %collective-permute-start.15 = (bf16[1,25,8,128]{3,2,1,0:T(8,128)(2,1)S(1)}, bf16[1,25,8,128]{3,2,1,0:T(8,128)(2,1)S(1)}, u32[]{:S(2)}, u32[]{:S(2)}) collective-permute-start(bf16[1,25,8,128]{3,2,1,0:T(8,128)(2,1)S(1)} %get-tuple-element.35), channel_id=1, source_target_pairs={{0,4},{2,6},{4,0},{6,2},{8,12},{10,14},{12,8},{14,10},{1,5},{3,7},... | collective-permute-start | bytes 153608 | tf_op jit(solution)/shard_map/ppermute | solution.py:37
  107.5 5.1 %collective-permute-start.16 = (bf16[1,25,8,128]{3,2,1,0:T(8,128)(2,1)S(1)}, bf16[1,25,8,128]{3,2,1,0:T(8,128)(2,1)S(1)}, u32[]{:S(2)}, u32[]{:S(2)}) collective-permute-start(bf16[1,25,8,128]{3,2,1,0:T(8,128)(2,1)S(1)} %get-tuple-element.36), channel_id=1, source_target_pairs={{0,8},{2,10},{4,12},{6,14},{8,0},{10,2},{12,4},{14,6},{1,9},{3,11}... | collective-permute-start | bytes 153608 | tf_op jit(solution)/shard_map/ppermute | solution.py:37
  107.5 6.0 %collective-permute-start.17 = (bf16[1,25,8,128]{3,2,1,0:T(8,128)(2,1)S(1)}, bf16[1,25,8,128]{3,2,1,0:T(8,128)(2,1)S(1)}, u32[]{:S(2)}, u32[]{:S(2)}) collective-permute-start(bf16[1,25,8,128]{3,2,1,0:T(8,128)(2,1)S(1)} %get-tuple-element.37), channel_id=1, source_target_pairs={{0,12},{2,14},{4,8},{6,10},{8,4},{10,6},{12,0},{14,2},{1,13},{3,15... | collective-permute-start | bytes 153608 | tf_op jit(solution)/shard_map/ppermute | solution.py:37
  113.6 4.5 %collective-permute-start.18 = (bf16[1,25,8,128]{3,2,1,0:T(8,128)(2,1)S(1)}, bf16[1,25,8,128]{3,2,1,0:T(8,128)(2,1)S(1)}, u32[]{:S(2)}, u32[]{:S(2)}) collective-permute-start(bf16[1,25,8,128]{3,2,1,0:T(8,128)(2,1)S(1)} %add_convert_fusion.5), channel_id=1, source_target_pairs={{0,4},{2,6},{4,0},{6,2},{8,12},{10,14},{12,8},{14,10},{1,5},{3,7},... | collective-permute-start | bytes 153608 | tf_op jit(solution)/shard_map/ppermute | solution.py:37
  114.3 5.0 %collective-permute-start.19 = (bf16[1,25,8,128]{3,2,1,0:T(8,128)(2,1)S(1)}, bf16[1,25,8,128]{3,2,1,0:T(8,128)(2,1)S(1)}, u32[]{:S(2)}, u32[]{:S(2)}) collective-permute-start(bf16[1,25,8,128]{3,2,1,0:T(8,128)(2,1)S(1)} %add_convert_fusion.5), channel_id=1, source_target_pairs={{0,8},{2,10},{4,12},{6,14},{8,0},{10,2},{12,4},{14,6},{1,9},{3,11}... | collective-permute-start | bytes 153608 | tf_op jit(solution)/shard_map/ppermute | solution.py:37
  116.6 5.9 %collective-permute-start.20 = (bf16[1,25,8,128]{3,2,1,0:T(8,128)(2,1)S(1)}, bf16[1,25,8,128]{3,2,1,0:T(8,128)(2,1)S(1)}, u32[]{:S(2)}, u32[]{:S(2)}) collective-permute-start(bf16[1,25,8,128]{3,2,1,0:T(8,128)(2,1)S(1)} %add_convert_fusion.5), channel_id=1, source_target_pairs={{0,12},{2,14},{4,8},{6,10},{8,4},{10,6},{12,0},{14,2},{1,13},{3,15... | collective-permute-start | bytes 153608 | tf_op jit(solution)/shard_map/ppermute | solution.py:37
  122.6 5.9 %collective-permute-start.21 = (bf16[52,8,128]{2,1,0:T(8,128)(2,1)S(1)}, bf16[52,8,128]{2,1,0:T(8,128)(2,1)S(1)}, u32[]{:S(2)}, u32[]{:S(2)}) collective-permute-start(bf16[52,8,128]{2,1,0:T(8,128)(2,1)S(1)} %bitcast.64), channel_id=1, source_target_pairs={{0,1},{1,0},{2,3},{3,2},{4,5},{5,4},{6,7},{7,6},{8,9},{9,8},{10,11... | collective-permute-start | bytes 319496 | tf_op jit(solution)/shard_map/ppermute | solution.py:37
  124.2 4.8 %collective-permute-start.23 = (bf16[48,8,128]{2,1,0:T(8,128)(2,1)S(1)}, bf16[48,8,128]{2,1,0:T(8,128)(2,1)S(1)}, u32[]{:S(2)}, u32[]{:S(2)}) collective-permute-start(bf16[48,8,128]{2,1,0:T(8,128)(2,1)S(1)} %bitcast.67), channel_id=1, source_target_pairs={{0,2},{2,0},{4,6},{6,4},{8,10},{10,8},{12,14},{14,12},{1,3},{3,1},... | collective-permute-start | bytes 294920 | tf_op jit(solution)/shard_map/ppermute | solution.py:37
  128.5 5.9 %collective-permute-start.22 = (bf16[104,8,128]{2,1,0:T(8,128)(2,1)S(1)}, bf16[104,8,128]{2,1,0:T(8,128)(2,1)S(1)}, u32[]{:S(2)}, u32[]{:S(2)}) collective-permute-start(bf16[104,8,128]{2,1,0:T(8,128)(2,1)S(1)} %pad_maximum_fusion.6), channel_id=1, source_target_pairs={{0,2},{2,0},{4,6},{6,4},{8,10},{10,8},{12,14},{14,12},{1,3},{3,1},... | collective-permute-start | bytes 638984 | tf_op jit(solution)/shard_map/ppermute | solution.py:37
  129.1 5.7 %collective-permute-start.24 = (bf16[96,8,128]{2,1,0:T(8,128)(2,1)S(1)}, bf16[96,8,128]{2,1,0:T(8,128)(2,1)S(1)}, u32[]{:S(2)}, u32[]{:S(2)}) collective-permute-start(bf16[96,8,128]{2,1,0:T(8,128)(2,1)S(1)} %pad_maximum_fusion.8), channel_id=1, source_target_pairs={{0,1},{1,0},{2,3},{3,2},{4,5},{5,4},{6,7},{7,6},{8,9},{9,8},{10,11... | collective-permute-start | bytes 589832 | tf_op jit(solution)/shard_map/ppermute | solution.py:37
  (24 other events, 131.9 us)

commit v5 on v4

--- a/solution.py
+++ b/solution.py
@@ -9,8 +9,8 @@
 
 HD = 128
 WINDOW = 1024
-SUB = 8
-PIECES = 2
+SUB = 16
+PIECES = 4
 
 query_scale = 168.0 ** (-0.5)
 adapter_scale = 0.5
@@ -55,23 +55,112 @@
     return jnp.sum((doc_ends[None, :] <= positions[:, None]).astype(jnp.int32), axis=1)
 
 
+def in_hbm(value):
+    return pltpu.with_memory_space_constraint(value, pltpu.HBM)
+
+
+def chunks_of(cols):
+    chunk = -(-cols // 6)
+    chunk += chunk % 2
+    return [slice(c * HD, min(c + chunk, cols) * HD) for c in range(0, cols, chunk)]
+
+
+def pack_kernel(hidden_hbm, down_hbm, key_hbm, val_hbm, *refs, pieces, heads, lanes):
+    messages = refs[:pieces]
+    hidden_ref, down_ref, sems = refs[pieces:]
+    loads, packs = [], []
+    for k, cut in enumerate(lanes):
+        loads.append(
+            [
+                pltpu.make_async_copy(hidden_hbm.at[:, cut], hidden_ref.at[:, cut], sems.at[2 * k]),
+                pltpu.make_async_copy(down_hbm.at[:, cut], down_ref.at[:, cut], sems.at[2 * k + 1]),
+            ]
+        )
+    at = 2 * len(lanes)
+    for i, message in enumerate(messages):
+        cut = slice(i * heads * HD, (i + 1) * heads * HD)
+        for j, rows in enumerate((key_hbm, val_hbm)):
+            target = message.at[:, j * heads * HD : (j + 1) * heads * HD]
+            packs.append(pltpu.make_async_copy(rows.at[:, cut], target, sems.at[at]))
+            at += 1
+    for pair in loads:
+        for load in pair:
+            load.start()
+    for pack in packs:
+        pack.start()
+    low = None
+    for pair, cut in zip(loads, lanes):
+        for load in pair:
+            load.wait()
+        part = lax.dot_general(
+            hidden_ref[:, cut],
+            down_ref[:, cut],
+            (((1,), (1,)), ((), ())),
+            preferred_element_type=f32,
+        )
+        low = part if low is None else low + part
+    messages[0][:, 2 * heads * HD :] = low.astype(bf16)
+    for pack in packs:
+        pack.wait()
+
+
+def pack(hidden, down, keys, vals, pieces):
+    tok, model_width = hidden.shape
+    width = down.shape[0]
+    heads = keys.shape[1] // HD // pieces
+    lanes = chunks_of(model_width // HD)
+    return pl.pallas_call(
+        partial(pack_kernel, pieces=pieces, heads=heads, lanes=lanes),
+        in_specs=[pl.BlockSpec(memory_space=pltpu.HBM)] * 4,
+        out_specs=[pl.BlockSpec(memory_space=pltpu.VMEM)] * pieces,
+        out_shape=[
+            pltpu.VMEM((tok, 2 * heads * HD + (width if i == 0 else 0)), bf16)
+            for i in range(pieces)
+        ],
+        scratch_shapes=[
+            pltpu.VMEM((tok, model_width), bf16),
+            pltpu.VMEM((width, model_width), bf16),
+            pltpu.SemaphoreType.DMA((2 * len(lanes) + 2 * pieces,)),
+        ],
+        compiler_params=pltpu.CompilerParams(vmem_limit_bytes=16 << 20),
+        name="pack",
+    )(in_hbm(hidden), in_hbm(down), in_hbm(keys), in_hbm(vals))
+
+
 def in_vmem(value):
     return pltpu.with_memory_space_constraint(value, pltpu.VMEM)
 
 
-def attention_kernel(*refs, n_blocks, piece, heads, tok, group, sub, chained, is_last):
+def attention_kernel(*refs, n_blocks, piece, heads, tok, group, sub, rank, chained, is_last):
     m_refs = refs[:n_blocks]
-    q_ref, g_ref, spread_ref, up_ref, bias_ref, cos_ref, sin_ref = refs[n_blocks : n_blocks + 7]
+    q_ref, up_ref, bias_ref, cos_ref, sin_ref, mask_ref, g_hbm = refs[n_blocks : n_blocks + 7]
     at = n_blocks + 7
+    if chained:
+        spread_ref, lg_in_ref = refs[at : at + 2]
+        at += 4
+    out_ref, u_ref = refs[at : at + 2]
+    at += 2
+    if not is_last:
+        lg_ref = refs[at]
+        at += 1
+    else:
+        low_refs = refs[at : at + n_blocks]
+        at += n_blocks
+    if not chained:
+        spread_ref = refs[at]
+        at += 1
     if is_last:
-        mask_ref = refs[at]
+        lg_ref = refs[at]
         at += 1
-    if chained:
-        lg_in_ref = refs[at]
-        at += 3
-    out_ref, u_ref, lg_ref = refs[at : at + 3]
-    lg_low_refs = refs[at + 3 :]
+    g_ref, g_sem = refs[at:]
     first_head = piece * heads
+    g_lanes = slice(first_head * group * HD, (first_head + heads) * group * HD)
+    g_load = pltpu.make_async_copy(g_hbm.at[:, g_lanes], g_ref, g_sem)
+    g_load.start()
+    if not chained:
+        low_lanes = slice(2 * heads * HD, None)
+        low = jnp.concatenate([r[:, low_lanes] for r in m_refs], axis=0).astype(f32)
+        spread_ref[...] = (low * mask_ref[...]).astype(bf16)
     spread = spread_ref[...]
     span = spread.shape[0]
     half = spread.shape[1] // 2
@@ -119,7 +208,7 @@
         for j in range(group):
             lanes = lanes_of(h * group + j)
             out_ref[cut, lanes] = out[j * sub : (j + 1) * sub]
-            gs.append(g_ref[cut, lanes])
+            gs.append(g_ref[cut, (h * group + j) * HD : (h * group + j + 1) * HD])
         g_t = (jnp.concatenate(gs, axis=0).T.astype(f32) * scale).astype(bf16)
         drift = jnp.sum(out_t.astype(f32) * g_t.astype(f32), axis=0, keepdims=True)
         dprob = jnp.dot(val[rows], g_t, preferred_element_type=f32)
@@ -160,6 +249,8 @@
             if i == 0:
                 prepared[h] = prepare(h)
             scores[h, i] = scored(h, i, prepared[h][0])
+        if t == 1:
+            g_load.wait()
         if 0 <= t - 1 < len(units):
             h, i = units[t - 1]
             states[h, i] = forward(h, i, scores[h, i][1], prepared[h][1])
@@ -169,33 +260,53 @@
             if i == subs - 1:
                 finish(h, grads[h])
     if is_last:
-        lg_ref[...] *= mask_ref[...]
-    for j, ref in enumerate(lg_low_refs):
-        ref[...] = lg_ref[j * tok : (j + 1) * tok].astype(bf16)
-
-
-def attention(blocks, piece, carried, mask, q_rows, g_rows, spread, up_cat, bias, cos, sin):
+        masked = (adapter_scale * lg_ref[...] * mask_ref[...]).astype(bf16)
+        compact = dot(picks(2 * half, rank), masked, last)
+        for j, ref in enumerate(low_refs):
+            ref[...] = compact[:, j * tok : (j + 1) * tok].astype(bf16)
+
+
+def picks(width, rank):
+    row = lax.broadcasted_iota(jnp.int32, (2 * rank, width), 0)
+    col = lax.broadcasted_iota(jnp.int32, (2 * rank, width), 1)
+    hit = (row // rank == col // (width // 2)) & (row % rank == col % rank)
+    return hit.astype(f32).astype(bf16)
+
+
+def attention(blocks, piece, pieces, carried, mask, q_rows, g_rows, up_cat, bias, cos, sin, rank):
     tok = q_rows.shape[0]
-    heads = blocks[0].shape[1] // (2 * HD)
     kv_heads, width, _ = up_cat.shape
+    heads = kv_heads // pieces
     group = q_rows.shape[1] // (kv_heads * HD)
     n_blocks = len(blocks)
-    span = spread.shape[0]
+    span = bias.shape[0]
     half = width // 2
     sub = HD if tok % HD == 0 else tok
-    operands = [*blocks, q_rows, g_rows, spread, up_cat, bias, cos, sin]
+    operands = [in_vmem(x) for x in (*blocks, q_rows, up_cat, bias, cos, sin, mask)]
+    operands.append(in_hbm(g_rows))
     aliases = {}
-    is_last = mask is not None
+    is_last = piece == pieces - 1
+    resident = [pl.BlockSpec(memory_space=pltpu.VMEM)]
+    in_specs = resident * (len(operands) - 1) + [pl.BlockSpec(memory_space=pltpu.HBM)]
+    if carried is not None:
+        at = len(operands)
+        aliases = {at + 2: 0, at + 3: 1}
+        if not is_last:
+            aliases[at + 1] = 2
+        out, u, lg, spread = carried
+        operands += [in_vmem(x) for x in (spread, lg, out, u)]
+        in_specs = in_specs + resident * 4
+    out_shape = [pltpu.VMEM(q_rows.shape, bf16), pltpu.VMEM((2, half, kv_heads * HD), bf16)]
+    scratch = []
     if is_last:
-        operands.append(mask)
-    if carried is not None:
-        out, u, lg = carried
-        at = len(operands)
-        operands += [lg, out, u]
-        aliases = {at: 2, at + 1: 0, at + 2: 1}
-    low_count = n_blocks - 1 if is_last else 0
+        out_shape += [pltpu.VMEM((2 * rank, tok), bf16)] * n_blocks
+        scratch = [pltpu.VMEM((span, width), f32)]
+    else:
+        out_shape.append(pltpu.VMEM((span, width), f32))
+    if carried is None:
+        out_shape.append(pltpu.VMEM((span, width), bf16))
     work = heads * group * tok * (span - tok + sub) * HD * 2 * 6
-    return pl.pallas_call(
+    result = pl.pallas_call(
         partial(
             attention_kernel,
             n_blocks=n_blocks,
@@ -204,43 +315,54 @@
             tok=tok,
             group=group,
             sub=sub,
+            rank=rank,
             chained=carried is not None,
             is_last=is_last,
         ),
-        in_specs=[pl.BlockSpec(memory_space=pltpu.VMEM)] * len(operands),
-        out_specs=[pl.BlockSpec(memory_space=pltpu.VMEM)] * (3 + low_count),
-        out_shape=[
-            pltpu.VMEM(q_rows.shape, bf16),
-            pltpu.VMEM((2, half, kv_heads * HD), bf16),
-            pltpu.VMEM((span, width), f32),
-        ]
-        + [pltpu.VMEM((tok, width), bf16)] * low_count,
+        in_specs=in_specs,
+        out_specs=resident * len(out_shape),
+        out_shape=out_shape,
+        scratch_shapes=scratch
+        + [pltpu.VMEM((tok, heads * group * HD), bf16), pltpu.SemaphoreType.DMA(())],
         input_output_aliases=aliases,
         compiler_params=pltpu.CompilerParams(vmem_limit_bytes=28 << 20),
         cost_estimate=pl.CostEstimate(flops=work, transcendentals=0, bytes_accessed=heads * tok * HD * 20),
         name="attention",
-    )(*[in_vmem(x) for x in operands])
-
-
-def product_kernel(*refs, n_recv, tok, cols, up_cols, chunk):
-    side_ref, lg_ref = refs[:2]
+    )(*operands)
+    if is_last:
+        return result
+    return (*result[:3], result[3] if carried is None else spread)
+
+
+def product_kernel(*refs, n_recv, lanes, up_cols):
+    side_ref, own_ref = refs[:2]
     recv = refs[2 : 2 + n_recv]
-    up_ref, hidden_hbm, handed_hbm, keep_ref, send_ref, handed_out, hidden_ref, sems = refs[2 + n_recv :]
-    loads = []
-    for k, c in enumerate(range(0, cols, chunk)):
-        lanes = slice(c * HD, min(c + chunk, cols) * HD)
-        loads.append(pltpu.make_async_copy(hidden_hbm.at[:, lanes], hidden_ref.at[:, lanes], sems.at[k]))
+    mask_ref, up_ref, hidden_hbm, handed_hbm = refs[2 + n_recv : 6 + n_recv]
+    keep_ref, send_ref, handed_out, hidden_ref, sems = refs[6 + n_recv :]
+    loads = [
+        pltpu.make_async_copy(hidden_hbm.at[:, cut], hidden_ref.at[:, cut], sems.at[k])
+        for k, cut in enumerate(lanes)
+    ]
     handing = pltpu.make_async_copy(handed_hbm, handed_out, sems.at[len(loads)])
     for load in loads:
         load.start()
     handing.start()
     side = side_ref[0]
-    total = lg_ref[lg_ref.shape[0] - tok :]
+    total = own_ref[...].astype(f32)
     for r in recv:
         total = total + r[...].astype(f32)
-    width = total.shape[1]
+    width = mask_ref.shape[0]
     half = width // 2
-    total = jnp.where(side == 0, total, pltpu.roll(total, half, 1)).astype(bf16)
+    cols = hidden_ref.shape[1] // HD
+    total = lax.dot_general(
+        picks(width, total.shape[0] // 2),
+        total.astype(bf16),
+        (((0,), (0,)), ((), ())),
+        preferred_element_type=f32,
+    )
+    total = total * mask_ref[...]
+    swapped = jnp.concatenate([total[half:], total[:half]], axis=0)
+    total = jnp.where(side == 0, total, swapped).astype(bf16)
     per_row = cols + up_cols
     rows = half // SUB
     for h in range(up_cols):
@@ -253,15 +375,13 @@
         rest = keep_ref.shape[0] - used
         keep_ref[pl.ds(used, rest)] = jnp.zeros((rest, SUB, HD), bf16)
         send_ref[pl.ds(used, rest)] = jnp.zeros((rest, SUB, HD), bf16)
-    step = 2 if cols % 2 == 0 and chunk % 2 == 0 else 1
+    step = 2 if cols % 2 == 0 else 1
+    starts = [cut.start // HD for cut in lanes]
     for c in range(0, cols, step):
-        if c % chunk == 0:
-            loads[c // chunk].wait()
-        w = lax.dot_general(
-            total,
-            hidden_ref[:, c * HD : (c + step) * HD],
-            (((0,), (0,)), ((), ())),
-            preferred_element_type=f32,
+        if c in starts:
+            loads[starts.index(c)].wait()
+        w = jnp.dot(
+            total, hidden_ref[:, c * HD : (c + step) * HD], preferred_element_type=f32
         ).astype(bf16)
         for j in range(step):
             for r in range(rows):
@@ -269,6 +389,14 @@
                 keep_ref[r * per_row + c + j] = tile[r * SUB : (r + 1) * SUB]
                 send_ref[r * per_row + c + j] = tile[half + r * SUB : half + (r + 1) * SUB]
     handing.wait()
+
+
+def merge_kernel(keep_ref, recv_ref, *out_refs):
+    at = 0
+    for ref in out_refs:
+        rows = slice(at, at + ref.shape[0])
+        ref[...] = (keep_ref[rows].astype(f32) + recv_ref[rows].astype(f32)).astype(bf16)
+        at += ref.shape[0]
 
 
 def assemble_kernel(
@@ -378,13 +506,9 @@
     steps = (reach + 1) // 2
 
     pieces = PIECES if kv_heads % PIECES == 0 else 1
-    count = kv_heads // pieces
-    keys, vals = frozen_key_rows[0], frozen_value_rows[0]
-    parts = []
-    for i in range(pieces):
-        cut = slice(i * count * HD, (i + 1) * count * HD)
-        own = jnp.concatenate([keys[:, cut], vals[:, cut]], axis=1)
-        parts.append(window_blocks(own, steps)[::-1] + [own])
+    down = adapter_down_maps.reshape(model_width, width).T
+    messages = pack(hidden[0], down, frozen_key_rows[0], frozen_value_rows[0], pieces)
+    parts = [window_blocks(m, steps)[::-1] + [m] for m in messages]
     returned = permute_cyclic(next_output_gradient, "section", -1)
 
     block_starts = jnp.stack([(ctx_index - d) * tok for d in range(2 * steps, -1, -1)])
@@ -394,8 +518,8 @@
     picked = key_docs[:, None] == jnp.arange(document_lengths.shape[1], dtype=jnp.int32)[None, :]
     tenant = jnp.sum(picked.astype(jnp.int32) * document_adapter[0][None, :], axis=1)
     lane_adapter = (jnp.arange(width, dtype=jnp.int32) // rank) % adapters
-    span_mask = jnp.where(tenant[:, None] == lane_adapter[None, :], adapter_scale, 0.0).astype(f32)
-    mask = (tenant[-tok:, None] == lane_adapter[None, :]).astype(f32)
+    mask = (tenant[:, None] == lane_adapter[None, :]).astype(f32)
+    own_mask = (lane_adapter[:, None] == tenant[None, -tok:]).astype(f32)
     gap = positions[None, :] - key_pos[:, None]
     allowed = (
         (key_docs[:, None] == docs[None, :])
@@ -409,12 +533,6 @@
     cos_half, sin_half = jnp.cos(angles), jnp.sin(angles)
     cos = jnp.concatenate([cos_half, cos_half], axis=1)
     sin = jnp.concatenate([-sin_half, sin_half], axis=1)
-
-    low = jnp.dot(
-        hidden[0], adapter_down_maps.reshape(model_width, width), preferred_element_type=f32
-    )
-    spread_own = (low * mask).astype(bf16)
-    spread = jnp.concatenate(window_blocks(spread_own, steps)[::-1] + [spread_own], axis=0)
     up_flat = adapter_up_maps.reshape(2, half, kv_heads, HD)
     zero = jnp.zeros((kv_heads, half, HD), bf16)
     up_heads = jnp.moveaxis(up_flat, 2, 1)
@@ -428,22 +546,23 @@
 
     carried = None
     for i in range(pieces):
-        result = attention(
+        carried = attention(
             parts[i],
             i,
+            pieces,
             carried,
-            span_mask if i == pieces - 1 else None,
+            mask,
             frozen_query_rows[0],
             returned[0],
-            spread,
             up_cat,
             bias,
             cos,
             sin,
+            rank,
         )
-        carried = result[:3]
-    out, ups, lg = carried
-    received = [permute_by(low, "ctx", j - 2 * steps) for j, low in enumerate(result[3:])]
+    out, ups = carried[:2]
+    lows = carried[2:]
+    received = [permute_by(low, "ctx", j - 2 * steps) for j, low in enumerate(lows[:-1])]
     handed = permute_cyclic(out, "section", 1)[None]
 
     other = (
@@ -460,14 +579,11 @@
     smem = pl.BlockSpec(memory_space=pltpu.SMEM)
     vmem = pl.BlockSpec(memory_space=pltpu.VMEM)
     any_space = pl.BlockSpec(memory_space=pl.ANY)
-    chunk = -(-cols // 6)
-    chunk += chunk % 2
+    lanes = chunks_of(cols)
     tile_shape = (units * group, SUB, HD)
     keep, send, handed = pl.pallas_call(
-        partial(
-            product_kernel, n_recv=len(received), tok=tok, cols=cols, up_cols=up_cols, chunk=chunk
-        ),
-        in_specs=[smem] + [vmem] * (2 + len(received)) + [any_space] * 2,
+        partial(product_kernel, n_recv=len(received), lanes=lanes, up_cols=up_cols),
+        in_specs=[smem] + [vmem] * (3 + len(received)) + [pl.BlockSpec(memory_space=pltpu.HBM)] * 2,
         out_specs=[vmem, vmem, any_space],
         out_shape=[
             pltpu.VMEM(tile_shape, bf16),
@@ -476,14 +592,25 @@
         ],
         scratch_shapes=[
             pltpu.VMEM((tok, model_width), bf16),
-            pltpu.SemaphoreType.DMA((-(-cols // chunk) + 1,)),
+            pltpu.SemaphoreType.DMA((len(lanes) + 1,)),
         ],
         compiler_params=pltpu.CompilerParams(vmem_limit_bytes=16 << 20),
         name="product",
-    )(side[None], in_vmem(lg), *[in_vmem(r) for r in received], in_vmem(ups), hidden[0], handed)
+    )(
+        side[None],
+        *[in_vmem(x) for x in (lows[-1], *received, own_mask, ups)],
+        in_hbm(hidden[0]),
+        in_hbm(handed),
+    )
     recv = permute_cyclic(send, "section", 1)
-    tiles = (keep.astype(f32) + recv.astype(f32)).astype(bf16)
-    colours = [tiles[: a * group], tiles[a * group :]]
+    colours = pl.pallas_call(
+        merge_kernel,
+        in_specs=[vmem, vmem],
+        out_specs=[vmem, vmem],
+        out_shape=[pltpu.VMEM((n * group, SUB, HD), bf16) for n in (a, b)],
+        compiler_params=pltpu.CompilerParams(vmem_limit_bytes=8 << 20),
+        name="merge",
+    )(in_vmem(keep), in_vmem(recv))
     for k in range(len(other[0])):
         colours = [scatter_stage(colours[c], other[c][k]) for c in range(2)]
     rounds = [tail[k : k + 2] for k in range(0, len(tail), 2)]

time: 140 us -> 152 us (1.086)
  Pallas kernels: 21.7 us -> 55.1 us
  local copies, waits for them, and re-layouts: 9.95 us -> 1.99 us
  waiting for transfers between devices: 52.4 us -> 45.9 us
  starting transfers between devices: 43 us -> 39.8 us
  matrix products: 2.65 us -> 0 us
    pallas_call x1 -> x3, Pallas kernels: 2.61 us -> 37.4 us  [the longest x1 33.9 us: step(): pl.pallas_call(partial(product_kernel, n_recv=len(received), lanes=lanes,...]
    ppermute x17 -> x18, waiting for transfers between devices: 39.2 us -> 32.3 us  [permute_xor(): return lax.ppermute(value, axis, [(i, i ^ bit) for i in range(count)])]
    unnamed x43 -> x31, local copies, waits for them, and re-layouts: 7.1 us -> 1.08 us
    ppermute x17 -> x18, starting transfers between devices: 28 us -> 23 us  [permute_xor(): return lax.ppermute(value, axis, [(i, i ^ bit) for i in range(count)])]
    dot_general x1 -> x0, matrix products: 2.65 us -> none  [step(): jnp.dot(hidden[0], adapter_down_maps.reshape(model_width, width), preferr...]
    ppermute x5 -> x6, starting transfers between devices: 14.7 us -> 16.4 us  [permute_by(): lax.ppermute(value, axis, [(i, i + steps) for i in range(first, last)])]
    concatenate x3 -> x0, other arithmetic: 1.77 us -> none  [the longest x2 0.92 us: step(): own = jnp.concatenate([keys[:, cut], vals[:, cut]], axis=1)]
    pallas_call x2 -> x4, Pallas kernels: 16.6 us -> 15.4 us  [attention(): pl.pallas_call(partial(attention_kernel, n_blocks=n_blocks, piece=piece,...]
  transfers between devices with their start and end apart: 27 -> 29, of which waited for: 17 -> 19; matrix products, arithmetic and copies ran while one was open for 8% -> 5% of each run, Pallas kernels for 6% -> 7%
where the time goes in v5:
time: 152 us; the launch traced here: 151 us
  Pallas kernels  55.1 us (36%)
  waiting for transfers between devices  45.9 us (30%)
  starting transfers between devices  39.8 us (26%)
  other arithmetic  6.99 us (5%)
  local copies, waits for them, and re-layouts  1.99 us (1%)
    pallas_call x1, Pallas kernels, step(): pl.pallas_call(partial(product_kernel, n_recv=len(received), lanes=lanes,...  33.9 us
    ppermute x18, waiting for transfers between devices, permute_xor(): return lax.ppermute(value, axis, [(i, i ^ bit) for i in range(count)])  32.3 us
    ppermute x18, starting transfers between devices, permute_xor(): return lax.ppermute(value, axis, [(i, i ^ bit) for i in range(count)])  23 us
    ppermute x6, starting transfers between devices, permute_by(): lax.ppermute(value, axis, [(i, i + steps) for i in range(first, last)])  16.4 us
    pallas_call x4, Pallas kernels, attention(): pl.pallas_call(partial(attention_kernel, n_blocks=n_blocks, piece=piece,...  15.4 us
    ppermute x6, waiting for transfers between devices, permute_by(): lax.ppermute(value, axis, [(i, i + steps) for i in range(first, last)])  9.44 us
    ppermute x5, waiting for transfers between devices, permute_cyclic(): lax.ppermute(value, axis, [(i, (i + by) % count) for i in range(count)])  4.19 us
    pallas_call x1, Pallas kernels, pack(): pl.pallas_call(partial(pack_kernel, pieces=pieces, heads=heads, lanes=lan...  3.31 us
  transfers between devices with their start and end apart: 29, of which 19 were waited for; matrix products, arithmetic and copies ran while one was open for 5% of the time, Pallas kernels for 7%

profile of v5, /device:TPU:0, one launch (start us, length us, event | category | flops | bytes accessed | tf_op | source)
XLA Modules:
  0.0 151.2 jit_solution(14077254929310521407)
XLA Ops:
  0.7 3.3 %pack.1 = (bf16[256,640]{1,0:T(8,128)(2,1)S(1)}, bf16[256,512]{1,0:T(8,128)(2,1)S(1)}, bf16[256,512]{1,0:T(8,128)(2,1)S(1)}, bf16[256,512]{1,0:T(8,128)(2,1)S(1)}) custom-call(bf16[256,5376]{1,0:T(8,128)(2,1)} %bitcast.56, bf16[128,5376]{1,0:T(8,128)(2,1)} %bitcast.58, bf16[256,1024]{1,0:T(8,128)(2,1)} %bitcast.72, bf16[256,1024]{1,0:T(8,128)(2,1)} %bitcast.73), custom_call_target="tpu_custom_call" | custom-call | tf_op jit(solution)/shard_map/pack/pallas_call | solution.py:112
  4.0 5.0 %collective-permute-start.3 = (bf16[256,640]{1,0:T(8,128)(2,1)S(1)}, bf16[256,640]{1,0:T(8,128)(2,1)S(1)}, u32[]{:S(2)}, u32[]{:S(2)}) collective-permute-start(bf16[256,640]{1,0:T(8,128)(2,1)S(1)} %get-tuple-element.30.refs_2_), channel_id=1, source_target_pairs={{0,4},{2,6},{4,8},{6,10},{8,12},{10,14},{1,5},{3,7},{5,9},{7,11},{... | collective-permute-start | bytes 983048 | tf_op jit(solution)/shard_map/ppermute | solution.py:27
  9.1 3.5 %collective-permute-start.7 = (bf16[256,512]{1,0:T(8,128)(2,1)S(1)}, bf16[256,512]{1,0:T(8,128)(2,1)S(1)}, u32[]{:S(2)}, u32[]{:S(2)}) collective-permute-start(bf16[256,512]{1,0:T(8,128)(2,1)S(1)} %get-tuple-element.33.refs_2_), channel_id=1, source_target_pairs={{0,4},{2,6},{4,8},{6,10},{8,12},{10,14},{1,5},{3,7},{5,9},{7,11},{... | collective-permute-start | bytes 786440 | tf_op jit(solution)/shard_map/ppermute | solution.py:27
  12.6 3.5 %collective-permute-start.5 = (bf16[256,512]{1,0:T(8,128)(2,1)S(1)}, bf16[256,512]{1,0:T(8,128)(2,1)S(1)}, u32[]{:S(2)}, u32[]{:S(2)}) collective-permute-start(bf16[256,512]{1,0:T(8,128)(2,1)S(1)} %get-tuple-element.32.refs_2_), channel_id=1, source_target_pairs={{0,4},{2,6},{4,8},{6,10},{8,12},{10,14},{1,5},{3,7},{5,9},{7,11},{... | collective-permute-start | bytes 786440 | tf_op jit(solution)/shard_map/ppermute | solution.py:27
  18.8 2.6 %fusion.7 = (f32[768,64]{1,0:T(8,128)}, f32[768,64]{1,0:T(8,128)}, f32[768,64]{1,0:T(8,128)}) fusion(f32[64]{0:T(128)S(1)} %multiply_power_fusion, f32[768]{0:T(1024)S(1)} %convert_element_type.91), kind=kLoop, calls=%fused_computation.41 | loop fusion | flops 98304 | bytes 593152 | tf_op jit(solution)/shard_map/neg | solution.py:535
  29.9 2.9 %collective-permute-done.refs_0_ = bf16[256,512]{1,0:T(8,128)(2,1)S(1)} collective-permute-done((bf16[256,512]{1,0:T(8,128)(2,1)S(1)}, bf16[256,512]{1,0:T(8,128)(2,1)S(1)}, u32[]{:S(2)}, u32[]{:S(2)}) %collective-permute-start) | collective-permute-done | bytes 262176 | tf_op jit(solution)/shard_map/ppermute | solution.py:27
  34.4 7.2 %collective-permute-done.4.refs_1_ = bf16[256,640]{1,0:T(8,128)(2,1)S(1)} collective-permute-done((bf16[256,640]{1,0:T(8,128)(2,1)S(1)}, bf16[256,640]{1,0:T(8,128)(2,1)S(1)}, u32[]{:S(2)}, u32[]{:S(2)}) %collective-permute-start.4) | collective-permute-done | bytes 327712 | tf_op jit(solution)/shard_map/ppermute | solution.py:37
  41.6 3.5 %attention.4 = (bf16[256,2048]{1,0:T(8,128)(2,1)S(1)}, bf16[2,64,1024]{2,1,0:T(8,128)(2,1)S(1)}, f32[768,128]{1,0:T(8,128)S(1)}, bf16[768,128]{1,0:T(8,128)(2,1)S(1)}) custom-call(bf16[256,640]{1,0:T(8,128)(2,1)S(1)} %collective-permute-done.3.refs_0_, bf16[256,640]{1,0:T(8,128)(2,1)S(1)} %collective-permute-done.4.refs_1_, ...), custom_call_target="tpu_custom_call" | custom-call | flops 1006632960 | bytes 1310720 | tf_op jit(solution)/shard_map/attention/pallas_call | solution.py:309
  45.2 3.9 %attention.5 = (bf16[256,2048]{1,0:T(8,128)(2,1)S(1)}, bf16[2,64,1024]{2,1,0:T(8,128)(2,1)S(1)}, f32[768,128]{1,0:T(8,128)S(1)}) custom-call(bf16[256,512]{1,0:T(8,128)(2,1)S(1)} %copy-done.10, bf16[256,512]{1,0:T(8,128)(2,1)S(1)} %collective-permute-done.8.refs_1_, ...), custom_call_target="tpu_custom_call", output_to_operand_aliasing={{0}: (12, {}), {1}: (13, {}), {2}: (11, {})} | custom-call | flops 1006632960 | bytes 1310720 | tf_op jit(solution)/shard_map/attention/pallas_call | solution.py:309
  49.1 3.9 %attention.6 = (bf16[256,2048]{1,0:T(8,128)(2,1)S(1)}, bf16[2,64,1024]{2,1,0:T(8,128)(2,1)S(1)}, f32[768,128]{1,0:T(8,128)S(1)}) custom-call(bf16[256,512]{1,0:T(8,128)(2,1)S(1)} %copy-done.8, bf16[256,512]{1,0:T(8,128)(2,1)S(1)} %collective-permute-done.6.refs_1_, ...), custom_call_target="tpu_custom_call", output_to_operand_aliasing={{0}: (12, {}), {1}: (13, {}), {2}: (11, {})} | custom-call | flops 1006632960 | bytes 1310720 | tf_op jit(solution)/shard_map/attention/pallas_call | solution.py:309
  53.0 4.2 %attention.7 = (bf16[256,2048]{1,0:T(8,128)(2,1)S(1)}, bf16[2,64,1024]{2,1,0:T(8,128)(2,1)S(1)}, bf16[32,256]{1,0:T(8,128)(2,1)S(1)}, bf16[32,256]{1,0:T(8,128)(2,1)S(1)}, bf16[32,256]{1,0:T(8,128)(2,1)S(1)}) custom-call(bf16[256,512]{1,0:T(8,128)(2,1)S(1)} %copy-done.4, ...), custom_call_target="tpu_custom_call", output_to_operand_aliasing={{0}: (12, {}), {1}: (13, {})} | custom-call | flops 1006632960 | bytes 1310720 | tf_op jit(solution)/shard_map/attention/pallas_call | solution.py:309
  60.0 2.9 %collective-permute-done.10.refs_3_ = bf16[32,256]{1,0:T(8,128)(2,1)S(1)} collective-permute-done((bf16[32,256]{1,0:T(8,128)(2,1)S(1)}, bf16[32,256]{1,0:T(8,128)(2,1)S(1)}, u32[]{:S(2)}, u32[]{:S(2)}) %collective-permute-start.10) | collective-permute-done | bytes 16416 | tf_op jit(solution)/shard_map/ppermute | solution.py:27
  62.9 2.9 %collective-permute-done.9.refs_2_ = bf16[32,256]{1,0:T(8,128)(2,1)S(1)} collective-permute-done((bf16[32,256]{1,0:T(8,128)(2,1)S(1)}, bf16[32,256]{1,0:T(8,128)(2,1)S(1)}, u32[]{:S(2)}, u32[]{:S(2)}) %collective-permute-start.9) | collective-permute-done | bytes 16416 | tf_op jit(solution)/shard_map/ppermute | solution.py:27
  66.7 33.9 %product.1 = (bf16[208,16,128]{2,1,0:T(8,128)(2,1)S(1)}, bf16[208,16,128]{2,1,0:T(8,128)(2,1)}, bf16[1,256,2048]{2,1,0:T(8,128)(2,1)}) custom-call(s32[1]{0:T(128)} %bitcast.refs_0_, bf16[32,256]{1,0:T(8,128)(2,1)S(1)} %get-tuple-element.43.refs_1_, bf16[32,256]{1,0:T(8,128)(2,1)S(1)} %collective-permute-done.9.refs_2_, ...), custom_call_target="tpu_custom_call" | custom-call | tf_op jit(solution)/shard_map/product/pallas_call | solution.py:584
  100.7 2.6 %collective-permute-done.12.recv_ref = bf16[208,16,128]{2,1,0:T(8,128)(2,1)S(1)} collective-permute-done((bf16[208,16,128]{2,1,0:T(8,128)(2,1)}, bf16[208,16,128]{2,1,0:T(8,128)(2,1)S(1)}, u32[]{:S(2)}, u32[]{:S(2)}) %collective-permute-start.12) | collective-permute-done | bytes 852000 | tf_op jit(solution)/shard_map/ppermute | solution.py:32
  106.2 4.3 %collective-permute-done.15 = bf16[48,16,128]{2,1,0:T(8,128)(2,1)S(1)} collective-permute-done((bf16[48,16,128]{2,1,0:T(8,128)(2,1)S(1)}, bf16[48,16,128]{2,1,0:T(8,128)(2,1)S(1)}, u32[]{:S(2)}, u32[]{:S(2)}) %collective-permute-start.15) | collective-permute-done | bytes 196640 | tf_op jit(solution)/shard_map/ppermute | solution.py:37
  115.3 2.2 %collective-permute-done.14 = bf16[28,16,128]{2,1,0:T(8,128)(2,1)S(1)} collective-permute-done((bf16[28,16,128]{2,1,0:T(8,128)(2,1)S(1)}, bf16[28,16,128]{2,1,0:T(8,128)(2,1)S(1)}, u32[]{:S(2)}, u32[]{:S(2)}) %collective-permute-start.14) | collective-permute-done | bytes 114720 | tf_op jit(solution)/shard_map/ppermute | solution.py:37
  117.5 2.1 %collective-permute-start.17 = (bf16[1,13,16,128]{3,2,1,0:T(8,128)(2,1)S(1)}, bf16[1,13,16,128]{3,2,1,0:T(8,128)(2,1)S(1)}, u32[]{:S(2)}, u32[]{:S(2)}) collective-permute-start(bf16[1,13,16,128]{3,2,1,0:T(8,128)(2,1)S(1)} %get-tuple-element.57), channel_id=1, source_target_pairs={{0,4},{2,6},{4,0},{6,2},{8,12},{10,14},{12,8},{14,10},{1,5},{3,7},... | collective-permute-start | bytes 159752 | tf_op jit(solution)/shard_map/ppermute | solution.py:37
  119.6 2.4 %collective-permute-start.19 = (bf16[1,13,16,128]{3,2,1,0:T(8,128)(2,1)S(1)}, bf16[1,13,16,128]{3,2,1,0:T(8,128)(2,1)S(1)}, u32[]{:S(2)}, u32[]{:S(2)}) collective-permute-start(bf16[1,13,16,128]{3,2,1,0:T(8,128)(2,1)S(1)} %get-tuple-element.59), channel_id=1, source_target_pairs={{0,12},{2,14},{4,8},{6,10},{8,4},{10,6},{12,0},{14,2},{1,13},{3,15... | collective-permute-start | bytes 159752 | tf_op jit(solution)/shard_map/ppermute | solution.py:37
  126.6 2.2 %collective-permute-start.21 = (bf16[1,13,16,128]{3,2,1,0:T(8,128)(2,1)S(1)}, bf16[1,13,16,128]{3,2,1,0:T(8,128)(2,1)S(1)}, u32[]{:S(2)}, u32[]{:S(2)}) collective-permute-start(bf16[1,13,16,128]{3,2,1,0:T(8,128)(2,1)S(1)} %add_convert_fusion.4), channel_id=1, source_target_pairs={{0,8},{2,10},{4,12},{6,14},{8,0},{10,2},{12,4},{14,6},{1,9},{3,11}... | collective-permute-start | bytes 159752 | tf_op jit(solution)/shard_map/ppermute | solution.py:37
  131.6 3.1 %collective-permute-done.22 = bf16[1,13,16,128]{3,2,1,0:T(8,128)(2,1)S(1)} collective-permute-done((bf16[1,13,16,128]{3,2,1,0:T(8,128)(2,1)S(1)}, bf16[1,13,16,128]{3,2,1,0:T(8,128)(2,1)S(1)}, u32[]{:S(2)}, u32[]{:S(2)}) %collective-permute-start.22) | collective-permute-done | bytes 53280 | tf_op jit(solution)/shard_map/ppermute | solution.py:37
  136.6 3.4 %collective-permute-done.23 = bf16[28,16,128]{2,1,0:T(8,128)(2,1)S(1)} collective-permute-done((bf16[28,16,128]{2,1,0:T(8,128)(2,1)S(1)}, bf16[28,16,128]{2,1,0:T(8,128)(2,1)S(1)}, u32[]{:S(2)}, u32[]{:S(2)}) %collective-permute-start.23) | collective-permute-done | bytes 114720 | tf_op jit(solution)/shard_map/ppermute | solution.py:37
  142.2 3.8 %collective-permute-done.24 = bf16[56,16,128]{2,1,0:T(8,128)(2,1)S(1)} collective-permute-done((bf16[56,16,128]{2,1,0:T(8,128)(2,1)S(1)}, bf16[56,16,128]{2,1,0:T(8,128)(2,1)S(1)}, u32[]{:S(2)}, u32[]{:S(2)}) %collective-permute-start.24) | collective-permute-done | bytes 229408 | tf_op jit(solution)/shard_map/ppermute | solution.py:37
  148.7 2.4 %assemble.1 = (f32[128,5376]{1,0:T(8,128)}, f32[128,1024]{1,0:T(8,128)}) custom-call(s32[3]{0:T(128)S(1)} %pad_add_fusion.1.scalars_ref, bf16[16,7,16,128]{3,2,1,0:T(8,128)(2,1)S(1)} %bitcast.52, bf16[16,6,16,128]{3,2,1,0:T(8,128)(2,1)S(1)} %bitcast.53, bf16[16,7,16,128]{3,2,1,0:T(8,128)(2,1)S(1)} %bitcast.54, bf16[16,6,16,128]{3,2,1,0:T(8,128)(2,1)S(1)} %bitcast.55), custom_call_target="tpu_custom_call" | custom-call | tf_op jit(solution)/shard_map/assemble/pallas_call | solution.py:642
  (118 shorter events, 38.4 us)
Async XLA Ops:
  4.0 22.9 %collective-permute-start.3 = (bf16[256,640]{1,0:T(8,128)(2,1)S(1)}, bf16[256,640]{1,0:T(8,128)(2,1)S(1)}, u32[]{:S(2)}, u32[]{:S(2)}) collective-permute-start(bf16[256,640]{1,0:T(8,128)(2,1)S(1)} %get-tuple-element.30.refs_2_), channel_id=1, source_target_pairs={{0,4},{2,6},{4,8},{6,10},{8,12},{10,14},{1,5},{3,7},{5,9},{7,11},{... | collective-permute-start | bytes 983048 | tf_op jit(solution)/shard_map/ppermute | solution.py:27
  9.0 32.6 %collective-permute-start.2 = (bf16[1,256,2048]{2,1,0:T(8,128)(2,1)}, bf16[1,256,2048]{2,1,0:T(8,128)(2,1)}, u32[]{:S(2)}, u32[]{:S(2)}) collective-permute-start(bf16[1,256,2048]{2,1,0:T(8,128)(2,1)} %param.13), channel_id=1, source_target_pairs={{0,16},{16,0},{1,17},{17,1},{2,18},{18,2},{3,19},{19,3},{4,20},{20... | collective-permute-start | bytes 3145736 | tf_op jit(solution)/shard_map/ppermute | solution.py:32
  9.1 16.2 %collective-permute-start.7 = (bf16[256,512]{1,0:T(8,128)(2,1)S(1)}, bf16[256,512]{1,0:T(8,128)(2,1)S(1)}, u32[]{:S(2)}, u32[]{:S(2)}) collective-permute-start(bf16[256,512]{1,0:T(8,128)(2,1)S(1)} %get-tuple-element.33.refs_2_), channel_id=1, source_target_pairs={{0,4},{2,6},{4,8},{6,10},{8,12},{10,14},{1,5},{3,7},{5,9},{7,11},{... | collective-permute-start | bytes 786440 | tf_op jit(solution)/shard_map/ppermute | solution.py:27
  12.6 15.7 %collective-permute-start.5 = (bf16[256,512]{1,0:T(8,128)(2,1)S(1)}, bf16[256,512]{1,0:T(8,128)(2,1)S(1)}, u32[]{:S(2)}, u32[]{:S(2)}) collective-permute-start(bf16[256,512]{1,0:T(8,128)(2,1)S(1)} %get-tuple-element.32.refs_2_), channel_id=1, source_target_pairs={{0,4},{2,6},{4,8},{6,10},{8,12},{10,14},{1,5},{3,7},{5,9},{7,11},{... | collective-permute-start | bytes 786440 | tf_op jit(solution)/shard_map/ppermute | solution.py:27
  16.0 16.7 %collective-permute-start = (bf16[256,512]{1,0:T(8,128)(2,1)S(1)}, bf16[256,512]{1,0:T(8,128)(2,1)S(1)}, u32[]{:S(2)}, u32[]{:S(2)}) collective-permute-start(bf16[256,512]{1,0:T(8,128)(2,1)S(1)} %get-tuple-element.29.refs_2_), channel_id=1, source_target_pairs={{0,4},{2,6},{4,8},{6,10},{8,12},{10,14},{1,5},{3,7},{5,9},{7,11},{... | collective-permute-start | bytes 786440 | tf_op jit(solution)/shard_map/ppermute | solution.py:27
  25.3 19.9 %collective-permute-start.8 = (bf16[256,512]{1,0:T(8,128)(2,1)S(1)}, bf16[256,512]{1,0:T(8,128)(2,1)S(1)}, u32[]{:S(2)}, u32[]{:S(2)}) collective-permute-start(bf16[256,512]{1,0:T(8,128)(2,1)S(1)} %broadcast_select_fusion.1), channel_id=1, source_target_pairs={{0,2},{2,0},{4,6},{6,4},{8,10},{10,8},{12,14},{14,12},{1,3},{3,1},... | collective-permute-start | bytes 786440 | tf_op jit(solution)/shard_map/ppermute | solution.py:37
  26.9 14.7 %collective-permute-start.4 = (bf16[256,640]{1,0:T(8,128)(2,1)S(1)}, bf16[256,640]{1,0:T(8,128)(2,1)S(1)}, u32[]{:S(2)}, u32[]{:S(2)}) collective-permute-start(bf16[256,640]{1,0:T(8,128)(2,1)S(1)} %broadcast_select_fusion), channel_id=1, source_target_pairs={{0,2},{2,0},{4,6},{6,4},{8,10},{10,8},{12,14},{14,12},{1,3},{3,1},... | collective-permute-start | bytes 983048 | tf_op jit(solution)/shard_map/ppermute | solution.py:37
  28.3 20.8 %collective-permute-start.6 = (bf16[256,512]{1,0:T(8,128)(2,1)S(1)}, bf16[256,512]{1,0:T(8,128)(2,1)S(1)}, u32[]{:S(2)}, u32[]{:S(2)}) collective-permute-start(bf16[256,512]{1,0:T(8,128)(2,1)S(1)} %broadcast_select_fusion.2), channel_id=1, source_target_pairs={{0,2},{2,0},{4,6},{6,4},{8,10},{10,8},{12,14},{14,12},{1,3},{3,1},... | collective-permute-start | bytes 786440 | tf_op jit(solution)/shard_map/ppermute | solution.py:37
  32.8 20.2 %collective-permute-start.1 = (bf16[256,512]{1,0:T(8,128)(2,1)S(1)}, bf16[256,512]{1,0:T(8,128)(2,1)S(1)}, u32[]{:S(2)}, u32[]{:S(2)}) collective-permute-start(bf16[256,512]{1,0:T(8,128)(2,1)S(1)} %broadcast_select_fusion.3), channel_id=1, source_target_pairs={{0,2},{2,0},{4,6},{6,4},{8,10},{10,8},{12,14},{14,12},{1,3},{3,1},... | collective-permute-start | bytes 786440 | tf_op jit(solution)/shard_map/ppermute | solution.py:37
  57.2 8.6 %collective-permute-start.11 = (bf16[256,2048]{1,0:T(8,128)(2,1)S(1)}, bf16[256,2048]{1,0:T(8,128)(2,1)S(1)}, u32[]{:S(2)}, u32[]{:S(2)}) collective-permute-start(bf16[256,2048]{1,0:T(8,128)(2,1)S(1)} %get-tuple-element.47), channel_id=1, source_target_pairs={{0,16},{16,0},{1,17},{17,1},{2,18},{18,2},{3,19},{19,3},{4,20},{20... | collective-permute-start | bytes 3145736 | tf_op jit(solution)/shard_map/ppermute | solution.py:32
  57.3 5.6 %collective-permute-start.10 = (bf16[32,256]{1,0:T(8,128)(2,1)S(1)}, bf16[32,256]{1,0:T(8,128)(2,1)S(1)}, u32[]{:S(2)}, u32[]{:S(2)}) collective-permute-start(bf16[32,256]{1,0:T(8,128)(2,1)S(1)} %get-tuple-element.45), channel_id=1, source_target_pairs={{2,0},{4,2},{6,4},{8,6},{10,8},{12,10},{14,12},{3,1},{5,3},{7,5},{... | collective-permute-start | bytes 49160 | tf_op jit(solution)/shard_map/ppermute | solution.py:27
  58.6 7.2 %collective-permute-start.9 = (bf16[32,256]{1,0:T(8,128)(2,1)S(1)}, bf16[32,256]{1,0:T(8,128)(2,1)S(1)}, u32[]{:S(2)}, u32[]{:S(2)}) collective-permute-start(bf16[32,256]{1,0:T(8,128)(2,1)S(1)} %get-tuple-element.44), channel_id=1, source_target_pairs={{4,0},{6,2},{8,4},{10,6},{12,8},{14,10},{5,1},{7,3},{9,5},{11,7},{... | collective-permute-start | bytes 49160 | tf_op jit(solution)/shard_map/ppermute | solution.py:27
  103.5 7.0 %collective-permute-start.15 = (bf16[48,16,128]{2,1,0:T(8,128)(2,1)S(1)}, bf16[48,16,128]{2,1,0:T(8,128)(2,1)S(1)}, u32[]{:S(2)}, u32[]{:S(2)}) collective-permute-start(bf16[48,16,128]{2,1,0:T(8,128)(2,1)S(1)} %constant_dynamic-slice_fusion.1), channel_id=1, source_target_pairs={{0,1},{1,0},{2,3},{3,2},{4,5},{5,4},{6,7},{7,6},{8,9},{9,8},{10,11... | collective-permute-start | bytes 589832 | tf_op jit(solution)/shard_map/ppermute | solution.py:37
  105.1 7.4 %collective-permute-start.13 = (bf16[56,16,128]{2,1,0:T(8,128)(2,1)S(1)}, bf16[56,16,128]{2,1,0:T(8,128)(2,1)S(1)}, u32[]{:S(2)}, u32[]{:S(2)}) collective-permute-start(bf16[56,16,128]{2,1,0:T(8,128)(2,1)S(1)} %constant_dynamic-slice_fusion.3), channel_id=1, source_target_pairs={{0,2},{2,0},{4,6},{6,4},{8,10},{10,8},{12,14},{14,12},{1,3},{3,1},... | collective-permute-start | bytes 688136 | tf_op jit(solution)/shard_map/ppermute | solution.py:37
  112.6 4.9 %collective-permute-start.14 = (bf16[28,16,128]{2,1,0:T(8,128)(2,1)S(1)}, bf16[28,16,128]{2,1,0:T(8,128)(2,1)S(1)}, u32[]{:S(2)}, u32[]{:S(2)}) collective-permute-start(bf16[28,16,128]{2,1,0:T(8,128)(2,1)S(1)} %constant_dynamic-slice_fusion.2), channel_id=1, source_target_pairs={{0,1},{1,0},{2,3},{3,2},{4,5},{5,4},{6,7},{7,6},{8,9},{9,8},{10,11... | collective-permute-start | bytes 344072 | tf_op jit(solution)/shard_map/ppermute | solution.py:37
  117.5 5.3 %collective-permute-start.17 = (bf16[1,13,16,128]{3,2,1,0:T(8,128)(2,1)S(1)}, bf16[1,13,16,128]{3,2,1,0:T(8,128)(2,1)S(1)}, u32[]{:S(2)}, u32[]{:S(2)}) collective-permute-start(bf16[1,13,16,128]{3,2,1,0:T(8,128)(2,1)S(1)} %get-tuple-element.57), channel_id=1, source_target_pairs={{0,4},{2,6},{4,0},{6,2},{8,12},{10,14},{12,8},{14,10},{1,5},{3,7},... | collective-permute-start | bytes 159752 | tf_op jit(solution)/shard_map/ppermute | solution.py:37
  119.6 5.1 %collective-permute-start.18 = (bf16[1,13,16,128]{3,2,1,0:T(8,128)(2,1)S(1)}, bf16[1,13,16,128]{3,2,1,0:T(8,128)(2,1)S(1)}, u32[]{:S(2)}, u32[]{:S(2)}) collective-permute-start(bf16[1,13,16,128]{3,2,1,0:T(8,128)(2,1)S(1)} %get-tuple-element.58), channel_id=1, source_target_pairs={{0,8},{2,10},{4,12},{6,14},{8,0},{10,2},{12,4},{14,6},{1,9},{3,11}... | collective-permute-start | bytes 159752 | tf_op jit(solution)/shard_map/ppermute | solution.py:37
  119.6 6.1 %collective-permute-start.19 = (bf16[1,13,16,128]{3,2,1,0:T(8,128)(2,1)S(1)}, bf16[1,13,16,128]{3,2,1,0:T(8,128)(2,1)S(1)}, u32[]{:S(2)}, u32[]{:S(2)}) collective-permute-start(bf16[1,13,16,128]{3,2,1,0:T(8,128)(2,1)S(1)} %get-tuple-element.59), channel_id=1, source_target_pairs={{0,12},{2,14},{4,8},{6,10},{8,4},{10,6},{12,0},{14,2},{1,13},{3,15... | collective-permute-start | bytes 159752 | tf_op jit(solution)/shard_map/ppermute | solution.py:37
  126.6 5.0 %collective-permute-start.21 = (bf16[1,13,16,128]{3,2,1,0:T(8,128)(2,1)S(1)}, bf16[1,13,16,128]{3,2,1,0:T(8,128)(2,1)S(1)}, u32[]{:S(2)}, u32[]{:S(2)}) collective-permute-start(bf16[1,13,16,128]{3,2,1,0:T(8,128)(2,1)S(1)} %add_convert_fusion.4), channel_id=1, source_target_pairs={{0,8},{2,10},{4,12},{6,14},{8,0},{10,2},{12,4},{14,6},{1,9},{3,11}... | collective-permute-start | bytes 159752 | tf_op jit(solution)/shard_map/ppermute | solution.py:37
  128.8 5.9 %collective-permute-start.22 = (bf16[1,13,16,128]{3,2,1,0:T(8,128)(2,1)S(1)}, bf16[1,13,16,128]{3,2,1,0:T(8,128)(2,1)S(1)}, u32[]{:S(2)}, u32[]{:S(2)}) collective-permute-start(bf16[1,13,16,128]{3,2,1,0:T(8,128)(2,1)S(1)} %add_convert_fusion.4), channel_id=1, source_target_pairs={{0,12},{2,14},{4,8},{6,10},{8,4},{10,6},{12,0},{14,2},{1,13},{3,15... | collective-permute-start | bytes 159752 | tf_op jit(solution)/shard_map/ppermute | solution.py:37
  134.8 5.2 %collective-permute-start.23 = (bf16[28,16,128]{2,1,0:T(8,128)(2,1)S(1)}, bf16[28,16,128]{2,1,0:T(8,128)(2,1)S(1)}, u32[]{:S(2)}, u32[]{:S(2)}) collective-permute-start(bf16[28,16,128]{2,1,0:T(8,128)(2,1)S(1)} %bitcast.62), channel_id=1, source_target_pairs={{0,1},{1,0},{2,3},{3,2},{4,5},{5,4},{6,7},{7,6},{8,9},{9,8},{10,11... | collective-permute-start | bytes 344072 | tf_op jit(solution)/shard_map/ppermute | solution.py:37
  135.5 5.6 %collective-permute-start.25 = (bf16[24,16,128]{2,1,0:T(8,128)(2,1)S(1)}, bf16[24,16,128]{2,1,0:T(8,128)(2,1)S(1)}, u32[]{:S(2)}, u32[]{:S(2)}) collective-permute-start(bf16[24,16,128]{2,1,0:T(8,128)(2,1)S(1)} %bitcast.67), channel_id=1, source_target_pairs={{0,2},{2,0},{4,6},{6,4},{8,10},{10,8},{12,14},{14,12},{1,3},{3,1},... | collective-permute-start | bytes 294920 | tf_op jit(solution)/shard_map/ppermute | solution.py:37
  139.9 6.1 %collective-permute-start.24 = (bf16[56,16,128]{2,1,0:T(8,128)(2,1)S(1)}, bf16[56,16,128]{2,1,0:T(8,128)(2,1)S(1)}, u32[]{:S(2)}, u32[]{:S(2)}) collective-permute-start(bf16[56,16,128]{2,1,0:T(8,128)(2,1)S(1)} %pad_maximum_fusion.4), channel_id=1, source_target_pairs={{0,2},{2,0},{4,6},{6,4},{8,10},{10,8},{12,14},{14,12},{1,3},{3,1},... | collective-permute-start | bytes 688136 | tf_op jit(solution)/shard_map/ppermute | solution.py:37
  141.1 5.7 %collective-permute-start.26 = (bf16[48,16,128]{2,1,0:T(8,128)(2,1)S(1)}, bf16[48,16,128]{2,1,0:T(8,128)(2,1)S(1)}, u32[]{:S(2)}, u32[]{:S(2)}) collective-permute-start(bf16[48,16,128]{2,1,0:T(8,128)(2,1)S(1)} %pad_maximum_fusion.5), channel_id=1, source_target_pairs={{0,1},{1,0},{2,3},{3,2},{4,5},{5,4},{6,7},{7,6},{8,9},{9,8},{10,11... | collective-permute-start | bytes 589832 | tf_op jit(solution)/shard_map/ppermute | solution.py:37
  (20 other events, 192.5 us)

commit v6 on v5

--- a/solution.py
+++ b/solution.py
@@ -337,13 +337,13 @@
 def product_kernel(*refs, n_recv, lanes, up_cols):
     side_ref, own_ref = refs[:2]
     recv = refs[2 : 2 + n_recv]
-    mask_ref, up_ref, hidden_hbm, handed_hbm = refs[2 + n_recv : 6 + n_recv]
+    mask_ref, up_ref, handed_ref, hidden_hbm = refs[2 + n_recv : 6 + n_recv]
     keep_ref, send_ref, handed_out, hidden_ref, sems = refs[6 + n_recv :]
     loads = [
         pltpu.make_async_copy(hidden_hbm.at[:, cut], hidden_ref.at[:, cut], sems.at[k])
         for k, cut in enumerate(lanes)
     ]
-    handing = pltpu.make_async_copy(handed_hbm, handed_out, sems.at[len(loads)])
+    handing = pltpu.make_async_copy(handed_ref, handed_out, sems.at[len(loads)])
     for load in loads:
         load.start()
     handing.start()
@@ -583,7 +583,7 @@
     tile_shape = (units * group, SUB, HD)
     keep, send, handed = pl.pallas_call(
         partial(product_kernel, n_recv=len(received), lanes=lanes, up_cols=up_cols),
-        in_specs=[smem] + [vmem] * (3 + len(received)) + [pl.BlockSpec(memory_space=pltpu.HBM)] * 2,
+        in_specs=[smem] + [vmem] * (4 + len(received)) + [pl.BlockSpec(memory_space=pltpu.HBM)],
         out_specs=[vmem, vmem, any_space],
         out_shape=[
             pltpu.VMEM(tile_shape, bf16),
@@ -598,9 +598,8 @@
         name="product",
     )(
         side[None],
-        *[in_vmem(x) for x in (lows[-1], *received, own_mask, ups)],
+        *[in_vmem(x) for x in (lows[-1], *received, own_mask, ups, handed)],
         in_hbm(hidden[0]),
-        in_hbm(handed),
     )
     recv = permute_cyclic(send, "section", 1)
     colours = pl.pallas_call(

time: 152 us -> 119 us (0.78)
  Pallas kernels: 55.1 us -> 24.1 us
    pallas_call x1, Pallas kernels: 33.9 us -> 2.82 us  [step(): pl.pallas_call(partial(product_kernel, n_recv=len(received), lanes=lanes,...]
  transfers between devices with their start and end apart: 29 -> 29, of which waited for: 19 -> 19; matrix products, arithmetic and copies ran while one was open for 5% -> 7% of each run, Pallas kernels for 7% -> 9%
where the time goes in v6:
time: 119 us
  waiting for transfers between devices  45.7 us (38%)
  starting transfers between devices  39.8 us (33%)
  Pallas kernels  24.1 us (20%)
  other arithmetic  6.99 us (6%)
  between operations  1.4 us (1%)
    ppermute x18, waiting for transfers between devices, permute_xor(): return lax.ppermute(value, axis, [(i, i ^ bit) for i in range(count)])  32.3 us
    ppermute x18, starting transfers between devices, permute_xor(): return lax.ppermute(value, axis, [(i, i ^ bit) for i in range(count)])  23 us
    ppermute x6, starting transfers between devices, permute_by(): lax.ppermute(value, axis, [(i, i + steps) for i in range(first, last)])  16.4 us
    pallas_call x4, Pallas kernels, attention(): pl.pallas_call(partial(attention_kernel, n_blocks=n_blocks, piece=piece,...  15.4 us
    ppermute x6, waiting for transfers between devices, permute_by(): lax.ppermute(value, axis, [(i, i + steps) for i in range(first, last)])  9.43 us
    ppermute x5, waiting for transfers between devices, permute_cyclic(): lax.ppermute(value, axis, [(i, (i + by) % count) for i in range(count)])  3.98 us
    pallas_call x1, Pallas kernels, pack(): pl.pallas_call(partial(pack_kernel, pieces=pieces, heads=heads, lanes=lan...  3.31 us
    pallas_call x1, Pallas kernels, step(): pl.pallas_call(partial(product_kernel, n_recv=len(received), lanes=lanes,...  2.82 us
  transfers between devices with their start and end apart: 29, of which 19 were waited for; matrix products, arithmetic and copies ran while one was open for 7% of the time, Pallas kernels for 9%

profile of v6, /device:TPU:0, one launch (start us, length us, event | category | flops | bytes accessed | tf_op | source)
XLA Modules:
  0.0 119.0 jit_solution(10010032957366090717)
XLA Ops:
  0.7 3.3 %pack.1 = (bf16[256,640]{1,0:T(8,128)(2,1)S(1)}, bf16[256,512]{1,0:T(8,128)(2,1)S(1)}, bf16[256,512]{1,0:T(8,128)(2,1)S(1)}, bf16[256,512]{1,0:T(8,128)(2,1)S(1)}) custom-call(bf16[256,5376]{1,0:T(8,128)(2,1)} %bitcast.57, bf16[128,5376]{1,0:T(8,128)(2,1)} %bitcast.59, bf16[256,1024]{1,0:T(8,128)(2,1)} %bitcast.72, bf16[256,1024]{1,0:T(8,128)(2,1)} %bitcast.73), custom_call_target="tpu_custom_call" | custom-call | tf_op jit(solution)/shard_map/pack/pallas_call | solution.py:112
  4.0 5.0 %collective-permute-start.3 = (bf16[256,640]{1,0:T(8,128)(2,1)S(1)}, bf16[256,640]{1,0:T(8,128)(2,1)S(1)}, u32[]{:S(2)}, u32[]{:S(2)}) collective-permute-start(bf16[256,640]{1,0:T(8,128)(2,1)S(1)} %get-tuple-element.30.refs_2_), channel_id=1, source_target_pairs={{0,4},{2,6},{4,8},{6,10},{8,12},{10,14},{1,5},{3,7},{5,9},{7,11},{... | collective-permute-start | bytes 983048 | tf_op jit(solution)/shard_map/ppermute | solution.py:27
  9.1 3.5 %collective-permute-start.7 = (bf16[256,512]{1,0:T(8,128)(2,1)S(1)}, bf16[256,512]{1,0:T(8,128)(2,1)S(1)}, u32[]{:S(2)}, u32[]{:S(2)}) collective-permute-start(bf16[256,512]{1,0:T(8,128)(2,1)S(1)} %get-tuple-element.33.refs_2_), channel_id=1, source_target_pairs={{0,4},{2,6},{4,8},{6,10},{8,12},{10,14},{1,5},{3,7},{5,9},{7,11},{... | collective-permute-start | bytes 786440 | tf_op jit(solution)/shard_map/ppermute | solution.py:27
  12.6 3.5 %collective-permute-start.5 = (bf16[256,512]{1,0:T(8,128)(2,1)S(1)}, bf16[256,512]{1,0:T(8,128)(2,1)S(1)}, u32[]{:S(2)}, u32[]{:S(2)}) collective-permute-start(bf16[256,512]{1,0:T(8,128)(2,1)S(1)} %get-tuple-element.32.refs_2_), channel_id=1, source_target_pairs={{0,4},{2,6},{4,8},{6,10},{8,12},{10,14},{1,5},{3,7},{5,9},{7,11},{... | collective-permute-start | bytes 786440 | tf_op jit(solution)/shard_map/ppermute | solution.py:27
  18.8 2.6 %fusion.7 = (f32[768,64]{1,0:T(8,128)}, f32[768,64]{1,0:T(8,128)}, f32[768,64]{1,0:T(8,128)}) fusion(f32[64]{0:T(128)S(1)} %multiply_power_fusion, f32[768]{0:T(1024)S(1)} %convert_element_type.91), kind=kLoop, calls=%fused_computation.41 | loop fusion | flops 98304 | bytes 593152 | tf_op jit(solution)/shard_map/neg | solution.py:535
  29.9 2.9 %collective-permute-done.refs_0_ = bf16[256,512]{1,0:T(8,128)(2,1)S(1)} collective-permute-done((bf16[256,512]{1,0:T(8,128)(2,1)S(1)}, bf16[256,512]{1,0:T(8,128)(2,1)S(1)}, u32[]{:S(2)}, u32[]{:S(2)}) %collective-permute-start) | collective-permute-done | bytes 262176 | tf_op jit(solution)/shard_map/ppermute | solution.py:27
  34.4 7.2 %collective-permute-done.4.refs_1_ = bf16[256,640]{1,0:T(8,128)(2,1)S(1)} collective-permute-done((bf16[256,640]{1,0:T(8,128)(2,1)S(1)}, bf16[256,640]{1,0:T(8,128)(2,1)S(1)}, u32[]{:S(2)}, u32[]{:S(2)}) %collective-permute-start.4) | collective-permute-done | bytes 327712 | tf_op jit(solution)/shard_map/ppermute | solution.py:37
  41.6 3.5 %attention.4 = (bf16[256,2048]{1,0:T(8,128)(2,1)S(1)}, bf16[2,64,1024]{2,1,0:T(8,128)(2,1)S(1)}, f32[768,128]{1,0:T(8,128)S(1)}, bf16[768,128]{1,0:T(8,128)(2,1)S(1)}) custom-call(bf16[256,640]{1,0:T(8,128)(2,1)S(1)} %collective-permute-done.3.refs_0_, bf16[256,640]{1,0:T(8,128)(2,1)S(1)} %collective-permute-done.4.refs_1_, ...), custom_call_target="tpu_custom_call" | custom-call | flops 1006632960 | bytes 1310720 | tf_op jit(solution)/shard_map/attention/pallas_call | solution.py:309
  45.2 3.8 %attention.5 = (bf16[256,2048]{1,0:T(8,128)(2,1)S(1)}, bf16[2,64,1024]{2,1,0:T(8,128)(2,1)S(1)}, f32[768,128]{1,0:T(8,128)S(1)}) custom-call(bf16[256,512]{1,0:T(8,128)(2,1)S(1)} %copy-done.10, bf16[256,512]{1,0:T(8,128)(2,1)S(1)} %collective-permute-done.8.refs_1_, ...), custom_call_target="tpu_custom_call", output_to_operand_aliasing={{0}: (12, {}), {1}: (13, {}), {2}: (11, {})} | custom-call | flops 1006632960 | bytes 1310720 | tf_op jit(solution)/shard_map/attention/pallas_call | solution.py:309
  49.1 3.9 %attention.6 = (bf16[256,2048]{1,0:T(8,128)(2,1)S(1)}, bf16[2,64,1024]{2,1,0:T(8,128)(2,1)S(1)}, f32[768,128]{1,0:T(8,128)S(1)}) custom-call(bf16[256,512]{1,0:T(8,128)(2,1)S(1)} %copy-done.8, bf16[256,512]{1,0:T(8,128)(2,1)S(1)} %collective-permute-done.6.refs_1_, ...), custom_call_target="tpu_custom_call", output_to_operand_aliasing={{0}: (12, {}), {1}: (13, {}), {2}: (11, {})} | custom-call | flops 1006632960 | bytes 1310720 | tf_op jit(solution)/shard_map/attention/pallas_call | solution.py:309
  53.0 4.2 %attention.7 = (bf16[256,2048]{1,0:T(8,128)(2,1)S(1)}, bf16[2,64,1024]{2,1,0:T(8,128)(2,1)S(1)}, bf16[32,256]{1,0:T(8,128)(2,1)S(1)}, bf16[32,256]{1,0:T(8,128)(2,1)S(1)}, bf16[32,256]{1,0:T(8,128)(2,1)S(1)}) custom-call(bf16[256,512]{1,0:T(8,128)(2,1)S(1)} %copy-done.4, ...), custom_call_target="tpu_custom_call", output_to_operand_aliasing={{0}: (12, {}), {1}: (13, {})} | custom-call | flops 1006632960 | bytes 1310720 | tf_op jit(solution)/shard_map/attention/pallas_call | solution.py:309
  60.0 2.9 %collective-permute-done.10.refs_3_ = bf16[32,256]{1,0:T(8,128)(2,1)S(1)} collective-permute-done((bf16[32,256]{1,0:T(8,128)(2,1)S(1)}, bf16[32,256]{1,0:T(8,128)(2,1)S(1)}, u32[]{:S(2)}, u32[]{:S(2)}) %collective-permute-start.10) | collective-permute-done | bytes 16416 | tf_op jit(solution)/shard_map/ppermute | solution.py:27
  62.9 2.9 %collective-permute-done.9.refs_2_ = bf16[32,256]{1,0:T(8,128)(2,1)S(1)} collective-permute-done((bf16[32,256]{1,0:T(8,128)(2,1)S(1)}, bf16[32,256]{1,0:T(8,128)(2,1)S(1)}, u32[]{:S(2)}, u32[]{:S(2)}) %collective-permute-start.9) | collective-permute-done | bytes 16416 | tf_op jit(solution)/shard_map/ppermute | solution.py:27
  65.8 2.8 %product.1 = (bf16[208,16,128]{2,1,0:T(8,128)(2,1)S(1)}, bf16[208,16,128]{2,1,0:T(8,128)(2,1)S(1)}, bf16[1,256,2048]{2,1,0:T(8,128)(2,1)}) custom-call(s32[1]{0:T(128)} %bitcast.refs_0_, bf16[32,256]{1,0:T(8,128)(2,1)S(1)} %get-tuple-element.43.refs_1_, bf16[32,256]{1,0:T(8,128)(2,1)S(1)} %collective-permute-done.9.refs_2_, ...), custom_call_target="tpu_custom_call" | custom-call | tf_op jit(solution)/shard_map/product/pallas_call | solution.py:584
  68.7 2.4 %collective-permute-done.12.recv_ref = bf16[208,16,128]{2,1,0:T(8,128)(2,1)S(1)} collective-permute-done((bf16[208,16,128]{2,1,0:T(8,128)(2,1)S(1)}, bf16[208,16,128]{2,1,0:T(8,128)(2,1)S(1)}, u32[]{:S(2)}, u32[]{:S(2)}) %collective-permute-start.12) | collective-permute-done | bytes 852000 | tf_op jit(solution)/shard_map/ppermute | solution.py:32
  74.0 4.3 %collective-permute-done.15 = bf16[48,16,128]{2,1,0:T(8,128)(2,1)S(1)} collective-permute-done((bf16[48,16,128]{2,1,0:T(8,128)(2,1)S(1)}, bf16[48,16,128]{2,1,0:T(8,128)(2,1)S(1)}, u32[]{:S(2)}, u32[]{:S(2)}) %collective-permute-start.15) | collective-permute-done | bytes 196640 | tf_op jit(solution)/shard_map/ppermute | solution.py:37
  83.1 2.2 %collective-permute-done.14 = bf16[28,16,128]{2,1,0:T(8,128)(2,1)S(1)} collective-permute-done((bf16[28,16,128]{2,1,0:T(8,128)(2,1)S(1)}, bf16[28,16,128]{2,1,0:T(8,128)(2,1)S(1)}, u32[]{:S(2)}, u32[]{:S(2)}) %collective-permute-start.14) | collective-permute-done | bytes 114720 | tf_op jit(solution)/shard_map/ppermute | solution.py:37
  85.3 2.1 %collective-permute-start.17 = (bf16[1,13,16,128]{3,2,1,0:T(8,128)(2,1)S(1)}, bf16[1,13,16,128]{3,2,1,0:T(8,128)(2,1)S(1)}, u32[]{:S(2)}, u32[]{:S(2)}) collective-permute-start(bf16[1,13,16,128]{3,2,1,0:T(8,128)(2,1)S(1)} %get-tuple-element.57), channel_id=1, source_target_pairs={{0,4},{2,6},{4,0},{6,2},{8,12},{10,14},{12,8},{14,10},{1,5},{3,7},... | collective-permute-start | bytes 159752 | tf_op jit(solution)/shard_map/ppermute | solution.py:37
  87.4 2.4 %collective-permute-start.19 = (bf16[1,13,16,128]{3,2,1,0:T(8,128)(2,1)S(1)}, bf16[1,13,16,128]{3,2,1,0:T(8,128)(2,1)S(1)}, u32[]{:S(2)}, u32[]{:S(2)}) collective-permute-start(bf16[1,13,16,128]{3,2,1,0:T(8,128)(2,1)S(1)} %get-tuple-element.59), channel_id=1, source_target_pairs={{0,12},{2,14},{4,8},{6,10},{8,4},{10,6},{12,0},{14,2},{1,13},{3,15... | collective-permute-start | bytes 159752 | tf_op jit(solution)/shard_map/ppermute | solution.py:37
  94.3 2.2 %collective-permute-start.21 = (bf16[1,13,16,128]{3,2,1,0:T(8,128)(2,1)S(1)}, bf16[1,13,16,128]{3,2,1,0:T(8,128)(2,1)S(1)}, u32[]{:S(2)}, u32[]{:S(2)}) collective-permute-start(bf16[1,13,16,128]{3,2,1,0:T(8,128)(2,1)S(1)} %add_convert_fusion.4), channel_id=1, source_target_pairs={{0,8},{2,10},{4,12},{6,14},{8,0},{10,2},{12,4},{14,6},{1,9},{3,11}... | collective-permute-start | bytes 159752 | tf_op jit(solution)/shard_map/ppermute | solution.py:37
  99.4 3.1 %collective-permute-done.22 = bf16[1,13,16,128]{3,2,1,0:T(8,128)(2,1)S(1)} collective-permute-done((bf16[1,13,16,128]{3,2,1,0:T(8,128)(2,1)S(1)}, bf16[1,13,16,128]{3,2,1,0:T(8,128)(2,1)S(1)}, u32[]{:S(2)}, u32[]{:S(2)}) %collective-permute-start.22) | collective-permute-done | bytes 53280 | tf_op jit(solution)/shard_map/ppermute | solution.py:37
  104.3 3.4 %collective-permute-done.23 = bf16[28,16,128]{2,1,0:T(8,128)(2,1)S(1)} collective-permute-done((bf16[28,16,128]{2,1,0:T(8,128)(2,1)S(1)}, bf16[28,16,128]{2,1,0:T(8,128)(2,1)S(1)}, u32[]{:S(2)}, u32[]{:S(2)}) %collective-permute-start.23) | collective-permute-done | bytes 114720 | tf_op jit(solution)/shard_map/ppermute | solution.py:37
  110.0 3.8 %collective-permute-done.24 = bf16[56,16,128]{2,1,0:T(8,128)(2,1)S(1)} collective-permute-done((bf16[56,16,128]{2,1,0:T(8,128)(2,1)S(1)}, bf16[56,16,128]{2,1,0:T(8,128)(2,1)S(1)}, u32[]{:S(2)}, u32[]{:S(2)}) %collective-permute-start.24) | collective-permute-done | bytes 229408 | tf_op jit(solution)/shard_map/ppermute | solution.py:37
  116.5 2.4 %assemble.1 = (f32[128,5376]{1,0:T(8,128)}, f32[128,1024]{1,0:T(8,128)}) custom-call(s32[3]{0:T(128)S(1)} %pad_add_fusion.1.scalars_ref, bf16[16,7,16,128]{3,2,1,0:T(8,128)(2,1)S(1)} %bitcast.52, bf16[16,6,16,128]{3,2,1,0:T(8,128)(2,1)S(1)} %bitcast.53, bf16[16,7,16,128]{3,2,1,0:T(8,128)(2,1)S(1)} %bitcast.55, bf16[16,6,16,128]{3,2,1,0:T(8,128)(2,1)S(1)} %bitcast.56), custom_call_target="tpu_custom_call" | custom-call | tf_op jit(solution)/shard_map/assemble/pallas_call | solution.py:641
  (116 shorter events, 37.4 us)
Async XLA Ops:
  4.0 22.9 %collective-permute-start.3 = (bf16[256,640]{1,0:T(8,128)(2,1)S(1)}, bf16[256,640]{1,0:T(8,128)(2,1)S(1)}, u32[]{:S(2)}, u32[]{:S(2)}) collective-permute-start(bf16[256,640]{1,0:T(8,128)(2,1)S(1)} %get-tuple-element.30.refs_2_), channel_id=1, source_target_pairs={{0,4},{2,6},{4,8},{6,10},{8,12},{10,14},{1,5},{3,7},{5,9},{7,11},{... | collective-permute-start | bytes 983048 | tf_op jit(solution)/shard_map/ppermute | solution.py:27
  9.0 32.6 %collective-permute-start.2 = (bf16[1,256,2048]{2,1,0:T(8,128)(2,1)}, bf16[1,256,2048]{2,1,0:T(8,128)(2,1)}, u32[]{:S(2)}, u32[]{:S(2)}) collective-permute-start(bf16[1,256,2048]{2,1,0:T(8,128)(2,1)} %param.13), channel_id=1, source_target_pairs={{0,16},{16,0},{1,17},{17,1},{2,18},{18,2},{3,19},{19,3},{4,20},{20... | collective-permute-start | bytes 3145736 | tf_op jit(solution)/shard_map/ppermute | solution.py:32
  9.1 16.2 %collective-permute-start.7 = (bf16[256,512]{1,0:T(8,128)(2,1)S(1)}, bf16[256,512]{1,0:T(8,128)(2,1)S(1)}, u32[]{:S(2)}, u32[]{:S(2)}) collective-permute-start(bf16[256,512]{1,0:T(8,128)(2,1)S(1)} %get-tuple-element.33.refs_2_), channel_id=1, source_target_pairs={{0,4},{2,6},{4,8},{6,10},{8,12},{10,14},{1,5},{3,7},{5,9},{7,11},{... | collective-permute-start | bytes 786440 | tf_op jit(solution)/shard_map/ppermute | solution.py:27
  12.6 15.7 %collective-permute-start.5 = (bf16[256,512]{1,0:T(8,128)(2,1)S(1)}, bf16[256,512]{1,0:T(8,128)(2,1)S(1)}, u32[]{:S(2)}, u32[]{:S(2)}) collective-permute-start(bf16[256,512]{1,0:T(8,128)(2,1)S(1)} %get-tuple-element.32.refs_2_), channel_id=1, source_target_pairs={{0,4},{2,6},{4,8},{6,10},{8,12},{10,14},{1,5},{3,7},{5,9},{7,11},{... | collective-permute-start | bytes 786440 | tf_op jit(solution)/shard_map/ppermute | solution.py:27
  16.0 16.7 %collective-permute-start = (bf16[256,512]{1,0:T(8,128)(2,1)S(1)}, bf16[256,512]{1,0:T(8,128)(2,1)S(1)}, u32[]{:S(2)}, u32[]{:S(2)}) collective-permute-start(bf16[256,512]{1,0:T(8,128)(2,1)S(1)} %get-tuple-element.29.refs_2_), channel_id=1, source_target_pairs={{0,4},{2,6},{4,8},{6,10},{8,12},{10,14},{1,5},{3,7},{5,9},{7,11},{... | collective-permute-start | bytes 786440 | tf_op jit(solution)/shard_map/ppermute | solution.py:27
  25.3 19.9 %collective-permute-start.8 = (bf16[256,512]{1,0:T(8,128)(2,1)S(1)}, bf16[256,512]{1,0:T(8,128)(2,1)S(1)}, u32[]{:S(2)}, u32[]{:S(2)}) collective-permute-start(bf16[256,512]{1,0:T(8,128)(2,1)S(1)} %broadcast_select_fusion.1), channel_id=1, source_target_pairs={{0,2},{2,0},{4,6},{6,4},{8,10},{10,8},{12,14},{14,12},{1,3},{3,1},... | collective-permute-start | bytes 786440 | tf_op jit(solution)/shard_map/ppermute | solution.py:37
  26.9 14.7 %collective-permute-start.4 = (bf16[256,640]{1,0:T(8,128)(2,1)S(1)}, bf16[256,640]{1,0:T(8,128)(2,1)S(1)}, u32[]{:S(2)}, u32[]{:S(2)}) collective-permute-start(bf16[256,640]{1,0:T(8,128)(2,1)S(1)} %broadcast_select_fusion), channel_id=1, source_target_pairs={{0,2},{2,0},{4,6},{6,4},{8,10},{10,8},{12,14},{14,12},{1,3},{3,1},... | collective-permute-start | bytes 983048 | tf_op jit(solution)/shard_map/ppermute | solution.py:37
  28.3 20.8 %collective-permute-start.6 = (bf16[256,512]{1,0:T(8,128)(2,1)S(1)}, bf16[256,512]{1,0:T(8,128)(2,1)S(1)}, u32[]{:S(2)}, u32[]{:S(2)}) collective-permute-start(bf16[256,512]{1,0:T(8,128)(2,1)S(1)} %broadcast_select_fusion.2), channel_id=1, source_target_pairs={{0,2},{2,0},{4,6},{6,4},{8,10},{10,8},{12,14},{14,12},{1,3},{3,1},... | collective-permute-start | bytes 786440 | tf_op jit(solution)/shard_map/ppermute | solution.py:37
  32.8 20.2 %collective-permute-start.1 = (bf16[256,512]{1,0:T(8,128)(2,1)S(1)}, bf16[256,512]{1,0:T(8,128)(2,1)S(1)}, u32[]{:S(2)}, u32[]{:S(2)}) collective-permute-start(bf16[256,512]{1,0:T(8,128)(2,1)S(1)} %broadcast_select_fusion.3), channel_id=1, source_target_pairs={{0,2},{2,0},{4,6},{6,4},{8,10},{10,8},{12,14},{14,12},{1,3},{3,1},... | collective-permute-start | bytes 786440 | tf_op jit(solution)/shard_map/ppermute | solution.py:37
  57.2 8.6 %collective-permute-start.11 = (bf16[256,2048]{1,0:T(8,128)(2,1)S(1)}, bf16[256,2048]{1,0:T(8,128)(2,1)S(1)}, u32[]{:S(2)}, u32[]{:S(2)}) collective-permute-start(bf16[256,2048]{1,0:T(8,128)(2,1)S(1)} %get-tuple-element.47), channel_id=1, source_target_pairs={{0,16},{16,0},{1,17},{17,1},{2,18},{18,2},{3,19},{19,3},{4,20},{20... | collective-permute-start | bytes 3145736 | tf_op jit(solution)/shard_map/ppermute | solution.py:32
  57.3 5.6 %collective-permute-start.10 = (bf16[32,256]{1,0:T(8,128)(2,1)S(1)}, bf16[32,256]{1,0:T(8,128)(2,1)S(1)}, u32[]{:S(2)}, u32[]{:S(2)}) collective-permute-start(bf16[32,256]{1,0:T(8,128)(2,1)S(1)} %get-tuple-element.45), channel_id=1, source_target_pairs={{2,0},{4,2},{6,4},{8,6},{10,8},{12,10},{14,12},{3,1},{5,3},{7,5},{... | collective-permute-start | bytes 49160 | tf_op jit(solution)/shard_map/ppermute | solution.py:27
  58.6 7.2 %collective-permute-start.9 = (bf16[32,256]{1,0:T(8,128)(2,1)S(1)}, bf16[32,256]{1,0:T(8,128)(2,1)S(1)}, u32[]{:S(2)}, u32[]{:S(2)}) collective-permute-start(bf16[32,256]{1,0:T(8,128)(2,1)S(1)} %get-tuple-element.44), channel_id=1, source_target_pairs={{4,0},{6,2},{8,4},{10,6},{12,8},{14,10},{5,1},{7,3},{9,5},{11,7},{... | collective-permute-start | bytes 49160 | tf_op jit(solution)/shard_map/ppermute | solution.py:27
  71.3 7.0 %collective-permute-start.15 = (bf16[48,16,128]{2,1,0:T(8,128)(2,1)S(1)}, bf16[48,16,128]{2,1,0:T(8,128)(2,1)S(1)}, u32[]{:S(2)}, u32[]{:S(2)}) collective-permute-start(bf16[48,16,128]{2,1,0:T(8,128)(2,1)S(1)} %constant_dynamic-slice_fusion.1), channel_id=1, source_target_pairs={{0,1},{1,0},{2,3},{3,2},{4,5},{5,4},{6,7},{7,6},{8,9},{9,8},{10,11... | collective-permute-start | bytes 589832 | tf_op jit(solution)/shard_map/ppermute | solution.py:37
  72.9 7.4 %collective-permute-start.13 = (bf16[56,16,128]{2,1,0:T(8,128)(2,1)S(1)}, bf16[56,16,128]{2,1,0:T(8,128)(2,1)S(1)}, u32[]{:S(2)}, u32[]{:S(2)}) collective-permute-start(bf16[56,16,128]{2,1,0:T(8,128)(2,1)S(1)} %constant_dynamic-slice_fusion.3), channel_id=1, source_target_pairs={{0,2},{2,0},{4,6},{6,4},{8,10},{10,8},{12,14},{14,12},{1,3},{3,1},... | collective-permute-start | bytes 688136 | tf_op jit(solution)/shard_map/ppermute | solution.py:37
  80.4 4.9 %collective-permute-start.14 = (bf16[28,16,128]{2,1,0:T(8,128)(2,1)S(1)}, bf16[28,16,128]{2,1,0:T(8,128)(2,1)S(1)}, u32[]{:S(2)}, u32[]{:S(2)}) collective-permute-start(bf16[28,16,128]{2,1,0:T(8,128)(2,1)S(1)} %constant_dynamic-slice_fusion.2), channel_id=1, source_target_pairs={{0,1},{1,0},{2,3},{3,2},{4,5},{5,4},{6,7},{7,6},{8,9},{9,8},{10,11... | collective-permute-start | bytes 344072 | tf_op jit(solution)/shard_map/ppermute | solution.py:37
  85.3 5.3 %collective-permute-start.17 = (bf16[1,13,16,128]{3,2,1,0:T(8,128)(2,1)S(1)}, bf16[1,13,16,128]{3,2,1,0:T(8,128)(2,1)S(1)}, u32[]{:S(2)}, u32[]{:S(2)}) collective-permute-start(bf16[1,13,16,128]{3,2,1,0:T(8,128)(2,1)S(1)} %get-tuple-element.57), channel_id=1, source_target_pairs={{0,4},{2,6},{4,0},{6,2},{8,12},{10,14},{12,8},{14,10},{1,5},{3,7},... | collective-permute-start | bytes 159752 | tf_op jit(solution)/shard_map/ppermute | solution.py:37
  87.4 5.1 %collective-permute-start.18 = (bf16[1,13,16,128]{3,2,1,0:T(8,128)(2,1)S(1)}, bf16[1,13,16,128]{3,2,1,0:T(8,128)(2,1)S(1)}, u32[]{:S(2)}, u32[]{:S(2)}) collective-permute-start(bf16[1,13,16,128]{3,2,1,0:T(8,128)(2,1)S(1)} %get-tuple-element.58), channel_id=1, source_target_pairs={{0,8},{2,10},{4,12},{6,14},{8,0},{10,2},{12,4},{14,6},{1,9},{3,11}... | collective-permute-start | bytes 159752 | tf_op jit(solution)/shard_map/ppermute | solution.py:37
  87.4 6.1 %collective-permute-start.19 = (bf16[1,13,16,128]{3,2,1,0:T(8,128)(2,1)S(1)}, bf16[1,13,16,128]{3,2,1,0:T(8,128)(2,1)S(1)}, u32[]{:S(2)}, u32[]{:S(2)}) collective-permute-start(bf16[1,13,16,128]{3,2,1,0:T(8,128)(2,1)S(1)} %get-tuple-element.59), channel_id=1, source_target_pairs={{0,12},{2,14},{4,8},{6,10},{8,4},{10,6},{12,0},{14,2},{1,13},{3,15... | collective-permute-start | bytes 159752 | tf_op jit(solution)/shard_map/ppermute | solution.py:37
  94.3 5.0 %collective-permute-start.21 = (bf16[1,13,16,128]{3,2,1,0:T(8,128)(2,1)S(1)}, bf16[1,13,16,128]{3,2,1,0:T(8,128)(2,1)S(1)}, u32[]{:S(2)}, u32[]{:S(2)}) collective-permute-start(bf16[1,13,16,128]{3,2,1,0:T(8,128)(2,1)S(1)} %add_convert_fusion.4), channel_id=1, source_target_pairs={{0,8},{2,10},{4,12},{6,14},{8,0},{10,2},{12,4},{14,6},{1,9},{3,11}... | collective-permute-start | bytes 159752 | tf_op jit(solution)/shard_map/ppermute | solution.py:37
  96.6 5.9 %collective-permute-start.22 = (bf16[1,13,16,128]{3,2,1,0:T(8,128)(2,1)S(1)}, bf16[1,13,16,128]{3,2,1,0:T(8,128)(2,1)S(1)}, u32[]{:S(2)}, u32[]{:S(2)}) collective-permute-start(bf16[1,13,16,128]{3,2,1,0:T(8,128)(2,1)S(1)} %add_convert_fusion.4), channel_id=1, source_target_pairs={{0,12},{2,14},{4,8},{6,10},{8,4},{10,6},{12,0},{14,2},{1,13},{3,15... | collective-permute-start | bytes 159752 | tf_op jit(solution)/shard_map/ppermute | solution.py:37
  102.5 5.2 %collective-permute-start.23 = (bf16[28,16,128]{2,1,0:T(8,128)(2,1)S(1)}, bf16[28,16,128]{2,1,0:T(8,128)(2,1)S(1)}, u32[]{:S(2)}, u32[]{:S(2)}) collective-permute-start(bf16[28,16,128]{2,1,0:T(8,128)(2,1)S(1)} %bitcast.62), channel_id=1, source_target_pairs={{0,1},{1,0},{2,3},{3,2},{4,5},{5,4},{6,7},{7,6},{8,9},{9,8},{10,11... | collective-permute-start | bytes 344072 | tf_op jit(solution)/shard_map/ppermute | solution.py:37
  103.3 5.6 %collective-permute-start.25 = (bf16[24,16,128]{2,1,0:T(8,128)(2,1)S(1)}, bf16[24,16,128]{2,1,0:T(8,128)(2,1)S(1)}, u32[]{:S(2)}, u32[]{:S(2)}) collective-permute-start(bf16[24,16,128]{2,1,0:T(8,128)(2,1)S(1)} %bitcast.67), channel_id=1, source_target_pairs={{0,2},{2,0},{4,6},{6,4},{8,10},{10,8},{12,14},{14,12},{1,3},{3,1},... | collective-permute-start | bytes 294920 | tf_op jit(solution)/shard_map/ppermute | solution.py:37
  107.7 6.1 %collective-permute-start.24 = (bf16[56,16,128]{2,1,0:T(8,128)(2,1)S(1)}, bf16[56,16,128]{2,1,0:T(8,128)(2,1)S(1)}, u32[]{:S(2)}, u32[]{:S(2)}) collective-permute-start(bf16[56,16,128]{2,1,0:T(8,128)(2,1)S(1)} %pad_maximum_fusion.4), channel_id=1, source_target_pairs={{0,2},{2,0},{4,6},{6,4},{8,10},{10,8},{12,14},{14,12},{1,3},{3,1},... | collective-permute-start | bytes 688136 | tf_op jit(solution)/shard_map/ppermute | solution.py:37
  108.9 5.7 %collective-permute-start.26 = (bf16[48,16,128]{2,1,0:T(8,128)(2,1)S(1)}, bf16[48,16,128]{2,1,0:T(8,128)(2,1)S(1)}, u32[]{:S(2)}, u32[]{:S(2)}) collective-permute-start(bf16[48,16,128]{2,1,0:T(8,128)(2,1)S(1)} %pad_maximum_fusion.5), channel_id=1, source_target_pairs={{0,1},{1,0},{2,3},{3,2},{4,5},{5,4},{6,7},{7,6},{8,9},{9,8},{10,11... | collective-permute-start | bytes 589832 | tf_op jit(solution)/shard_map/ppermute | solution.py:37
  (19 other events, 191.4 us)
